TPU v7x, 256 devices: a 8x8x2 block of a 8x8x16 slice. The times are simulated.
256 devices in a mesh: grp: 2 (over z), tp: 128 (over x, y, core).
Axes of the slice: x: 8, y: 8, z: 2, core: 2. Of those that a mesh axis runs over, the one named last changes fastest.
The devices are a block of a 8x8x16 slice.
Arguments:
- hidden_in: float32 [64, 4608], P('grp'), parts along dimension 0, may hold values from -6 to 6
- prefill_cache: bfloat16 [128, 1, 2, 4, 128, 8, 256], P('tp', None, None, 'grp'), parts along dimension 3, may hold values from -6 to 6
- lengths: int32 [64], P('grp'), parts along dimension 0, may hold values from 1 to 1023
- page_table: int32 [64, 128], P('grp'), parts along dimension 0, may hold values from 0 to 127, each once within a row
- qkv_weight: bfloat16 [1, 8192, 4608], P(None, 'tp'), may hold values from -0.09375 to 0.09375
- out_weight: bfloat16 [1, 4608, 4096], P(None, 'tp'), may hold values from -0.09375 to 0.09375
- gate_up_weight: bfloat16 [1, 2, 18432, 4608], P(None, None, 'tp'), may hold values from -0.09375 to 0.09375
- down_weight: bfloat16 [1, 18432, 4608], P(None, 'tp'), may hold values from -0.15625 to 0.15625
- norm_gains: float32 [1, 4, 4608], replicated, may hold values from 0.25 to 1.75
Outputs:
- hidden_out: float32 [64, 4608], P('grp', 'tp'), parts along dimension 0
- decode_cache: bfloat16 [128, 1, 2, 64, 8, 2048], P('tp', None, None, 'grp'), parts along dimension 3
There are 2 independent parts, one for each index of `grp`. A program takes and returns all parts, laid end to end along the dimension named above; an argument that names none is the same for every part. Nothing has to cross between parts.
Inputs may be any that keep to these rules, and one draw needn't show every extreme that they name: Request r's new token takes position lengths[r]. Each row is a permutation of 0 to 127; page j of request r holds cache positions page_table[r, j] * 8 to page_table[r, j] * 8 + 7.
All inputs are finite; a program needn't handle non-finite values.
Results may differ from a plain program's by a relative error of at most 0.012.
The roundings to bfloat16 on the way count: a program that leaves them out, or rounds other values in their place, can miss the bound.
Values may be sent and summed in bfloat16 or wider, within the bound.
No kernel may reach another device: no remote copies, remote signals or barrier semaphores. Data moves between devices by JAX's collectives and lax.ppermute only.
A program may use at most 64 MiB of HBM per device.

v0:
```python
import functools

import jax
import jax.numpy as jnp
from jax import lax
from jax.experimental import pallas as pl
from jax.experimental.pallas import tpu as pltpu
from jax.sharding import Mesh
from jax.sharding import PartitionSpec as P

D = 4608
HEADS = 32
KV_HEADS = 16
HEAD_DIM = 128
PREFILL_TP = 8
TP = ("tp_0", "tp_1", "tp_2")
XY = ("tp_0", "tp_1")

EPSILON = 1e-06
SOFTCAP = 50.0
LANES = 128
ROWS = 8
BF16 = jnp.bfloat16
F32 = jnp.float32

CHIPS = 64
QUARTERS = PREFILL_TP // 2
GROUPS = CHIPS // QUARTERS
SHARE = D // (2 * CHIPS)
BLOCKS = D // LANES
BATCH = 32
PER_GROUP = 2
PAGE_TILES = 2 * PER_GROUP * 2
BULK_TILES = 2 * PAGE_TILES + 1
VMEM_LIMIT = 48 * 1024 * 1024


def smem():
    return pl.BlockSpec(memory_space=pltpu.SMEM)


def vmem():
    return pl.BlockSpec(memory_space=pltpu.VMEM)


def anywhere():
    return pl.BlockSpec(memory_space=pl.ANY)


def call(kernel, out_shape, in_specs, out_specs, name, **more):
    return pl.pallas_call(
        kernel,
        out_shape=out_shape,
        in_specs=in_specs,
        out_specs=out_specs,
        name=name,
        compiler_params=pltpu.CompilerParams(vmem_limit_bytes=VMEM_LIMIT),
        **more,
    )


def shaped(shape, dtype):
    return jax.ShapeDtypeStruct(shape, dtype)


def nt_dot(left, right):
    return lax.dot_general(left, right, (((1,), (1,)), ((), ())), preferred_element_type=F32)


def nn_dot(left, right):
    return lax.dot_general(left, right, (((1,), (0,)), ((), ())), preferred_element_type=F32)


def iota(shape, dim):
    return lax.broadcasted_iota(jnp.int32, shape, dim)


def capped(raw_scores):
    return SOFTCAP * jnp.tanh(raw_scores / SOFTCAP)


def pages_kernel(me_ref, table_ref, cache_ref, out_ref):
    me = me_ref[0]
    core = me & 1
    group = me >> 3

    def place(j, carry):
        for e in range(PER_GROUP):
            block = table_ref[PER_GROUP * group + e, j]
            chip = block >> 1
            base = ((block & 1) ^ core) * PAGE_TILES + e * 2
            for kv in range(2):
                page = cache_ref[kv, e, j]
                out_ref[chip, base + kv * 4] = page[:, :LANES]
                out_ref[chip, base + kv * 4 + 1] = page[:, LANES:]
        return carry

    lax.fori_loop(0, 2 * CHIPS, place, 0, unroll=4)


def qkv_kernel(
    me_ref, hidden_ref, gain_ref, own_ref, other_ref, cos_ref, sin_ref, buf_ref, out_ref, tile_ref, sem
):
    me = me_ref[0]
    first = (me & 1) == 0
    head = me >> 1
    x = hidden_ref[...]
    meansq = jnp.sum(x * x, axis=-1, keepdims=True) * (1.0 / D)
    normed = (x * lax.rsqrt(meansq + EPSILON) * (1.0 + gain_ref[0, 0:1, :])).astype(BF16)
    own = nt_dot(normed, own_ref[0]).astype(BF16).astype(F32)
    other = nt_dot(normed, other_ref[0]).astype(BF16).astype(F32)
    front = jnp.where(first, own, other)
    back = jnp.where(first, other, own)
    cosine = cos_ref[...]
    sine = sin_ref[...]
    turned = head < HEADS + KV_HEADS
    new_front = jnp.where(turned, front * cosine - back * sine, front)
    new_back = jnp.where(turned, back * cosine + front * sine, back)
    whole = jnp.concatenate([new_front, new_back], axis=1)
    for u in range(BATCH // ROWS):
        rows = whole[ROWS * u : ROWS * u + ROWS, :].astype(BF16)
        per = CHIPS * ROWS // BATCH
        tile_ref[per * u : per * u + per] = jnp.broadcast_to(rows[None], (per, ROWS, LANES))
    copy = pltpu.make_async_copy(tile_ref, out_ref.at[:, BULK_TILES - 1], sem)
    copy.start()
    copy.wait()


def attend_kernel(me_ref, got_ref, seen_ref, cache_ref, out_ref):
    me = me_ref[0]
    group = me >> 3
    slot = me & 7
    rows_at = (group & 3) * PER_GROUP
    n_src = CHIPS * ROWS
    o = iota((32, n_src), 0)
    n = iota((32, n_src), 1)
    e = o & 1
    m = (o >> 1) & 3
    kind = o >> 3
    q_head = slot * 4 + m
    k_head = HEADS + slot * 2 + (m >> 1)
    v_head = k_head + KV_HEADS
    fix_head = HEADS + slot * 2 + (m & 1) + KV_HEADS * (m >> 1)
    chosen = jnp.where(kind == 0, q_head, jnp.where(kind == 1, k_head, jnp.where(kind == 2, v_head, fix_head)))
    pick = jnp.where(n == chosen * ROWS + rows_at + e, 1.0, 0.0).astype(BF16)
    source = got_ref[:, 0].astype(F32).reshape(n_src, LANES).astype(BF16)
    picked = nn_dot(pick, source)
    q = picked[0:8]
    new_k = picked[8:16]
    new_v = picked[16:24]
    q16 = q.astype(BF16)
    scale = (D / HEADS) ** (-0.5)
    row = iota((ROWS, 1), 0)
    scores = jnp.zeros((ROWS, 8 * 2 * CHIPS), F32)
    for ee in range(PER_GROUP):
        for a in range(2):
            keys = cache_ref[0, ee, :, a * LANES : a * LANES + LANES]
            part = nt_dot(q16, keys)
            scores = jnp.where(((row & 1) == ee) & ((row >> 2) == a), part, scores)
    weights = jnp.where(seen_ref[...] > 0.5, jnp.exp(capped(scores * scale)), 0.0)
    own = jnp.exp(capped(jnp.sum(q * new_k, axis=-1, keepdims=True) * scale))
    denominator = jnp.sum(weights, axis=-1, keepdims=True) + own
    w16 = weights.astype(BF16)
    numerator = own.astype(BF16).astype(F32) * new_v
    for ee in range(PER_GROUP):
        for a in range(2):
            values = cache_ref[1, ee, :, a * LANES : a * LANES + LANES]
            part = nn_dot(w16, values)
            numerator = numerator + jnp.where(((row & 1) == ee) & ((row >> 2) == a), part, 0.0)
    attended = numerator / denominator
    payload = jnp.concatenate([attended, picked[24:32]], axis=0).astype(BF16)
    out_ref[...] = jnp.broadcast_to(payload[None], (CHIPS, 2 * ROWS, LANES))


def mix_kernel(me_ref, own_ref, other_ref, weight_ref, out_ref):
    me = me_ref[0]
    first = (me & 1) == 0
    n_src = CHIPS * ROWS
    o = iota((n_src, n_src), 0)
    n = iota((n_src, n_src), 1)
    quarter = o >> 7
    m = (o >> 5) & 3
    group = (o >> 1) & 15
    source_row = (group * QUARTERS + quarter) * ROWS + m * 2 + (o & 1)
    pick = jnp.where(n == source_row, 1.0, 0.0).astype(BF16)
    own = own_ref[...][:, :ROWS].astype(F32)
    other = other_ref[...][:, :ROWS].astype(F32)
    mixed = jnp.zeros((BATCH, SHARE), F32)
    for c in range(2):
        mine = jnp.where(first, own, other) if c == 0 else jnp.where(first, other, own)
        rows = nn_dot(pick, mine.reshape(n_src, LANES).astype(BF16)).astype(BF16)
        left = jnp.concatenate([rows[BATCH * b : BATCH * b + BATCH] for b in range(16)], axis=1)
        right = jnp.concatenate(
            [weight_ref[0, :, (2 * y + c) * 512 : (2 * y + c) * 512 + 512] for y in range(QUARTERS)], axis=1
        )
        mixed = mixed + nt_dot(left, right)
    wide = jnp.concatenate(
        [mixed.astype(BF16).astype(F32), jnp.zeros((BATCH, LANES - SHARE), F32)], axis=1
    )
    turned = pltpu.roll(wide, (me * SHARE) % LANES, 1).astype(BF16)
    out_ref[...] = jnp.broadcast_to(turned[None], (CHIPS, BATCH, LANES))


def window(blocks, j):
    lane = iota((BATCH, LANES), 1)
    v, off = divmod(j * SHARE, LANES)
    here = blocks(v)
    if off + SHARE > LANES:
        here = jnp.where(lane >= off, here, blocks(v + 1))
    return here


def ffn_kernel(
    me_ref,
    own_ref,
    other_ref,
    hidden_ref,
    gain_ref,
    gate_up_ref,
    down_ref,
    keep_ref,
    send_ref,
    stream_ref,
    wide_ref,
    blocks_ref,
    ffn_ref,
):
    me = me_ref[0]
    first = (me & 1) == 0
    lane = iota((BATCH, LANES), 1)
    total = jnp.zeros((BATCH, LANES), F32)
    for v in range(BLOCKS):
        block = jnp.zeros((BATCH, LANES), F32)
        for j in range((LANES * v) // SHARE, (LANES * v + LANES - 1) // SHARE + 1):
            own = own_ref[j >> 1]
            other = other_ref[j >> 1]
            piece = (jnp.where(first, own, other) if j % 2 == 0 else jnp.where(first, other, own)).astype(F32)
            start = j * SHARE - LANES * v
            block = piece if start <= 0 else jnp.where(lane >= start, piece, block)
        blocks_ref[v] = block
        total = total + block * block
    scale = lax.rsqrt(jnp.sum(total, axis=-1, keepdims=True) * (1.0 / D) + EPSILON)
    total = jnp.zeros((BATCH, LANES), F32)
    for v in range(BLOCKS):
        cols = slice(LANES * v, LANES * v + LANES)
        block = hidden_ref[:, cols] + blocks_ref[v] * scale * (1.0 + gain_ref[0, 1:2, cols])
        wide_ref[v] = block
        total = total + block * block
    scale = lax.rsqrt(jnp.sum(total, axis=-1, keepdims=True) * (1.0 / D) + EPSILON)
    for v in range(BLOCKS):
        cols = slice(LANES * v, LANES * v + LANES)
        ffn_ref[:, cols] = (wide_ref[v] * scale * (1.0 + gain_ref[0, 2:3, cols])).astype(BF16)
    ffn_in = ffn_ref[...]
    gate = nt_dot(ffn_in, gate_up_ref[0, 0])
    up = nt_dot(ffn_in, gate_up_ref[0, 1])
    active = (jax.nn.gelu(gate, approximate=True) * up).astype(BF16)
    for v in range(BLOCKS):
        blocks_ref[v] = nn_dot(active, down_ref[0, :, LANES * v : LANES * v + LANES])
    for p in range(CHIPS):
        even = window(lambda v: blocks_ref[v], 2 * p)
        odd = window(lambda v: blocks_ref[v], 2 * p + 1)
        keep_ref[p] = jnp.where(first, even, odd).astype(BF16)
        send_ref[p] = jnp.where(first, odd, even).astype(BF16)
    start = me * SHARE
    at = start // LANES
    off = start % LANES
    after = jnp.minimum(at + 1, BLOCKS - 1)
    stream_ref[...] = jnp.where(lane >= off, wide_ref[at], wide_ref[after])


def to_front(x, me):
    off = (me * SHARE) % LANES
    return pltpu.roll(x, (LANES - off) % LANES, 1)


def portion_kernel(me_ref, got_ref, portion_ref, square_ref):
    me = me_ref[0]
    total = jnp.zeros((BATCH, LANES), F32)
    for p in range(CHIPS):
        total = total + got_ref[p].astype(F32)
    mine = to_front(total, me)
    portion_ref[...] = mine
    lane = iota((BATCH, LANES), 1)
    square = jnp.sum(jnp.where(lane < SHARE, mine * mine, 0.0), axis=-1, keepdims=True)
    square_ref[...] = jnp.sum(jnp.where(iota((BATCH, LANES), 0) == lane, square, 0.0), axis=0, keepdims=True)


def finish_kernel(me_ref, portion_ref, stream_ref, squares_ref, gain_ref, out_ref):
    me = me_ref[0]
    squares = jnp.sum(squares_ref[...], axis=0)
    lane = iota((BATCH, LANES), 1)
    column = jnp.sum(jnp.where(iota((BATCH, LANES), 0) == lane, squares, 0.0), axis=-1, keepdims=True)
    scale = lax.rsqrt(column * (1.0 / D) + EPSILON)
    done = to_front(stream_ref[...], me) + portion_ref[...] * scale * (1.0 + gain_ref[...])
    out_ref[...] = done[:, :SHARE]


def decode_kernel(me_ref, lengths_ref, got_ref, other_ref, own_new_ref, other_new_ref, out_ref):
    me = me_ref[0]
    core = me & 1

    def place(first_core):
        def body(g, carry):
            for y in range(QUARTERS):
                s = g * QUARTERS + y
                for side, ref in ((0, got_ref), (1, other_ref)):
                    slot = 2 * y + (first_core if side == 0 else 1 - first_core)
                    for kv in range(2):
                        for e in range(PER_GROUP):
                            for h in range(2):
                                cols = slice((2 * slot + h) * LANES, (2 * slot + h) * LANES + LANES)
                                out_ref[kv, g * PER_GROUP + e, :, cols] = ref[s, kv * 4 + e * 2 + h]
            return carry

        lax.fori_loop(0, GROUPS, body, 0)

    @pl.when(core == 0)
    def _():
        place(0)

    @pl.when(core == 1)
    def _():
        place(1)

    def fresh(r, carry):
        length = lengths_ref[r]

        @pl.when((length >> 3) == me)
        def _():
            g = r >> 1
            e = r & 1
            token = iota((ROWS, LANES), 0) == (length & 7)
            which = iota((2 * ROWS, LANES), 0)
            for y in range(QUARTERS):
                s = g * QUARTERS + y
                own = own_new_ref[s].astype(F32)
                other = other_new_ref[s].astype(F32)
                for c in range(2):
                    rows = jnp.where(core == c, own, other)
                    for kv in range(2):
                        for a in range(2):
                            at = ROWS + kv * 4 + a * 2 + e
                            line = jnp.sum(jnp.where(which == at, rows, 0.0), axis=0, keepdims=True)
                            slot = 2 * (2 * y + c) + a
                            cols = slice(slot * LANES, slot * LANES + LANES)
                            old = out_ref[kv, r, :, cols].astype(F32)
                            out_ref[kv, r, :, cols] = jnp.where(token, line, old).astype(BF16)

        return carry

    lax.fori_loop(0, BATCH, fresh, 0)


def core_swap(shard):
    return lax.ppermute(shard, "tp_2", [(0, 1), (1, 0)])


def to_chips(tiles):
    return lax.all_to_all(tiles, XY, 0, 0, tiled=True)


def pages_call(me, table, cache):
    return call(
        pages_kernel,
        shaped((CHIPS, BULK_TILES, ROWS, LANES), BF16),
        [smem(), smem(), vmem()],
        vmem(),
        "pages",
    )(me, table, cache)


def qkv_call(me, hidden, gains, own, other, cosine, sine, buf):
    return call(
        qkv_kernel,
        shaped(buf.shape, BF16),
        [smem()] + [vmem()] * 6 + [anywhere()],
        anywhere(),
        "qkv",
        scratch_shapes=[pltpu.VMEM((CHIPS, ROWS, LANES), BF16), pltpu.SemaphoreType.DMA],
        input_output_aliases={7: 0},
    )(me, hidden, gains, own, other, cosine, sine, buf)


def attend_call(me, got, seen, cache):
    return pl.pallas_call(
        attend_kernel,
        grid=(1,),
        out_shape=shaped((CHIPS, 2 * ROWS, LANES), BF16),
        in_specs=[
            smem(),
            pl.BlockSpec((CHIPS, 1, ROWS, LANES), lambda i: (0, BULK_TILES - 1, 0, 0)),
            vmem(),
            vmem(),
        ],
        out_specs=vmem(),
        name="attend",
        compiler_params=pltpu.CompilerParams(vmem_limit_bytes=VMEM_LIMIT),
    )(me, got, seen, cache)


def mix_call(me, own, other, weight):
    return call(mix_kernel, shaped((CHIPS, BATCH, LANES), BF16), [smem()] + [vmem()] * 3, vmem(), "mix")(
        me, own, other, weight
    )


def ffn_call(me, own, other, hidden, gains, gate_up, down):
    wide = shaped((CHIPS, BATCH, LANES), BF16)
    return call(
        ffn_kernel,
        (wide, wide, shaped((BATCH, LANES), F32)),
        [smem()] + [vmem()] * 6,
        (vmem(), vmem(), vmem()),
        "ffn",
        scratch_shapes=[
            pltpu.VMEM((BLOCKS, BATCH, LANES), F32),
            pltpu.VMEM((BLOCKS, BATCH, LANES), F32),
            pltpu.VMEM((BATCH, D), BF16),
        ],
    )(me, own, other, hidden, gains, gate_up, down)


def portion_call(me, got):
    return call(
        portion_kernel,
        (shaped((BATCH, LANES), F32), shaped((1, LANES), F32)),
        [smem(), vmem()],
        (vmem(), vmem()),
        "portion",
    )(me, got)


def finish_call(me, portion, stream, squares, gain):
    return call(finish_kernel, shaped((BATCH, SHARE), F32), [smem()] + [vmem()] * 4, vmem(), "finish")(
        me, portion, stream, squares, gain
    )


def decode_call(me, lengths, got, other, own_new, other_new):
    return pl.pallas_call(
        decode_kernel,
        grid=(1,),
        out_shape=shaped((2, BATCH, ROWS, KV_HEADS * HEAD_DIM), BF16),
        in_specs=[
            smem(),
            smem(),
            pl.BlockSpec((CHIPS, PAGE_TILES, ROWS, LANES), lambda i: (0, 0, 0, 0)),
            vmem(),
            vmem(),
            vmem(),
        ],
        out_specs=vmem(),
        name="decode",
        compiler_params=pltpu.CompilerParams(vmem_limit_bytes=VMEM_LIMIT),
    )(me, lengths, got, other, own_new, other_new)


def rope_tables(lengths):
    half_dim = HEAD_DIM // 2
    exponent = jnp.arange(half_dim, dtype=F32) * (-2.0 / HEAD_DIM)
    frequency = jnp.power(jnp.float32(10000.0), exponent)
    angles = lengths.astype(F32)[:, None] * frequency
    return jnp.cos(angles), jnp.sin(angles)


def on_device(
    hidden_in,
    prefill_cache,
    lengths,
    page_table,
    qkv_weight,
    out_weight,
    gate_up_weight,
    down_weight,
    norm_gains,
):
    my_index = lax.axis_index(TP)
    me = jnp.full((1,), my_index, jnp.int32)
    group = my_index // PREFILL_TP
    cache = prefill_cache[0, 0]
    other_rows = core_swap(qkv_weight)
    buf = pages_call(me, page_table, cache)
    cosine, sine = rope_tables(lengths)
    buf = qkv_call(me, hidden_in, norm_gains, qkv_weight, other_rows, cosine, sine, buf)
    with jax.named_scope("bulk"):
        got = to_chips(buf)
    rows = lax.dynamic_slice_in_dim(page_table, group * PER_GROUP, PER_GROUP, 0)
    limits = lax.dynamic_slice_in_dim(lengths, group * PER_GROUP, PER_GROUP, 0)
    position = rows[:, :, None] * ROWS + jnp.arange(ROWS, dtype=jnp.int32)
    seen = (position < limits[:, None, None]).astype(F32).reshape(PER_GROUP, -1)
    seen = jnp.tile(seen, (4, 1))
    gain = lax.dynamic_slice_in_dim(norm_gains[0, 3], my_index * SHARE, SHARE, 0)
    gain = jnp.pad(gain, (0, LANES - SHARE))[None]
    payload = attend_call(me, got, seen, cache.reshape(2, PER_GROUP, -1, 2 * HEAD_DIM))
    with jax.named_scope("attended"):
        own_att = to_chips(payload)
    other_att = core_swap(own_att)
    other_pages = core_swap(got[:, PAGE_TILES : 2 * PAGE_TILES])
    payload = mix_call(me, own_att, other_att, out_weight)
    with jax.named_scope("mixed"):
        own_mix = to_chips(payload)
    other_mix = core_swap(own_mix)
    keep, send, stream = ffn_call(me, own_mix, other_mix, hidden_in, norm_gains, gate_up_weight, down_weight)
    chip = (keep.astype(F32) + core_swap(send).astype(F32)).astype(BF16)
    with jax.named_scope("branch"):
        got_branch = to_chips(chip)
    portion, square = portion_call(me, got_branch)
    square = square + core_swap(square)
    with jax.named_scope("squares"):
        squares = to_chips(jnp.broadcast_to(square[None], (CHIPS, 1, LANES)))
    result = finish_call(me, portion, stream, squares, gain)
    decoded = decode_call(me, lengths, got, other_pages, own_att, other_att)
    return result, decoded[None, None]


def solution(mesh):
    torus = Mesh(mesh.devices.reshape(mesh.shape["grp"], 8, 8, 2), ("grp", "tp_0", "tp_1", "tp_2"))
    return jax.shard_map(
        on_device,
        mesh=torus,
        in_specs=(
            P("grp", None),
            P(TP, None, None, "grp", None, None, None),
            P("grp"),
            P("grp", None),
            P(None, TP, None),
            P(None, TP, None),
            P(None, None, TP, None),
            P(None, TP, None),
            P(),
        ),
        out_specs=(P("grp", TP), P(TP, None, None, "grp", None, None)),
        check_vma=False,
    )
```

profile of v0, /device:TPU:513, one launch (start us, length us, event | category | flops | bytes accessed | tf_op | source)
XLA Modules:
  0.0 202.6 jit_solution(2081627442643231565)
XLA Ops:
  0.6 20.5 %collective-permute-start = (bf16[1,64,4608]{2,1,0:T(8,128)(2,1)}, bf16[1,64,4608]{2,1,0:T(8,128)(2,1)S(1)}, u32[]{:S(2)}, u32[]{:S(2)}) collective-permute-start(bf16[1,64,4608]{2,1,0:T(8,128)(2,1)} %own_ref.1), channel_id=1, source_target_pairs={{0,1},{1,0},{2,3},{3,2},{4,5},{5,4},{6,7},{7,6},{8,9},{9,8},{10,11... | collective-permute-start | bytes 1769480 | tf_op jit(solution)/shard_map/ppermute | solution.py:355
  21.2 0.7 convert_element_type.21
  21.8 1.6 copy-done.1
  23.4 0.7 copy-done.8
  24.1 2.0 %pages.1.buf_ref = bf16[64,17,8,128]{3,2,1,0:T(8,128)(2,1)S(1)} custom-call(s32[1]{0:T(128)} %bitcast.me_ref, s32[32,128]{1,0:T(8,128)S(1)} %copy-done.8, bf16[2,2,128,8,256]{4,3,2,1,0:T(8,128)(2,1)S(1)} %bitcast.10), custom_call_target="tpu_custom_call" | custom-call | tf_op jit(solution)/shard_map/pages/pallas_call | solution.py:363
  26.4 0.7 qkv.1
  27.1 1.4 copy-done
  28.5 6.7 %all-to-all-start = ((bf16[64,17,8,128]{3,2,1,0:T(8,128)(2,1)}), bf16[64,17,8,128]{3,2,1,0:T(8,128)(2,1)S(1)}, u32[]{:S(2)}, u32[]{:S(2)}) async-start(bf16[64,17,8,128]{3,2,1,0:T(8,128)(2,1)} %copy-done), calls=%async_computation | async-start | bytes 4456448 | tf_op jit(solution)/shard_map/bulk/all_to_all | solution.py:359
  35.3 0.7 dynamic-slice_multiply_fusion
  36.4 54.5 %all-to-all-done.got_ref = bf16[64,17,8,128]{3,2,1,0:T(8,128)(2,1)S(1)} async-done(((bf16[64,17,8,128]{3,2,1,0:T(8,128)(2,1)}), bf16[64,17,8,128]{3,2,1,0:T(8,128)(2,1)S(1)}, u32[]{:S(2)}, u32[]{:S(2)}) %all-to-all-start) | async-done | bytes 2228256 | tf_op jit(solution)/shard_map/bulk/all_to_all | solution.py:359
  90.9 1.6 copy-done.2
  92.5 0.8 attend.1
  93.3 26.0 %all_to_all.25.own_ref.own_new_ref = bf16[64,16,128]{2,1,0:T(8,128)(2,1)S(1)} all-to-all(bf16[64,16,128]{2,1,0:T(8,128)(2,1)S(1)} %attend.1), channel_id=1, replica_groups=mesh['grp'=2,'tp_0'=8,'tp_1'=8,'tp_2'=2] {'tp_0','tp_1'}, dimensions={0} | all-to-all | bytes 524288 | tf_op jit(solution)/shard_map/attended/all_to_all | solution.py:359
  119.3 3.5 %collective-permute-start.1 = (bf16[64,16,128]{2,1,0:T(8,128)(2,1)S(1)}, bf16[64,16,128]{2,1,0:T(8,128)(2,1)S(1)}, u32[]{:S(2)}, u32[]{:S(2)}) collective-permute-start(bf16[64,16,128]{2,1,0:T(8,128)(2,1)S(1)} %all_to_all.25.own_ref.own_new_ref), channel_id=1, source_target_pairs={{0,1},{1,0},{2,3},{3,2},{4,5},{5,4},{6,7},{7,6},{8,9},{9,8},{10,11... | collective-permute-start | bytes 786440 | tf_op jit(solution)/shard_map/ppermute | solution.py:355
  122.8 1.2 collective-permute-done.1.other_ref.other_new_ref
  124.0 1.0 mix.1
  125.0 21.7 %all_to_all.26.own_ref = bf16[64,32,128]{2,1,0:T(8,128)(2,1)S(1)} all-to-all(bf16[64,32,128]{2,1,0:T(8,128)(2,1)S(1)} %mix.1), channel_id=1, replica_groups=mesh['grp'=2,'tp_0'=8,'tp_1'=8,'tp_2'=2] {'tp_0','tp_1'}, dimensions={0} | all-to-all | bytes 1048576 | tf_op jit(solution)/shard_map/mixed/all_to_all | solution.py:359
  146.6 2.2 %collective-permute-start.2 = (bf16[64,32,128]{2,1,0:T(8,128)(2,1)S(1)}, bf16[64,32,128]{2,1,0:T(8,128)(2,1)S(1)}, u32[]{:S(2)}, u32[]{:S(2)}) collective-permute-start(bf16[64,32,128]{2,1,0:T(8,128)(2,1)S(1)} %all_to_all.26.own_ref), channel_id=1, source_target_pairs={{0,1},{1,0},{2,3},{3,2},{4,5},{5,4},{6,7},{7,6},{8,9},{9,8},{10,11... | collective-permute-start | bytes 1572872 | tf_op jit(solution)/shard_map/ppermute | solution.py:355
  148.9 1.5 collective-permute-done.2.other_ref
  150.4 3.7 %ffn.1 = (bf16[64,32,128]{2,1,0:T(8,128)(2,1)S(1)}, bf16[64,32,128]{2,1,0:T(8,128)(2,1)S(1)}, f32[32,128]{1,0:T(8,128)S(1)}) custom-call(s32[1]{0:T(128)} %bitcast.me_ref, bf16[64,32,128]{2,1,0:T(8,128)(2,1)S(1)} %all_to_all.26.own_ref, bf16[64,32,128]{2,1,0:T(8,128)(2,1)S(1)} %collective-permute-done.2.other_ref, f32[32,4608]{1,0:T(8,128)S(1)} %copy-done.3, ...), custom_call_target="tpu_custom_call" | custom-call | tf_op jit(solution)/shard_map/ffn/pallas_call | solution.py:409
  154.6 1.5 collective-permute-done.3
  156.1 0.9 add_convert_fusion
  157.1 7.4 %all-to-all-start.3 = ((bf16[64,32,128]{2,1,0:T(8,128)(2,1)}), bf16[64,32,128]{2,1,0:T(8,128)(2,1)S(1)}, u32[]{:S(2)}, u32[]{:S(2)}) async-start(bf16[64,32,128]{2,1,0:T(8,128)(2,1)} %add_convert_fusion), calls=%async_computation.3 | async-start | bytes 1048576 | tf_op jit(solution)/shard_map/branch/all_to_all | solution.py:359
  164.5 1.1 slice.8
  165.6 0.7 collective-permute-start.5
  166.3 13.6 %all-to-all-done.3.got_ref = bf16[64,32,128]{2,1,0:T(8,128)(2,1)S(1)} async-done(((bf16[64,32,128]{2,1,0:T(8,128)(2,1)}), bf16[64,32,128]{2,1,0:T(8,128)(2,1)S(1)}, u32[]{:S(2)}, u32[]{:S(2)}) %all-to-all-start.3) | async-done | bytes 524320 | tf_op jit(solution)/shard_map/branch/all_to_all | solution.py:359
  180.1 3.2 %collective-permute-start.4 = (f32[1,128]{1,0:T(1,128)S(1)}, f32[1,128]{1,0:T(1,128)S(1)}, u32[]{:S(2)}, u32[]{:S(2)}) collective-permute-start(f32[1,128]{1,0:T(1,128)S(1)} %get-tuple-element.11), channel_id=1, source_target_pairs={{0,1},{1,0},{2,3},{3,2},{4,5},{5,4},{6,7},{7,6},{8,9},{9,8},{10,11... | collective-permute-start | bytes 1544 | tf_op jit(solution)/shard_map/ppermute | solution.py:355
  183.4 0.7 collective-permute-done.4
  184.8 7.2 %all-to-all-start.4 = ((f32[64,1,128]{2,1,0:T(1,128)}), f32[64,1,128]{2,1,0:T(1,128)S(1)}, u32[]{:S(2)}, u32[]{:S(2)}) async-start(f32[64,1,128]{2,1,0:T(1,128)} %broadcast_in_dim.24), calls=%async_computation.4 | async-start | bytes 65536 | tf_op jit(solution)/shard_map/squares/all_to_all | solution.py:359
  192.0 3.3 %decode.1 = bf16[2,32,8,2048]{3,2,1,0:T(8,128)(2,1)} custom-call(s32[1]{0:T(128)} %bitcast.me_ref, s32[32]{0:T(128)S(1)} %copy-done.9, bf16[64,17,8,128]{3,2,1,0:T(8,128)(2,1)S(1)} %all-to-all-done.got_ref, bf16[64,8,8,128]{3,2,1,0:T(8,128)(2,1)} %collective-permute-done.5.other_ref, bf16[64,16,128]{2,1,0:T(8,128)(2,1)S(1)} %all_to_all.25.own_ref.own_new_ref, ...), custom_call_target="tpu_custom_call" | custom-call | tf_op jit(solution)/shard_map/decode/pallas_call | solution.py:440
  195.3 6.5 %all-to-all-done.4.squares_ref = f32[64,1,128]{2,1,0:T(1,128)S(1)} async-done(((f32[64,1,128]{2,1,0:T(1,128)}), f32[64,1,128]{2,1,0:T(1,128)S(1)}, u32[]{:S(2)}, u32[]{:S(2)}) %all-to-all-start.4) | async-done | bytes 32800 | tf_op jit(solution)/shard_map/squares/all_to_all | solution.py:359
  201.8 0.8 finish.1
  (35 shorter events, 2.2 us)
Async XLA Ops:
  0.6 25.7 %collective-permute-start = (bf16[1,64,4608]{2,1,0:T(8,128)(2,1)}, bf16[1,64,4608]{2,1,0:T(8,128)(2,1)S(1)}, u32[]{:S(2)}, u32[]{:S(2)}) collective-permute-start(bf16[1,64,4608]{2,1,0:T(8,128)(2,1)} %own_ref.1), channel_id=1, source_target_pairs={{0,1},{1,0},{2,3},{3,2},{4,5},{5,4},{6,7},{7,6},{8,9},{9,8},{10,11... | collective-permute-start | bytes 1769480 | tf_op jit(solution)/shard_map/ppermute | solution.py:355
  21.8 1.6 copy-start.1
  23.4 0.7 copy-start.8
  24.1 2.2 %copy-start.3 = (f32[32,4608]{1,0:T(8,128)S(1)}, f32[32,4608]{1,0:T(8,128)}, u32[]{:S(2)}) copy-start(f32[32,4608]{1,0:T(8,128)} %hidden_ref.3) | copy-start | bytes 1769476
  24.1 2.2 %copy-start.5 = (bf16[1,64,4608]{2,1,0:T(8,128)(2,1)S(1)}, bf16[1,64,4608]{2,1,0:T(8,128)(2,1)}, u32[]{:S(2)}) copy-start(bf16[1,64,4608]{2,1,0:T(8,128)(2,1)} %own_ref.1) | copy-start | bytes 1769476
  24.1 2.2 %copy-start.6 = (f32[1,4,4608]{2,1,0:T(4,128)S(1)}, f32[1,4,4608]{2,1,0:T(4,128)}, u32[]{:S(2)}) copy-start(f32[1,4,4608]{2,1,0:T(4,128)} %gain_ref.3) | copy-start | bytes 221188
  27.1 1.4 copy-start
  28.5 6.7 %copy-start.9 = (s32[32]{0:T(128)S(1)}, s32[32]{0:T(128)}, u32[]{:S(2)}) copy-start(s32[32]{0:T(128)} %lengths_ref.1) | copy-start | bytes 388
  28.5 62.4 %all-to-all-start = ((bf16[64,17,8,128]{3,2,1,0:T(8,128)(2,1)}), bf16[64,17,8,128]{3,2,1,0:T(8,128)(2,1)S(1)}, u32[]{:S(2)}, u32[]{:S(2)}) async-start(bf16[64,17,8,128]{3,2,1,0:T(8,128)(2,1)} %copy-done), calls=%async_computation | async-start | bytes 4456448 | tf_op jit(solution)/shard_map/bulk/all_to_all | solution.py:359
  90.9 1.6 copy-start.2
  92.5 31.5 %copy-start.7 = (bf16[1,36,4096]{2,1,0:T(8,128)(2,1)S(1)}, bf16[1,36,4096]{2,1,0:T(8,128)(2,1)}, u32[]{:S(2)}) copy-start(bf16[1,36,4096]{2,1,0:T(8,128)(2,1)} %weight_ref.1) | copy-start | bytes 884740
  93.3 57.1 %copy-start.4 = (bf16[1,144,4608]{2,1,0:T(8,128)(2,1)S(1)}, bf16[1,144,4608]{2,1,0:T(8,128)(2,1)}, u32[]{:S(2)}) copy-start(bf16[1,144,4608]{2,1,0:T(8,128)(2,1)} %down_ref.1) | copy-start | bytes 3981316
  119.3 4.7 %collective-permute-start.1 = (bf16[64,16,128]{2,1,0:T(8,128)(2,1)S(1)}, bf16[64,16,128]{2,1,0:T(8,128)(2,1)S(1)}, u32[]{:S(2)}, u32[]{:S(2)}) collective-permute-start(bf16[64,16,128]{2,1,0:T(8,128)(2,1)S(1)} %all_to_all.25.own_ref.own_new_ref), channel_id=1, source_target_pairs={{0,1},{1,0},{2,3},{3,2},{4,5},{5,4},{6,7},{7,6},{8,9},{9,8},{10,11... | collective-permute-start | bytes 786440 | tf_op jit(solution)/shard_map/ppermute | solution.py:355
  146.6 3.8 %collective-permute-start.2 = (bf16[64,32,128]{2,1,0:T(8,128)(2,1)S(1)}, bf16[64,32,128]{2,1,0:T(8,128)(2,1)S(1)}, u32[]{:S(2)}, u32[]{:S(2)}) collective-permute-start(bf16[64,32,128]{2,1,0:T(8,128)(2,1)S(1)} %all_to_all.26.own_ref), channel_id=1, source_target_pairs={{0,1},{1,0},{2,3},{3,2},{4,5},{5,4},{6,7},{7,6},{8,9},{9,8},{10,11... | collective-permute-start | bytes 1572872 | tf_op jit(solution)/shard_map/ppermute | solution.py:355
  154.1 2.0 %collective-permute-start.3 = (bf16[64,32,128]{2,1,0:T(8,128)(2,1)S(1)}, bf16[64,32,128]{2,1,0:T(8,128)(2,1)S(1)}, u32[]{:S(2)}, u32[]{:S(2)}) collective-permute-start(bf16[64,32,128]{2,1,0:T(8,128)(2,1)S(1)} %get-tuple-element.8), channel_id=1, source_target_pairs={{0,1},{1,0},{2,3},{3,2},{4,5},{5,4},{6,7},{7,6},{8,9},{9,8},{10,11... | collective-permute-start | bytes 1572872 | tf_op jit(solution)/shard_map/ppermute | solution.py:355
  157.1 22.8 %all-to-all-start.3 = ((bf16[64,32,128]{2,1,0:T(8,128)(2,1)}), bf16[64,32,128]{2,1,0:T(8,128)(2,1)S(1)}, u32[]{:S(2)}, u32[]{:S(2)}) async-start(bf16[64,32,128]{2,1,0:T(8,128)(2,1)} %add_convert_fusion), calls=%async_computation.3 | async-start | bytes 1048576 | tf_op jit(solution)/shard_map/branch/all_to_all | solution.py:359
  165.6 26.4 %collective-permute-start.5 = (bf16[64,8,8,128]{3,2,1,0:T(8,128)(2,1)}, bf16[64,8,8,128]{3,2,1,0:T(8,128)(2,1)}, u32[]{:S(2)}, u32[]{:S(2)}) collective-permute-start(bf16[64,8,8,128]{3,2,1,0:T(8,128)(2,1)} %slice.8), channel_id=1, source_target_pairs={{0,1},{1,0},{2,3},{3,2},{4,5},{5,4},{6,7},{7,6},{8,9},{9,8},{10,11... | collective-permute-start | bytes 3145736 | tf_op jit(solution)/shard_map/ppermute | solution.py:355
  180.1 4.0 %collective-permute-start.4 = (f32[1,128]{1,0:T(1,128)S(1)}, f32[1,128]{1,0:T(1,128)S(1)}, u32[]{:S(2)}, u32[]{:S(2)}) collective-permute-start(f32[1,128]{1,0:T(1,128)S(1)} %get-tuple-element.11), channel_id=1, source_target_pairs={{0,1},{1,0},{2,3},{3,2},{4,5},{5,4},{6,7},{7,6},{8,9},{9,8},{10,11... | collective-permute-start | bytes 1544 | tf_op jit(solution)/shard_map/ppermute | solution.py:355
  184.8 17.1 %all-to-all-start.4 = ((f32[64,1,128]{2,1,0:T(1,128)}), f32[64,1,128]{2,1,0:T(1,128)S(1)}, u32[]{:S(2)}, u32[]{:S(2)}) async-start(f32[64,1,128]{2,1,0:T(1,128)} %broadcast_in_dim.24), calls=%async_computation.4 | async-start | bytes 65536 | tf_op jit(solution)/shard_map/squares/all_to_all | solution.py:359
where the time goes:
time: 203 us
  waiting for transfers between devices  79.6 us (39%)
  starting transfers between devices  51.9 us (26%)
  blocking collectives  47.7 us (23%)
  Pallas kernels  12.5 us (6%)
  local copies, waits for them, and re-layouts  7.58 us (4%)
  other arithmetic  2.51 us (1%)
    all_to_all x3, waiting for transfers between devices, to_chips(): return lax.all_to_all(tiles, XY, 0, 0, tiled=True)  74.6 us
    all_to_all x2, blocking collectives, to_chips(): return lax.all_to_all(tiles, XY, 0, 0, tiled=True)  47.7 us
    ppermute x6, starting transfers between devices, core_swap(): return lax.ppermute(shard, 'tp_2', [(0, 1), (1, 0)])  30.6 us
    all_to_all x3, starting transfers between devices, to_chips(): return lax.all_to_all(tiles, XY, 0, 0, tiled=True)  21.3 us
    unnamed x20, local copies, waits for them, and re-layouts  5.32 us
    ppermute x6, waiting for transfers between devices, core_swap(): return lax.ppermute(shard, 'tp_2', [(0, 1), (1, 0)])  4.99 us
  transfers between devices with their start and end apart: 9, of which 7 were waited for; matrix products, arithmetic and copies ran while one was open for 2% of the time, Pallas kernels for 3%

commit v1 on v0

--- a/solution.py
+++ b/solution.py
@@ -1,5 +1,3 @@
-import functools
-
 import jax
 import jax.numpy as jnp
 from jax import lax
@@ -29,10 +27,11 @@
 SHARE = D // (2 * CHIPS)
 BLOCKS = D // LANES
 BATCH = 32
+HALF = BATCH // 2
 PER_GROUP = 2
 PAGE_TILES = 2 * PER_GROUP * 2
 BULK_TILES = 2 * PAGE_TILES + 1
-VMEM_LIMIT = 48 * 1024 * 1024
+VMEM_LIMIT = 24 * 1024 * 1024
 
 
 def smem():
@@ -43,17 +42,12 @@
     return pl.BlockSpec(memory_space=pltpu.VMEM)
 
 
-def anywhere():
-    return pl.BlockSpec(memory_space=pl.ANY)
-
-
-def call(kernel, out_shape, in_specs, out_specs, name, **more):
+def call(kernel, out_shape, in_specs, out_specs, **more):
     return pl.pallas_call(
         kernel,
         out_shape=out_shape,
         in_specs=in_specs,
         out_specs=out_specs,
-        name=name,
         compiler_params=pltpu.CompilerParams(vmem_limit_bytes=VMEM_LIMIT),
         **more,
     )
@@ -79,10 +73,12 @@
     return SOFTCAP * jnp.tanh(raw_scores / SOFTCAP)
 
 
-def pages_kernel(me_ref, table_ref, cache_ref, out_ref):
+def pages_kernel(me_ref, table_ref, cache_ref, out_ref, held_ref, sem):
     me = me_ref[0]
     core = me & 1
     group = me >> 3
+    keep = pltpu.make_async_copy(cache_ref, held_ref, sem)
+    keep.start()
 
     def place(j, carry):
         for e in range(PER_GROUP):
@@ -96,6 +92,7 @@
         return carry
 
     lax.fori_loop(0, 2 * CHIPS, place, 0, unroll=4)
+    keep.wait()
 
 
 def qkv_kernel(
@@ -126,7 +123,7 @@
     copy.wait()
 
 
-def attend_kernel(me_ref, got_ref, seen_ref, cache_ref, out_ref):
+def attend_kernel(me_ref, lengths_ref, got_ref, table_ref, cache_ref, out_ref):
     me = me_ref[0]
     group = me >> 3
     slot = me & 7
@@ -157,7 +154,17 @@
             keys = cache_ref[0, ee, :, a * LANES : a * LANES + LANES]
             part = nt_dot(q16, keys)
             scores = jnp.where(((row & 1) == ee) & ((row >> 2) == a), part, scores)
-    weights = jnp.where(seen_ref[...] > 0.5, jnp.exp(capped(scores * scale)), 0.0)
+    pages = 2 * CHIPS
+    table_row = iota((BATCH, pages), 0)
+    lines = []
+    for ee in range(PER_GROUP):
+        chosen_row = jnp.where(table_row == group * PER_GROUP + ee, table_ref[...], 0)
+        lines.append(jnp.sum(chosen_row, axis=0, keepdims=True))
+    blocks = jnp.where((row & 1) == 0, lines[0], lines[1]).astype(F32).astype(BF16)
+    spread = jnp.where(iota((pages, ROWS * pages), 1) >> 3 == iota((pages, ROWS * pages), 0), 1.0, 0.0)
+    position = nn_dot(blocks, spread.astype(BF16)).astype(jnp.int32) * ROWS + (iota((ROWS, ROWS * pages), 1) & 7)
+    limit = jnp.where((row & 1) == 0, lengths_ref[group * PER_GROUP], lengths_ref[group * PER_GROUP + 1])
+    weights = jnp.where(position < limit, jnp.exp(capped(scores * scale)), 0.0)
     own = jnp.exp(capped(jnp.sum(q * new_k, axis=-1, keepdims=True) * scale))
     denominator = jnp.sum(weights, axis=-1, keepdims=True) + own
     w16 = weights.astype(BF16)
@@ -194,20 +201,23 @@
             [weight_ref[0, :, (2 * y + c) * 512 : (2 * y + c) * 512 + 512] for y in range(QUARTERS)], axis=1
         )
         mixed = mixed + nt_dot(left, right)
-    wide = jnp.concatenate(
-        [mixed.astype(BF16).astype(F32), jnp.zeros((BATCH, LANES - SHARE), F32)], axis=1
-    )
-    turned = pltpu.roll(wide, (me * SHARE) % LANES, 1).astype(BF16)
-    out_ref[...] = jnp.broadcast_to(turned[None], (CHIPS, BATCH, LANES))
-
-
-def window(blocks, j):
-    lane = iota((BATCH, LANES), 1)
+    values = mixed.astype(BF16).astype(F32)
+    gap = jnp.zeros((HALF, LANES // 2 - SHARE), F32)
+    packed = jnp.concatenate([values[:HALF], gap, values[HALF:], gap], axis=1)
+    turned = pltpu.roll(packed, (me * SHARE) % LANES, 1).astype(BF16)
+    out_ref[...] = jnp.broadcast_to(turned[None], (CHIPS, HALF, LANES))
+
+
+def window(low_ref, high_ref, j):
+    lane = iota((HALF, LANES), 1)
+    far = (lane + LANES // 2) % LANES
     v, off = divmod(j * SHARE, LANES)
-    here = blocks(v)
+    low = low_ref[v]
+    high = high_ref[v]
     if off + SHARE > LANES:
-        here = jnp.where(lane >= off, here, blocks(v + 1))
-    return here
+        low = jnp.where(lane >= off, low, low_ref[v + 1])
+        high = jnp.where(far >= off, high, high_ref[v + 1])
+    return jnp.where((lane - off) % LANES < LANES // 2, low, high)
 
 
 def ffn_kernel(
@@ -222,28 +232,33 @@
     send_ref,
     stream_ref,
     wide_ref,
-    blocks_ref,
+    low_ref,
+    high_ref,
     ffn_ref,
 ):
     me = me_ref[0]
     first = (me & 1) == 0
     lane = iota((BATCH, LANES), 1)
+    near = iota((HALF, LANES), 1)
+    far = (near + LANES // 2) % LANES
     total = jnp.zeros((BATCH, LANES), F32)
     for v in range(BLOCKS):
-        block = jnp.zeros((BATCH, LANES), F32)
+        low = high = None
         for j in range((LANES * v) // SHARE, (LANES * v + LANES - 1) // SHARE + 1):
             own = own_ref[j >> 1]
             other = other_ref[j >> 1]
             piece = (jnp.where(first, own, other) if j % 2 == 0 else jnp.where(first, other, own)).astype(F32)
             start = j * SHARE - LANES * v
-            block = piece if start <= 0 else jnp.where(lane >= start, piece, block)
-        blocks_ref[v] = block
+            low = piece if low is None else jnp.where(near >= start, piece, low)
+            high = piece if high is None else jnp.where(far >= start, piece, high)
+        block = jnp.concatenate([low, pltpu.roll(high, LANES // 2, 1)], axis=0)
+        wide_ref[v] = block
         total = total + block * block
     scale = lax.rsqrt(jnp.sum(total, axis=-1, keepdims=True) * (1.0 / D) + EPSILON)
     total = jnp.zeros((BATCH, LANES), F32)
     for v in range(BLOCKS):
         cols = slice(LANES * v, LANES * v + LANES)
-        block = hidden_ref[:, cols] + blocks_ref[v] * scale * (1.0 + gain_ref[0, 1:2, cols])
+        block = hidden_ref[:, cols] + wide_ref[v] * scale * (1.0 + gain_ref[0, 1:2, cols])
         wide_ref[v] = block
         total = total + block * block
     scale = lax.rsqrt(jnp.sum(total, axis=-1, keepdims=True) * (1.0 / D) + EPSILON)
@@ -255,10 +270,12 @@
     up = nt_dot(ffn_in, gate_up_ref[0, 1])
     active = (jax.nn.gelu(gate, approximate=True) * up).astype(BF16)
     for v in range(BLOCKS):
-        blocks_ref[v] = nn_dot(active, down_ref[0, :, LANES * v : LANES * v + LANES])
+        block = nn_dot(active, down_ref[0, :, LANES * v : LANES * v + LANES])
+        low_ref[v] = block[:HALF]
+        high_ref[v] = pltpu.roll(block[HALF:], LANES // 2, 1)
     for p in range(CHIPS):
-        even = window(lambda v: blocks_ref[v], 2 * p)
-        odd = window(lambda v: blocks_ref[v], 2 * p + 1)
+        even = window(low_ref, high_ref, 2 * p)
+        odd = window(low_ref, high_ref, 2 * p + 1)
         keep_ref[p] = jnp.where(first, even, odd).astype(BF16)
         send_ref[p] = jnp.where(first, odd, even).astype(BF16)
     start = me * SHARE
@@ -275,23 +292,30 @@
 
 def portion_kernel(me_ref, got_ref, portion_ref, square_ref):
     me = me_ref[0]
-    total = jnp.zeros((BATCH, LANES), F32)
+    total = jnp.zeros((HALF, LANES), F32)
     for p in range(CHIPS):
         total = total + got_ref[p].astype(F32)
-    mine = to_front(total, me)
+    packed = to_front(total, me)
+    mine = jnp.concatenate([packed, pltpu.roll(packed, LANES // 2, 1)], axis=0)
     portion_ref[...] = mine
     lane = iota((BATCH, LANES), 1)
     square = jnp.sum(jnp.where(lane < SHARE, mine * mine, 0.0), axis=-1, keepdims=True)
-    square_ref[...] = jnp.sum(jnp.where(iota((BATCH, LANES), 0) == lane, square, 0.0), axis=0, keepdims=True)
-
-
-def finish_kernel(me_ref, portion_ref, stream_ref, squares_ref, gain_ref, out_ref):
-    me = me_ref[0]
-    squares = jnp.sum(squares_ref[...], axis=0)
+    line = jnp.sum(jnp.where(iota((BATCH, LANES), 0) == lane, square, 0.0), axis=0, keepdims=True)
+    square_ref[...] = jnp.broadcast_to(line[None], (CHIPS, 1, LANES))
+
+
+def finish_kernel(me_ref, portion_ref, stream_ref, own_ref, other_ref, gain_ref, out_ref):
+    me = me_ref[0]
+    squares = jnp.sum(own_ref[...] + other_ref[...], axis=0)
     lane = iota((BATCH, LANES), 1)
     column = jnp.sum(jnp.where(iota((BATCH, LANES), 0) == lane, squares, 0.0), axis=-1, keepdims=True)
     scale = lax.rsqrt(column * (1.0 / D) + EPSILON)
-    done = to_front(stream_ref[...], me) + portion_ref[...] * scale * (1.0 + gain_ref[...])
+    at = (me * SHARE) // LANES
+    after = jnp.minimum(at + 1, BLOCKS - 1)
+    here = gain_ref[0, 3:4, pl.ds(pl.multiple_of(at * LANES, LANES), LANES)]
+    there = gain_ref[0, 3:4, pl.ds(pl.multiple_of(after * LANES, LANES), LANES)]
+    gain = jnp.where(lane >= (me * SHARE) % LANES, here, there)
+    done = to_front(stream_ref[...], me) + portion_ref[...] * scale * (1.0 + to_front(gain, me))
     out_ref[...] = done[:, :SHARE]
 
 
@@ -362,10 +386,10 @@
 def pages_call(me, table, cache):
     return call(
         pages_kernel,
-        shaped((CHIPS, BULK_TILES, ROWS, LANES), BF16),
+        (shaped((CHIPS, BULK_TILES, ROWS, LANES), BF16), shaped(cache.shape, BF16)),
         [smem(), smem(), vmem()],
-        vmem(),
-        "pages",
+        (vmem(), vmem()),
+        scratch_shapes=[pltpu.SemaphoreType.DMA],
     )(me, table, cache)
 
 
@@ -373,20 +397,20 @@
     return call(
         qkv_kernel,
         shaped(buf.shape, BF16),
-        [smem()] + [vmem()] * 6 + [anywhere()],
-        anywhere(),
-        "qkv",
+        [smem()] + [vmem()] * 6 + [pl.BlockSpec(memory_space=pl.ANY)],
+        pl.BlockSpec(memory_space=pl.ANY),
         scratch_shapes=[pltpu.VMEM((CHIPS, ROWS, LANES), BF16), pltpu.SemaphoreType.DMA],
         input_output_aliases={7: 0},
     )(me, hidden, gains, own, other, cosine, sine, buf)
 
 
-def attend_call(me, got, seen, cache):
+def attend_call(me, lengths, got, table, cache):
     return pl.pallas_call(
         attend_kernel,
         grid=(1,),
         out_shape=shaped((CHIPS, 2 * ROWS, LANES), BF16),
         in_specs=[
+            smem(),
             smem(),
             pl.BlockSpec((CHIPS, 1, ROWS, LANES), lambda i: (0, BULK_TILES - 1, 0, 0)),
             vmem(),
@@ -395,26 +419,24 @@
         out_specs=vmem(),
         name="attend",
         compiler_params=pltpu.CompilerParams(vmem_limit_bytes=VMEM_LIMIT),
-    )(me, got, seen, cache)
+    )(me, lengths, got, table, cache)
 
 
 def mix_call(me, own, other, weight):
-    return call(mix_kernel, shaped((CHIPS, BATCH, LANES), BF16), [smem()] + [vmem()] * 3, vmem(), "mix")(
-        me, own, other, weight
-    )
+    return call(mix_kernel, shaped((CHIPS, HALF, LANES), BF16), [smem()] + [vmem()] * 3, vmem())(me, own, other, weight)
 
 
 def ffn_call(me, own, other, hidden, gains, gate_up, down):
-    wide = shaped((CHIPS, BATCH, LANES), BF16)
+    wide = shaped((CHIPS, HALF, LANES), BF16)
     return call(
         ffn_kernel,
         (wide, wide, shaped((BATCH, LANES), F32)),
         [smem()] + [vmem()] * 6,
         (vmem(), vmem(), vmem()),
-        "ffn",
         scratch_shapes=[
             pltpu.VMEM((BLOCKS, BATCH, LANES), F32),
-            pltpu.VMEM((BLOCKS, BATCH, LANES), F32),
+            pltpu.VMEM((BLOCKS, HALF, LANES), F32),
+            pltpu.VMEM((BLOCKS, HALF, LANES), F32),
             pltpu.VMEM((BATCH, D), BF16),
         ],
     )(me, own, other, hidden, gains, gate_up, down)
@@ -423,16 +445,15 @@
 def portion_call(me, got):
     return call(
         portion_kernel,
-        (shaped((BATCH, LANES), F32), shaped((1, LANES), F32)),
+        (shaped((BATCH, LANES), F32), shaped((CHIPS, 1, LANES), F32)),
         [smem(), vmem()],
         (vmem(), vmem()),
-        "portion",
     )(me, got)
 
 
-def finish_call(me, portion, stream, squares, gain):
-    return call(finish_kernel, shaped((BATCH, SHARE), F32), [smem()] + [vmem()] * 4, vmem(), "finish")(
-        me, portion, stream, squares, gain
+def finish_call(me, portion, stream, own, other, gains):
+    return call(finish_kernel, shaped((BATCH, SHARE), F32), [smem()] + [vmem()] * 5, vmem())(
+        me, portion, stream, own, other, gains
     )
 
 
@@ -474,41 +495,27 @@
     down_weight,
     norm_gains,
 ):
-    my_index = lax.axis_index(TP)
-    me = jnp.full((1,), my_index, jnp.int32)
-    group = my_index // PREFILL_TP
+    me = jnp.full((1,), lax.axis_index(TP), jnp.int32)
     cache = prefill_cache[0, 0]
     other_rows = core_swap(qkv_weight)
-    buf = pages_call(me, page_table, cache)
+    buf, held = pages_call(me, page_table, cache)
     cosine, sine = rope_tables(lengths)
     buf = qkv_call(me, hidden_in, norm_gains, qkv_weight, other_rows, cosine, sine, buf)
-    with jax.named_scope("bulk"):
-        got = to_chips(buf)
-    rows = lax.dynamic_slice_in_dim(page_table, group * PER_GROUP, PER_GROUP, 0)
-    limits = lax.dynamic_slice_in_dim(lengths, group * PER_GROUP, PER_GROUP, 0)
-    position = rows[:, :, None] * ROWS + jnp.arange(ROWS, dtype=jnp.int32)
-    seen = (position < limits[:, None, None]).astype(F32).reshape(PER_GROUP, -1)
-    seen = jnp.tile(seen, (4, 1))
-    gain = lax.dynamic_slice_in_dim(norm_gains[0, 3], my_index * SHARE, SHARE, 0)
-    gain = jnp.pad(gain, (0, LANES - SHARE))[None]
-    payload = attend_call(me, got, seen, cache.reshape(2, PER_GROUP, -1, 2 * HEAD_DIM))
-    with jax.named_scope("attended"):
-        own_att = to_chips(payload)
+    got = to_chips(buf)
+    payload = attend_call(me, lengths, got, page_table, held.reshape(2, PER_GROUP, -1, 2 * HEAD_DIM))
+    own_att = to_chips(payload)
     other_att = core_swap(own_att)
-    other_pages = core_swap(got[:, PAGE_TILES : 2 * PAGE_TILES])
+    leaving = got[:, PAGE_TILES : 2 * PAGE_TILES]
+    other_pages = core_swap(leaving)
     payload = mix_call(me, own_att, other_att, out_weight)
-    with jax.named_scope("mixed"):
-        own_mix = to_chips(payload)
+    own_mix = to_chips(payload)
     other_mix = core_swap(own_mix)
     keep, send, stream = ffn_call(me, own_mix, other_mix, hidden_in, norm_gains, gate_up_weight, down_weight)
     chip = (keep.astype(F32) + core_swap(send).astype(F32)).astype(BF16)
-    with jax.named_scope("branch"):
-        got_branch = to_chips(chip)
+    got_branch = to_chips(chip)
     portion, square = portion_call(me, got_branch)
-    square = square + core_swap(square)
-    with jax.named_scope("squares"):
-        squares = to_chips(jnp.broadcast_to(square[None], (CHIPS, 1, LANES)))
-    result = finish_call(me, portion, stream, squares, gain)
+    squares = to_chips(square)
+    result = finish_call(me, portion, stream, squares, core_swap(squares), norm_gains)
     decoded = decode_call(me, lengths, got, other_pages, own_att, other_att)
     return result, decoded[None, None]
 

time: 203 us -> 192 us (0.946)
  blocking collectives: 47.7 us -> 142 us
  waiting for transfers between devices: 79.6 us -> 3.12 us
  starting transfers between devices: 51.9 us -> 30.5 us
  local copies, waits for them, and re-layouts: 7.58 us -> 3.34 us
    all_to_all x2 -> x5, blocking collectives: 47.7 us -> 142 us  [to_chips(): return lax.all_to_all(tiles, XY, 0, 0, tiled=True)]
    all_to_all x3 -> x0, waiting for transfers between devices: 74.6 us -> none  [to_chips(): return lax.all_to_all(tiles, XY, 0, 0, tiled=True)]
    all_to_all x3 -> x0, starting transfers between devices: 21.3 us -> none  [to_chips(): return lax.all_to_all(tiles, XY, 0, 0, tiled=True)]
    unnamed x20, local copies, waits for them, and re-layouts: 5.32 us -> 3.22 us
  transfers between devices with their start and end apart: 9 -> 6, of which waited for: 7 -> 3; matrix products, arithmetic and copies ran while one was open for 2% -> 1% of each run, Pallas kernels for 3% -> 3%
where the time goes in v1:
time: 192 us; the launch traced here: 191 us
  blocking collectives  142 us (74%)
  starting transfers between devices  30.5 us (16%)
  Pallas kernels  10.8 us (6%)
  local copies, waits for them, and re-layouts  3.34 us (2%)
  waiting for transfers between devices  3.12 us (2%)
    all_to_all x5, blocking collectives, to_chips(): return lax.all_to_all(tiles, XY, 0, 0, tiled=True)  142 us
    ppermute x6, starting transfers between devices, core_swap(): return lax.ppermute(shard, 'tp_2', [(0, 1), (1, 0)])  30.5 us
  transfers between devices with their start and end apart: 6, of which 3 were waited for; matrix products, arithmetic and copies ran while one was open for 1% of the time, Pallas kernels for 3%

profile of v1, /device:TPU:513, one launch (start us, length us, event | category | flops | bytes accessed | tf_op | source)
XLA Modules:
  0.0 191.2 jit_solution(16247798749012358008)
XLA Ops:
  0.6 20.5 %collective-permute-start = (bf16[1,64,4608]{2,1,0:T(8,128)(2,1)}, bf16[1,64,4608]{2,1,0:T(8,128)(2,1)S(1)}, u32[]{:S(2)}, u32[]{:S(2)}) collective-permute-start(bf16[1,64,4608]{2,1,0:T(8,128)(2,1)} %own_ref.1), channel_id=1, source_target_pairs={{0,1},{1,0},{2,3},{3,2},{4,5},{5,4},{6,7},{7,6},{8,9},{9,8},{10,11... | collective-permute-start | bytes 1769480 | tf_op jit(solution)/shard_map/ppermute | solution.py:379
  21.2 0.7 convert_element_type.12
  21.8 1.6 copy-done.2
  23.4 0.7 copy-done.8
  24.1 2.2 %shard_map.104 = (bf16[64,17,8,128]{3,2,1,0:T(8,128)(2,1)S(1)}, bf16[2,2,128,8,256]{4,3,2,1,0:T(8,128)(2,1)S(1)}) custom-call(s32[1]{0:T(128)} %bitcast.me_ref, s32[32,128]{1,0:T(8,128)S(1)} %copy-done.8, bf16[2,2,128,8,256]{4,3,2,1,0:T(8,128)(2,1)S(1)} %bitcast.5), custom_call_target="tpu_custom_call" | custom-call | tf_op jit(solution)/shard_map/pallas_call | solution.py:387
  26.3 0.1 multiply_sine_fusion
  26.5 0.0 copy-start.4
  26.5 0.9 copy-done.4
  27.4 0.7 shard_map.105
  28.1 0.0 copy-start.9
  28.1 65.5 %all_to_all.25.got_ref = bf16[64,17,8,128]{3,2,1,0:T(8,128)(2,1)S(1)} all-to-all(bf16[64,17,8,128]{3,2,1,0:T(8,128)(2,1)S(1)} %shard_map.105), channel_id=1, replica_groups=mesh['grp'=2,'tp_0'=8,'tp_1'=8,'tp_2'=2] {'tp_0','tp_1'}, dimensions={0} | all-to-all | bytes 4456448 | tf_op jit(solution)/shard_map/all_to_all | solution.py:383
  93.7 1.3 attend.1
  95.0 0.0 copy-start.3
  95.0 24.4 %all_to_all.26.own_ref.own_new_ref = bf16[64,16,128]{2,1,0:T(8,128)(2,1)S(1)} all-to-all(bf16[64,16,128]{2,1,0:T(8,128)(2,1)S(1)} %attend.1), channel_id=1, replica_groups=mesh['grp'=2,'tp_0'=8,'tp_1'=8,'tp_2'=2] {'tp_0','tp_1'}, dimensions={0} | all-to-all | bytes 524288 | tf_op jit(solution)/shard_map/all_to_all | solution.py:383
  119.4 3.5 %collective-permute-start.1 = (bf16[64,16,128]{2,1,0:T(8,128)(2,1)S(1)}, bf16[64,16,128]{2,1,0:T(8,128)(2,1)S(1)}, u32[]{:S(2)}, u32[]{:S(2)}) collective-permute-start(bf16[64,16,128]{2,1,0:T(8,128)(2,1)S(1)} %all_to_all.26.own_ref.own_new_ref), channel_id=1, source_target_pairs={{0,1},{1,0},{2,3},{3,2},{4,5},{5,4},{6,7},{7,6},{8,9},{9,8},{10,11... | collective-permute-start | bytes 786440 | tf_op jit(solution)/shard_map/ppermute | solution.py:379
  122.9 1.2 collective-permute-done.1.other_ref.other_new_ref
  124.1 1.0 shard_map.106
  125.1 17.5 %all_to_all.27.own_ref = bf16[64,16,128]{2,1,0:T(8,128)(2,1)S(1)} all-to-all(bf16[64,16,128]{2,1,0:T(8,128)(2,1)S(1)} %shard_map.106), channel_id=1, replica_groups=mesh['grp'=2,'tp_0'=8,'tp_1'=8,'tp_2'=2] {'tp_0','tp_1'}, dimensions={0} | all-to-all | bytes 524288 | tf_op jit(solution)/shard_map/all_to_all | solution.py:383
  142.6 2.8 %collective-permute-start.2 = (bf16[64,16,128]{2,1,0:T(8,128)(2,1)S(1)}, bf16[64,16,128]{2,1,0:T(8,128)(2,1)S(1)}, u32[]{:S(2)}, u32[]{:S(2)}) collective-permute-start(bf16[64,16,128]{2,1,0:T(8,128)(2,1)S(1)} %all_to_all.27.own_ref), channel_id=1, source_target_pairs={{0,1},{1,0},{2,3},{3,2},{4,5},{5,4},{6,7},{7,6},{8,9},{9,8},{10,11... | collective-permute-start | bytes 786440 | tf_op jit(solution)/shard_map/ppermute | solution.py:379
  145.5 1.2 collective-permute-done.2.other_ref
  146.6 2.0 %shard_map.107 = (bf16[64,16,128]{2,1,0:T(8,128)(2,1)S(1)}, bf16[64,16,128]{2,1,0:T(8,128)(2,1)S(1)}, f32[32,128]{1,0:T(8,128)S(1)}) custom-call(s32[1]{0:T(128)} %bitcast.me_ref, bf16[64,16,128]{2,1,0:T(8,128)(2,1)S(1)} %all_to_all.27.own_ref, bf16[64,16,128]{2,1,0:T(8,128)(2,1)S(1)} %collective-permute-done.2.other_ref, f32[32,4608]{1,0:T(8,128)S(1)} %copy-done.1, ...), custom_call_target="tpu_custom_call" | custom-call | tf_op jit(solution)/shard_map/pallas_call | solution.py:431
  148.6 0.5 collective-permute-start.3
  149.1 0.1 slice.4
  149.3 0.2 collective-permute-start.5
  149.5 0.8 collective-permute-done.3
  150.3 0.1 add_convert_fusion
  150.4 17.7 %all_to_all.28.got_ref = bf16[64,16,128]{2,1,0:T(8,128)(2,1)S(1)} all-to-all(bf16[64,16,128]{2,1,0:T(8,128)(2,1)S(1)} %add_convert_fusion), channel_id=1, replica_groups=mesh['grp'=2,'tp_0'=8,'tp_1'=8,'tp_2'=2] {'tp_0','tp_1'}, dimensions={0} | all-to-all | bytes 524288 | tf_op jit(solution)/shard_map/all_to_all | solution.py:383
  168.1 0.3 shard_map.108
  168.4 16.6 %all_to_all.29.own_ref = f32[64,1,128]{2,1,0:T(1,128)S(1)} all-to-all(f32[64,1,128]{2,1,0:T(1,128)S(1)} %get-tuple-element.15), channel_id=1, replica_groups=mesh['grp'=2,'tp_0'=8,'tp_1'=8,'tp_2'=2] {'tp_0','tp_1'}, dimensions={0} | all-to-all | bytes 65536 | tf_op jit(solution)/shard_map/all_to_all | solution.py:383
  185.0 2.9 %collective-permute-start.4 = (f32[64,1,128]{2,1,0:T(1,128)S(1)}, f32[64,1,128]{2,1,0:T(1,128)S(1)}, u32[]{:S(2)}, u32[]{:S(2)}) collective-permute-start(f32[64,1,128]{2,1,0:T(1,128)S(1)} %all_to_all.29.own_ref), channel_id=1, source_target_pairs={{0,1},{1,0},{2,3},{3,2},{4,5},{5,4},{6,7},{7,6},{8,9},{9,8},{10,11... | collective-permute-start | bytes 98312 | tf_op jit(solution)/shard_map/ppermute | solution.py:379
  187.9 2.5 %decode.1 = bf16[2,32,8,2048]{3,2,1,0:T(8,128)(2,1)} custom-call(s32[1]{0:T(128)} %bitcast.me_ref, s32[32]{0:T(128)S(1)} %copy-done.9, bf16[64,17,8,128]{3,2,1,0:T(8,128)(2,1)S(1)} %all_to_all.25.got_ref, bf16[64,8,8,128]{3,2,1,0:T(8,128)(2,1)S(1)} %collective-permute-done.5.other_ref, bf16[64,16,128]{2,1,0:T(8,128)(2,1)S(1)} %all_to_all.26.own_ref.own_new_ref, ...), custom_call_target="tpu_custom_call" | custom-call | tf_op jit(solution)/shard_map/decode/pallas_call | solution.py:461
  190.4 0.8 shard_map.109
  (18 shorter events, 0.0 us)
Async XLA Ops:
  0.6 25.9 %copy-start.1 = (f32[32,4608]{1,0:T(8,128)S(1)}, f32[32,4608]{1,0:T(8,128)}, u32[]{:S(2)}) copy-start(f32[32,4608]{1,0:T(8,128)} %hidden_ref.3) | copy-start | bytes 1769476
  0.6 25.9 %collective-permute-start = (bf16[1,64,4608]{2,1,0:T(8,128)(2,1)}, bf16[1,64,4608]{2,1,0:T(8,128)(2,1)S(1)}, u32[]{:S(2)}, u32[]{:S(2)}) collective-permute-start(bf16[1,64,4608]{2,1,0:T(8,128)(2,1)} %own_ref.1), channel_id=1, source_target_pairs={{0,1},{1,0},{2,3},{3,2},{4,5},{5,4},{6,7},{7,6},{8,9},{9,8},{10,11... | collective-permute-start | bytes 1769480 | tf_op jit(solution)/shard_map/ppermute | solution.py:379
  21.8 1.6 copy-start.2
  23.4 0.7 copy-start.8
  24.1 2.4 %copy-start.6 = (bf16[1,64,4608]{2,1,0:T(8,128)(2,1)S(1)}, bf16[1,64,4608]{2,1,0:T(8,128)(2,1)}, u32[]{:S(2)}) copy-start(bf16[1,64,4608]{2,1,0:T(8,128)(2,1)} %own_ref.1) | copy-start | bytes 1769476
  26.5 0.9 copy-start.4
  28.1 65.6 %copy-start.9 = (s32[32]{0:T(128)S(1)}, s32[32]{0:T(128)}, u32[]{:S(2)}) copy-start(s32[32]{0:T(128)} %lengths_ref.3) | copy-start | bytes 388
  93.7 30.4 %copy-start.7 = (bf16[1,36,4096]{2,1,0:T(8,128)(2,1)S(1)}, bf16[1,36,4096]{2,1,0:T(8,128)(2,1)}, u32[]{:S(2)}) copy-start(bf16[1,36,4096]{2,1,0:T(8,128)(2,1)} %weight_ref.1) | copy-start | bytes 884740
  93.7 53.0 %copy-start = (bf16[1,2,144,4608]{3,2,1,0:T(8,128)(2,1)S(1)}, bf16[1,2,144,4608]{3,2,1,0:T(8,128)(2,1)}, u32[]{:S(2)}) copy-start(bf16[1,2,144,4608]{3,2,1,0:T(8,128)(2,1)} %gate_up_ref.1) | copy-start | bytes 7962628
  93.7 53.0 %copy-start.5 = (f32[1,4,4608]{2,1,0:T(4,128)S(1)}, f32[1,4,4608]{2,1,0:T(4,128)}, u32[]{:S(2)}) copy-start(f32[1,4,4608]{2,1,0:T(4,128)} %gain_ref.5) | copy-start | bytes 221188
  95.0 51.6 %copy-start.3 = (bf16[1,144,4608]{2,1,0:T(8,128)(2,1)S(1)}, bf16[1,144,4608]{2,1,0:T(8,128)(2,1)}, u32[]{:S(2)}) copy-start(bf16[1,144,4608]{2,1,0:T(8,128)(2,1)} %down_ref.1) | copy-start | bytes 3981316
  119.4 4.7 %collective-permute-start.1 = (bf16[64,16,128]{2,1,0:T(8,128)(2,1)S(1)}, bf16[64,16,128]{2,1,0:T(8,128)(2,1)S(1)}, u32[]{:S(2)}, u32[]{:S(2)}) collective-permute-start(bf16[64,16,128]{2,1,0:T(8,128)(2,1)S(1)} %all_to_all.26.own_ref.own_new_ref), channel_id=1, source_target_pairs={{0,1},{1,0},{2,3},{3,2},{4,5},{5,4},{6,7},{7,6},{8,9},{9,8},{10,11... | collective-permute-start | bytes 786440 | tf_op jit(solution)/shard_map/ppermute | solution.py:379
  142.6 4.0 %collective-permute-start.2 = (bf16[64,16,128]{2,1,0:T(8,128)(2,1)S(1)}, bf16[64,16,128]{2,1,0:T(8,128)(2,1)S(1)}, u32[]{:S(2)}, u32[]{:S(2)}) collective-permute-start(bf16[64,16,128]{2,1,0:T(8,128)(2,1)S(1)} %all_to_all.27.own_ref), channel_id=1, source_target_pairs={{0,1},{1,0},{2,3},{3,2},{4,5},{5,4},{6,7},{7,6},{8,9},{9,8},{10,11... | collective-permute-start | bytes 786440 | tf_op jit(solution)/shard_map/ppermute | solution.py:379
  148.6 1.7 collective-permute-start.3
  149.3 38.6 %collective-permute-start.5 = (bf16[64,8,8,128]{3,2,1,0:T(8,128)(2,1)S(1)}, bf16[64,8,8,128]{3,2,1,0:T(8,128)(2,1)S(1)}, u32[]{:S(2)}, u32[]{:S(2)}) collective-permute-start(bf16[64,8,8,128]{3,2,1,0:T(8,128)(2,1)S(1)} %slice.4), channel_id=1, source_target_pairs={{0,1},{1,0},{2,3},{3,2},{4,5},{5,4},{6,7},{7,6},{8,9},{9,8},{10,11... | collective-permute-start | bytes 3145736 | tf_op jit(solution)/shard_map/ppermute | solution.py:379
  185.0 5.4 %collective-permute-start.4 = (f32[64,1,128]{2,1,0:T(1,128)S(1)}, f32[64,1,128]{2,1,0:T(1,128)S(1)}, u32[]{:S(2)}, u32[]{:S(2)}) collective-permute-start(f32[64,1,128]{2,1,0:T(1,128)S(1)} %all_to_all.29.own_ref), channel_id=1, source_target_pairs={{0,1},{1,0},{2,3},{3,2},{4,5},{5,4},{6,7},{7,6},{8,9},{9,8},{10,11... | collective-permute-start | bytes 98312 | tf_op jit(solution)/shard_map/ppermute | solution.py:379

commit v2 on v1

--- a/solution.py
+++ b/solution.py
@@ -42,6 +42,10 @@
     return pl.BlockSpec(memory_space=pltpu.VMEM)
 
 
+def hbm():
+    return pl.BlockSpec(memory_space=pltpu.HBM)
+
+
 def call(kernel, out_shape, in_specs, out_specs, **more):
     return pl.pallas_call(
         kernel,
@@ -73,26 +77,76 @@
     return SOFTCAP * jnp.tanh(raw_scores / SOFTCAP)
 
 
-def pages_kernel(me_ref, table_ref, cache_ref, out_ref, held_ref, sem):
+def pages_kernel(
+    me_ref,
+    lengths_hbm,
+    table_hbm,
+    cache_hbm,
+    weight_hbm,
+    hidden_hbm,
+    gain_hbm,
+    out_ref,
+    held_ref,
+    weight_ref,
+    hidden_ref,
+    gain_ref,
+    length_ref,
+    position_ref,
+    lengths_ref,
+    table_ref,
+    rows_ref,
+    sems,
+):
     me = me_ref[0]
     core = me & 1
     group = me >> 3
-    keep = pltpu.make_async_copy(cache_ref, held_ref, sem)
-    keep.start()
-
-    def place(j, carry):
-        for e in range(PER_GROUP):
-            block = table_ref[PER_GROUP * group + e, j]
-            chip = block >> 1
-            base = ((block & 1) ^ core) * PAGE_TILES + e * 2
-            for kv in range(2):
-                page = cache_ref[kv, e, j]
-                out_ref[chip, base + kv * 4] = page[:, :LANES]
-                out_ref[chip, base + kv * 4 + 1] = page[:, LANES:]
-        return carry
-
-    lax.fori_loop(0, 2 * CHIPS, place, 0, unroll=4)
-    keep.wait()
+    loads = [
+        (lengths_hbm, lengths_ref),
+        (table_hbm, rows_ref),
+        (table_hbm, table_ref),
+        (cache_hbm.at[0, 0], held_ref.at[0, 0]),
+        (cache_hbm.at[1, 0], held_ref.at[1, 0]),
+        (cache_hbm.at[0, 1], held_ref.at[0, 1]),
+        (cache_hbm.at[1, 1], held_ref.at[1, 1]),
+        (hidden_hbm, hidden_ref),
+        (weight_hbm, weight_ref),
+        (gain_hbm, gain_ref),
+    ]
+    loads = [pltpu.make_async_copy(src, dst, sems.at[i]) for i, (src, dst) in enumerate(loads)]
+    for load in loads:
+        load.start()
+    for load in loads[:3]:
+        load.wait()
+    row = iota((BATCH, HEAD_DIM // 2), 0)
+    spread_length = jnp.zeros((BATCH, HEAD_DIM // 2), F32)
+    for r in range(BATCH):
+        spread_length = jnp.where(row == r, lengths_ref[r].astype(F32), spread_length)
+    length_ref[...] = spread_length
+    pages = 2 * CHIPS
+    table_row = iota((BATCH, pages), 0)
+    lines = []
+    for e in range(PER_GROUP):
+        chosen_row = jnp.where(table_row == group * PER_GROUP + e, rows_ref[...], 0)
+        lines.append(jnp.sum(chosen_row, axis=0, keepdims=True))
+    blocks = jnp.where((iota((ROWS, 1), 0) & 1) == 0, lines[0], lines[1]).astype(F32).astype(BF16)
+    spread = jnp.where(iota((pages, ROWS * pages), 1) >> 3 == iota((pages, ROWS * pages), 0), 1.0, 0.0)
+    inside = iota((ROWS, ROWS * pages), 1) & 7
+    position_ref[...] = nn_dot(blocks, spread.astype(BF16)).astype(jnp.int32) * ROWS + inside
+    for e in range(PER_GROUP):
+        for kv in range(2):
+            loads[3 + 2 * e + kv].wait()
+
+            def place(j, carry):
+                block = table_ref[PER_GROUP * group + e, j]
+                at = ((block & 1) ^ core) * PAGE_TILES + kv * 4 + e * 2
+                page = held_ref[kv, e, j]
+                out_ref[block >> 1, at] = page[:, :LANES]
+                out_ref[block >> 1, at + 1] = page[:, LANES:]
+                return carry
+
+            lax.fori_loop(0, pages, place, 0, unroll=8)
+    for load in loads[7:]:
+        load.wait()
 
 
 def qkv_kernel(
@@ -123,7 +177,9 @@
     copy.wait()
 
 
-def attend_kernel(me_ref, lengths_ref, got_ref, table_ref, cache_ref, out_ref):
+def attend_kernel(me_ref, lengths_ref, got_ref, position_ref, cache_ref, out_ref, leaving_ref, sem):
+    leave = pltpu.make_async_copy(got_ref.at[:, PAGE_TILES : 2 * PAGE_TILES], leaving_ref, sem)
+    leave.start()
     me = me_ref[0]
     group = me >> 3
     slot = me & 7
@@ -140,7 +196,7 @@
     fix_head = HEADS + slot * 2 + (m & 1) + KV_HEADS * (m >> 1)
     chosen = jnp.where(kind == 0, q_head, jnp.where(kind == 1, k_head, jnp.where(kind == 2, v_head, fix_head)))
     pick = jnp.where(n == chosen * ROWS + rows_at + e, 1.0, 0.0).astype(BF16)
-    source = got_ref[:, 0].astype(F32).reshape(n_src, LANES).astype(BF16)
+    source = got_ref[:, BULK_TILES - 1].astype(F32).reshape(n_src, LANES).astype(BF16)
     picked = nn_dot(pick, source)
     q = picked[0:8]
     new_k = picked[8:16]
@@ -154,17 +210,8 @@
             keys = cache_ref[0, ee, :, a * LANES : a * LANES + LANES]
             part = nt_dot(q16, keys)
             scores = jnp.where(((row & 1) == ee) & ((row >> 2) == a), part, scores)
-    pages = 2 * CHIPS
-    table_row = iota((BATCH, pages), 0)
-    lines = []
-    for ee in range(PER_GROUP):
-        chosen_row = jnp.where(table_row == group * PER_GROUP + ee, table_ref[...], 0)
-        lines.append(jnp.sum(chosen_row, axis=0, keepdims=True))
-    blocks = jnp.where((row & 1) == 0, lines[0], lines[1]).astype(F32).astype(BF16)
-    spread = jnp.where(iota((pages, ROWS * pages), 1) >> 3 == iota((pages, ROWS * pages), 0), 1.0, 0.0)
-    position = nn_dot(blocks, spread.astype(BF16)).astype(jnp.int32) * ROWS + (iota((ROWS, ROWS * pages), 1) & 7)
     limit = jnp.where((row & 1) == 0, lengths_ref[group * PER_GROUP], lengths_ref[group * PER_GROUP + 1])
-    weights = jnp.where(position < limit, jnp.exp(capped(scores * scale)), 0.0)
+    weights = jnp.where(position_ref[...] < limit, jnp.exp(capped(scores * scale)), 0.0)
     own = jnp.exp(capped(jnp.sum(q * new_k, axis=-1, keepdims=True) * scale))
     denominator = jnp.sum(weights, axis=-1, keepdims=True) + own
     w16 = weights.astype(BF16)
@@ -177,6 +224,7 @@
     attended = numerator / denominator
     payload = jnp.concatenate([attended, picked[24:32]], axis=0).astype(BF16)
     out_ref[...] = jnp.broadcast_to(payload[None], (CHIPS, 2 * ROWS, LANES))
+    leave.wait()
 
 
 def mix_kernel(me_ref, own_ref, other_ref, weight_ref, out_ref):
@@ -383,14 +431,28 @@
     return lax.all_to_all(tiles, XY, 0, 0, tiled=True)
 
 
-def pages_call(me, table, cache):
+def pages_call(me, lengths, table, cache, weight, hidden, gains):
+    fixed = [pltpu.with_memory_space_constraint(x, pltpu.HBM) for x in (lengths, table, cache, weight, hidden, gains)]
     return call(
         pages_kernel,
-        (shaped((CHIPS, BULK_TILES, ROWS, LANES), BF16), shaped(cache.shape, BF16)),
-        [smem(), smem(), vmem()],
-        (vmem(), vmem()),
-        scratch_shapes=[pltpu.SemaphoreType.DMA],
-    )(me, table, cache)
+        (
+            pltpu.VMEM((CHIPS, BULK_TILES, ROWS, LANES), BF16),
+            pltpu.VMEM(cache.shape, BF16),
+            pltpu.VMEM(weight.shape, BF16),
+            pltpu.VMEM(hidden.shape, F32),
+            pltpu.VMEM(gains.shape, F32),
+            pltpu.VMEM((BATCH, HEAD_DIM // 2), F32),
+            pltpu.VMEM((ROWS, ROWS * 2 * CHIPS), jnp.int32),
+        ),
+        [smem()] + [hbm()] * 6,
+        (vmem(),) * 7,
+        scratch_shapes=[
+            pltpu.SMEM(lengths.shape, jnp.int32),
+            pltpu.SMEM(table.shape, jnp.int32),
+            pltpu.VMEM(table.shape, jnp.int32),
+            pltpu.SemaphoreType.DMA((10,)),
+        ],
+    )(me, *fixed)
 
 
 def qkv_call(me, hidden, gains, own, other, cosine, sine, buf):
@@ -404,22 +466,17 @@
     )(me, hidden, gains, own, other, cosine, sine, buf)
 
 
-def attend_call(me, lengths, got, table, cache):
-    return pl.pallas_call(
+def attend_call(me, lengths, got, position, cache):
+    return call(
         attend_kernel,
-        grid=(1,),
-        out_shape=shaped((CHIPS, 2 * ROWS, LANES), BF16),
-        in_specs=[
-            smem(),
-            smem(),
-            pl.BlockSpec((CHIPS, 1, ROWS, LANES), lambda i: (0, BULK_TILES - 1, 0, 0)),
-            vmem(),
-            vmem(),
-        ],
-        out_specs=vmem(),
-        name="attend",
-        compiler_params=pltpu.CompilerParams(vmem_limit_bytes=VMEM_LIMIT),
-    )(me, lengths, got, table, cache)
+        (
+            pltpu.VMEM((CHIPS, 2 * ROWS, LANES), BF16),
+            pltpu.VMEM((CHIPS, PAGE_TILES, ROWS, LANES), BF16),
+        ),
+        [smem(), smem()] + [vmem()] * 3,
+        (vmem(), vmem()),
+        scratch_shapes=[pltpu.SemaphoreType.DMA],
+    )(me, lengths, got, position, cache)
 
 
 def mix_call(me, own, other, weight):
@@ -458,29 +515,15 @@
 
 
 def decode_call(me, lengths, got, other, own_new, other_new):
-    return pl.pallas_call(
-        decode_kernel,
-        grid=(1,),
-        out_shape=shaped((2, BATCH, ROWS, KV_HEADS * HEAD_DIM), BF16),
-        in_specs=[
-            smem(),
-            smem(),
-            pl.BlockSpec((CHIPS, PAGE_TILES, ROWS, LANES), lambda i: (0, 0, 0, 0)),
-            vmem(),
-            vmem(),
-            vmem(),
-        ],
-        out_specs=vmem(),
-        name="decode",
-        compiler_params=pltpu.CompilerParams(vmem_limit_bytes=VMEM_LIMIT),
+    return call(
+        decode_kernel, pltpu.VMEM((2, BATCH, ROWS, KV_HEADS * HEAD_DIM), BF16), [smem(), smem()] + [vmem()] * 4, vmem()
     )(me, lengths, got, other, own_new, other_new)
 
 
-def rope_tables(lengths):
+def rope_tables(spread_length):
     half_dim = HEAD_DIM // 2
     exponent = jnp.arange(half_dim, dtype=F32) * (-2.0 / HEAD_DIM)
-    frequency = jnp.power(jnp.float32(10000.0), exponent)
-    angles = lengths.astype(F32)[:, None] * frequency
+    angles = spread_length * jnp.power(jnp.float32(10000.0), exponent)
     return jnp.cos(angles), jnp.sin(angles)
 
 
@@ -496,26 +539,29 @@
     norm_gains,
 ):
     me = jnp.full((1,), lax.axis_index(TP), jnp.int32)
-    cache = prefill_cache[0, 0]
     other_rows = core_swap(qkv_weight)
-    buf, held = pages_call(me, page_table, cache)
-    cosine, sine = rope_tables(lengths)
-    buf = qkv_call(me, hidden_in, norm_gains, qkv_weight, other_rows, cosine, sine, buf)
+    buf, held, own_rows, hidden, gains, spread_length, position = pages_call(
+        me, lengths, page_table, prefill_cache[0, 0], qkv_weight, hidden_in, norm_gains
+    )
+    cosine, sine = rope_tables(spread_length)
+    buf = qkv_call(me, hidden, gains, own_rows, other_rows, cosine, sine, buf)
     got = to_chips(buf)
-    payload = attend_call(me, lengths, got, page_table, held.reshape(2, PER_GROUP, -1, 2 * HEAD_DIM))
+    payload, leaving = attend_call(
+        me, lengths, got, position, held.reshape(2, PER_GROUP, -1, 2 * HEAD_DIM)
+    )
     own_att = to_chips(payload)
     other_att = core_swap(own_att)
-    leaving = got[:, PAGE_TILES : 2 * PAGE_TILES]
     other_pages = core_swap(leaving)
     payload = mix_call(me, own_att, other_att, out_weight)
     own_mix = to_chips(payload)
     other_mix = core_swap(own_mix)
-    keep, send, stream = ffn_call(me, own_mix, other_mix, hidden_in, norm_gains, gate_up_weight, down_weight)
-    chip = (keep.astype(F32) + core_swap(send).astype(F32)).astype(BF16)
+    keep, send, stream = ffn_call(me, own_mix, other_mix, hidden, gains, gate_up_weight, down_weight)
+    sent = core_swap(send)
+    chip = (keep.astype(F32) + sent.astype(F32)).astype(BF16)
     got_branch = to_chips(chip)
     portion, square = portion_call(me, got_branch)
     squares = to_chips(square)
-    result = finish_call(me, portion, stream, squares, core_swap(squares), norm_gains)
+    result = finish_call(me, portion, stream, squares, core_swap(squares), gains)
     decoded = decode_call(me, lengths, got, other_pages, own_att, other_att)
     return result, decoded[None, None]
 

time: 192 us -> 187 us (0.974)
  blocking collectives: 142 us -> 140 us
  local copies, waits for them, and re-layouts: 3.34 us -> 1.34 us
where the time goes in v2:
time: 187 us
  blocking collectives  140 us (75%)
  starting transfers between devices  30.4 us (16%)
  Pallas kernels  11 us (6%)
  waiting for transfers between devices  3.35 us (2%)
    all_to_all x5, blocking collectives, to_chips(): return lax.all_to_all(tiles, XY, 0, 0, tiled=True)  140 us
    ppermute x6, starting transfers between devices, core_swap(): return lax.ppermute(shard, 'tp_2', [(0, 1), (1, 0)])  30.4 us
  transfers between devices with their start and end apart: 6, of which 3 were waited for; matrix products, arithmetic and copies ran while one was open for 1% of the time, Pallas kernels for 3%

profile of v2, /device:TPU:513, one launch (start us, length us, event | category | flops | bytes accessed | tf_op | source)
XLA Modules:
  0.0 187.0 jit_solution(4772957570316407622)
XLA Ops:
  0.6 20.5 %collective-permute-start = (bf16[1,64,4608]{2,1,0:T(8,128)(2,1)}, bf16[1,64,4608]{2,1,0:T(8,128)(2,1)S(1)}, u32[]{:S(2)}, u32[]{:S(2)}) collective-permute-start(bf16[1,64,4608]{2,1,0:T(8,128)(2,1)} %weight_hbm.1), channel_id=1, source_target_pairs={{0,1},{1,0},{2,3},{3,2},{4,5},{5,4},{6,7},{7,6},{8,9},{9,8},{10,11... | collective-permute-start | bytes 1769480 | tf_op jit(solution)/shard_map/ppermute | solution.py:427
  21.2 3.6 %shard_map.104 = (bf16[64,17,8,128]{3,2,1,0:T(8,128)(2,1)S(1)}, bf16[2,2,128,8,256]{4,3,2,1,0:T(8,128)(2,1)S(1)}, bf16[1,64,4608]{2,1,0:T(8,128)(2,1)S(1)}, f32[...) custom-call(s32[1]{0:T(128)} %bitcast.me_ref, s32[32]{0:T(128)} %lengths_ref.3, ...), custom_call_target="tpu_custom_call" | custom-call | tf_op jit(solution)/shard_map/pallas_call | solution.py:436
  24.8 0.1 multiply_sine_fusion
  24.9 0.0 collective-permute-done.other_ref
  24.9 0.7 shard_map.105
  25.6 0.0 copy-start.3
  25.6 65.7 %all_to_all.25.got_ref = bf16[64,17,8,128]{3,2,1,0:T(8,128)(2,1)S(1)} all-to-all(bf16[64,17,8,128]{3,2,1,0:T(8,128)(2,1)S(1)} %shard_map.105), channel_id=1, replica_groups=mesh['grp'=2,'tp_0'=8,'tp_1'=8,'tp_2'=2] {'tp_0','tp_1'}, dimensions={0} | all-to-all | bytes 4456448 | tf_op jit(solution)/shard_map/all_to_all | solution.py:431
  91.3 0.0 copy-done.3
  91.3 1.4 shard_map.106
  92.8 0.0 copy-start.1
  92.8 22.5 %all_to_all.26.own_ref.own_new_ref = bf16[64,16,128]{2,1,0:T(8,128)(2,1)S(1)} all-to-all(bf16[64,16,128]{2,1,0:T(8,128)(2,1)S(1)} %get-tuple-element.23), channel_id=1, replica_groups=mesh['grp'=2,'tp_0'=8,'tp_1'=8,'tp_2'=2] {'tp_0','tp_1'}, dimensions={0} | all-to-all | bytes 524288 | tf_op jit(solution)/shard_map/all_to_all | solution.py:431
  115.3 3.5 %collective-permute-start.1 = (bf16[64,16,128]{2,1,0:T(8,128)(2,1)S(1)}, bf16[64,16,128]{2,1,0:T(8,128)(2,1)S(1)}, u32[]{:S(2)}, u32[]{:S(2)}) collective-permute-start(bf16[64,16,128]{2,1,0:T(8,128)(2,1)S(1)} %all_to_all.26.own_ref.own_new_ref), channel_id=1, source_target_pairs={{0,1},{1,0},{2,3},{3,2},{4,5},{5,4},{6,7},{7,6},{8,9},{9,8},{10,11... | collective-permute-start | bytes 786440 | tf_op jit(solution)/shard_map/ppermute | solution.py:427
  118.8 1.2 collective-permute-done.1.other_ref.other_new_ref
  119.9 1.0 shard_map.107
  121.0 17.5 %all_to_all.27.own_ref = bf16[64,16,128]{2,1,0:T(8,128)(2,1)S(1)} all-to-all(bf16[64,16,128]{2,1,0:T(8,128)(2,1)S(1)} %shard_map.107), channel_id=1, replica_groups=mesh['grp'=2,'tp_0'=8,'tp_1'=8,'tp_2'=2] {'tp_0','tp_1'}, dimensions={0} | all-to-all | bytes 524288 | tf_op jit(solution)/shard_map/all_to_all | solution.py:431
  138.5 2.8 %collective-permute-start.2 = (bf16[64,16,128]{2,1,0:T(8,128)(2,1)S(1)}, bf16[64,16,128]{2,1,0:T(8,128)(2,1)S(1)}, u32[]{:S(2)}, u32[]{:S(2)}) collective-permute-start(bf16[64,16,128]{2,1,0:T(8,128)(2,1)S(1)} %all_to_all.27.own_ref), channel_id=1, source_target_pairs={{0,1},{1,0},{2,3},{3,2},{4,5},{5,4},{6,7},{7,6},{8,9},{9,8},{10,11... | collective-permute-start | bytes 786440 | tf_op jit(solution)/shard_map/ppermute | solution.py:427
  141.3 1.2 collective-permute-done.2.other_ref
  142.5 0.0 copy-done.1
  142.5 2.0 %shard_map.108 = (bf16[64,16,128]{2,1,0:T(8,128)(2,1)S(1)}, bf16[64,16,128]{2,1,0:T(8,128)(2,1)S(1)}, f32[32,128]{1,0:T(8,128)S(1)}) custom-call(s32[1]{0:T(128)} %bitcast.me_ref, bf16[64,16,128]{2,1,0:T(8,128)(2,1)S(1)} %all_to_all.27.own_ref, bf16[64,16,128]{2,1,0:T(8,128)(2,1)S(1)} %collective-permute-done.2.other_ref, ...), custom_call_target="tpu_custom_call" | custom-call | tf_op jit(solution)/shard_map/pallas_call | solution.py:488
  144.5 0.5 collective-permute-start.3
  145.0 0.1 collective-permute-start.5
  145.1 1.0 collective-permute-done.3
  146.1 0.1 add_convert_fusion
  146.2 17.7 %all_to_all.28.got_ref = bf16[64,16,128]{2,1,0:T(8,128)(2,1)S(1)} all-to-all(bf16[64,16,128]{2,1,0:T(8,128)(2,1)S(1)} %add_convert_fusion), channel_id=1, replica_groups=mesh['grp'=2,'tp_0'=8,'tp_1'=8,'tp_2'=2] {'tp_0','tp_1'}, dimensions={0} | all-to-all | bytes 524288 | tf_op jit(solution)/shard_map/all_to_all | solution.py:431
  163.9 0.3 shard_map.109
  164.2 16.6 %all_to_all.29.own_ref = f32[64,1,128]{2,1,0:T(1,128)S(1)} all-to-all(f32[64,1,128]{2,1,0:T(1,128)S(1)} %get-tuple-element.28), channel_id=1, replica_groups=mesh['grp'=2,'tp_0'=8,'tp_1'=8,'tp_2'=2] {'tp_0','tp_1'}, dimensions={0} | all-to-all | bytes 65536 | tf_op jit(solution)/shard_map/all_to_all | solution.py:431
  180.9 2.9 %collective-permute-start.4 = (f32[64,1,128]{2,1,0:T(1,128)S(1)}, f32[64,1,128]{2,1,0:T(1,128)S(1)}, u32[]{:S(2)}, u32[]{:S(2)}) collective-permute-start(f32[64,1,128]{2,1,0:T(1,128)S(1)} %all_to_all.29.own_ref), channel_id=1, source_target_pairs={{0,1},{1,0},{2,3},{3,2},{4,5},{5,4},{6,7},{7,6},{8,9},{9,8},{10,11... | collective-permute-start | bytes 98312 | tf_op jit(solution)/shard_map/ppermute | solution.py:427
  183.7 0.0 collective-permute-done.5.other_ref
  183.7 1.2 shard_map.111
  184.9 1.3 copy.13
  186.2 0.0 collective-permute-done.4.other_ref
  186.2 0.8 shard_map.110
  (5 shorter events, 0.0 us)
Async XLA Ops:
  0.6 24.3 %collective-permute-start = (bf16[1,64,4608]{2,1,0:T(8,128)(2,1)}, bf16[1,64,4608]{2,1,0:T(8,128)(2,1)S(1)}, u32[]{:S(2)}, u32[]{:S(2)}) collective-permute-start(bf16[1,64,4608]{2,1,0:T(8,128)(2,1)} %weight_hbm.1), channel_id=1, source_target_pairs={{0,1},{1,0},{2,3},{3,2},{4,5},{5,4},{6,7},{7,6},{8,9},{9,8},{10,11... | collective-permute-start | bytes 1769480 | tf_op jit(solution)/shard_map/ppermute | solution.py:427
  25.6 65.7 %copy-start.3 = (s32[32]{0:T(128)S(1)}, s32[32]{0:T(128)}, u32[]{:S(2)}) copy-start(s32[32]{0:T(128)} %lengths_ref.3) | copy-start | bytes 388
  91.3 28.6 %copy-start.2 = (bf16[1,36,4096]{2,1,0:T(8,128)(2,1)S(1)}, bf16[1,36,4096]{2,1,0:T(8,128)(2,1)}, u32[]{:S(2)}) copy-start(bf16[1,36,4096]{2,1,0:T(8,128)(2,1)} %weight_ref.1) | copy-start | bytes 884740
  91.3 51.2 %copy-start = (bf16[1,2,144,4608]{3,2,1,0:T(8,128)(2,1)S(1)}, bf16[1,2,144,4608]{3,2,1,0:T(8,128)(2,1)}, u32[]{:S(2)}) copy-start(bf16[1,2,144,4608]{3,2,1,0:T(8,128)(2,1)} %gate_up_ref.1) | copy-start | bytes 7962628
  92.8 49.7 %copy-start.1 = (bf16[1,144,4608]{2,1,0:T(8,128)(2,1)S(1)}, bf16[1,144,4608]{2,1,0:T(8,128)(2,1)}, u32[]{:S(2)}) copy-start(bf16[1,144,4608]{2,1,0:T(8,128)(2,1)} %down_ref.1) | copy-start | bytes 3981316
  115.3 4.6 %collective-permute-start.1 = (bf16[64,16,128]{2,1,0:T(8,128)(2,1)S(1)}, bf16[64,16,128]{2,1,0:T(8,128)(2,1)S(1)}, u32[]{:S(2)}, u32[]{:S(2)}) collective-permute-start(bf16[64,16,128]{2,1,0:T(8,128)(2,1)S(1)} %all_to_all.26.own_ref.own_new_ref), channel_id=1, source_target_pairs={{0,1},{1,0},{2,3},{3,2},{4,5},{5,4},{6,7},{7,6},{8,9},{9,8},{10,11... | collective-permute-start | bytes 786440 | tf_op jit(solution)/shard_map/ppermute | solution.py:427
  138.5 4.0 %collective-permute-start.2 = (bf16[64,16,128]{2,1,0:T(8,128)(2,1)S(1)}, bf16[64,16,128]{2,1,0:T(8,128)(2,1)S(1)}, u32[]{:S(2)}, u32[]{:S(2)}) collective-permute-start(bf16[64,16,128]{2,1,0:T(8,128)(2,1)S(1)} %all_to_all.27.own_ref), channel_id=1, source_target_pairs={{0,1},{1,0},{2,3},{3,2},{4,5},{5,4},{6,7},{7,6},{8,9},{9,8},{10,11... | collective-permute-start | bytes 786440 | tf_op jit(solution)/shard_map/ppermute | solution.py:427
  144.5 1.7 collective-permute-start.3
  145.0 38.8 %collective-permute-start.5 = (bf16[64,8,8,128]{3,2,1,0:T(8,128)(2,1)S(1)}, bf16[64,8,8,128]{3,2,1,0:T(8,128)(2,1)S(1)}, u32[]{:S(2)}, u32[]{:S(2)}) collective-permute-start(bf16[64,8,8,128]{3,2,1,0:T(8,128)(2,1)S(1)} %get-tuple-element.29), channel_id=1, source_target_pairs={{0,1},{1,0},{2,3},{3,2},{4,5},{5,4},{6,7},{7,6},{8,9},{9,8},{10,11... | collective-permute-start | bytes 3145736 | tf_op jit(solution)/shard_map/ppermute | solution.py:427
  180.9 5.4 %collective-permute-start.4 = (f32[64,1,128]{2,1,0:T(1,128)S(1)}, f32[64,1,128]{2,1,0:T(1,128)S(1)}, u32[]{:S(2)}, u32[]{:S(2)}) collective-permute-start(f32[64,1,128]{2,1,0:T(1,128)S(1)} %all_to_all.29.own_ref), channel_id=1, source_target_pairs={{0,1},{1,0},{2,3},{3,2},{4,5},{5,4},{6,7},{7,6},{8,9},{9,8},{10,11... | collective-permute-start | bytes 98312 | tf_op jit(solution)/shard_map/ppermute | solution.py:427

commit v3 on v2

--- a/solution.py
+++ b/solution.py
@@ -71,6 +71,10 @@
 
 def iota(shape, dim):
     return lax.broadcasted_iota(jnp.int32, shape, dim)
+
+
+def bulk_place(chip):
+    return ((chip & 7) << 3) | (chip >> 3)
 
 
 def capped(raw_scores):
@@ -140,8 +144,9 @@
                 block = table_ref[PER_GROUP * group + e, j]
                 at = ((block & 1) ^ core) * PAGE_TILES + kv * 4 + e * 2
                 page = held_ref[kv, e, j]
-                out_ref[block >> 1, at] = page[:, :LANES]
-                out_ref[block >> 1, at + 1] = page[:, LANES:]
+                chip = bulk_place(block >> 1)
+                out_ref[chip, at] = page[:, :LANES]
+                out_ref[chip, at + 1] = page[:, LANES:]
                 return carry
 
             lax.fori_loop(0, pages, place, 0, unroll=8)
@@ -168,10 +173,9 @@
     new_front = jnp.where(turned, front * cosine - back * sine, front)
     new_back = jnp.where(turned, back * cosine + front * sine, back)
     whole = jnp.concatenate([new_front, new_back], axis=1)
-    for u in range(BATCH // ROWS):
-        rows = whole[ROWS * u : ROWS * u + ROWS, :].astype(BF16)
-        per = CHIPS * ROWS // BATCH
-        tile_ref[per * u : per * u + per] = jnp.broadcast_to(rows[None], (per, ROWS, LANES))
+    rows = [whole[ROWS * u : ROWS * u + ROWS, :].astype(BF16) for u in range(BATCH // ROWS)]
+    for chip in range(CHIPS):
+        tile_ref[bulk_place(chip)] = rows[chip * BATCH // (CHIPS * ROWS)]
     copy = pltpu.make_async_copy(tile_ref, out_ref.at[:, BULK_TILES - 1], sem)
     copy.start()
     copy.wait()
@@ -195,7 +199,7 @@
     v_head = k_head + KV_HEADS
     fix_head = HEADS + slot * 2 + (m & 1) + KV_HEADS * (m >> 1)
     chosen = jnp.where(kind == 0, q_head, jnp.where(kind == 1, k_head, jnp.where(kind == 2, v_head, fix_head)))
-    pick = jnp.where(n == chosen * ROWS + rows_at + e, 1.0, 0.0).astype(BF16)
+    pick = jnp.where(n == bulk_place(chosen) * ROWS + rows_at + e, 1.0, 0.0).astype(BF16)
     source = got_ref[:, BULK_TILES - 1].astype(F32).reshape(n_src, LANES).astype(BF16)
     picked = nn_dot(pick, source)
     q = picked[0:8]
@@ -374,7 +378,7 @@
     def place(first_core):
         def body(g, carry):
             for y in range(QUARTERS):
-                s = g * QUARTERS + y
+                s = bulk_place(g * QUARTERS + y)
                 for side, ref in ((0, got_ref), (1, other_ref)):
                     slot = 2 * y + (first_core if side == 0 else 1 - first_core)
                     for kv in range(2):
@@ -545,7 +549,7 @@
     )
     cosine, sine = rope_tables(spread_length)
     buf = qkv_call(me, hidden, gains, own_rows, other_rows, cosine, sine, buf)
-    got = to_chips(buf)
+    got = lax.all_to_all(buf, XY[::-1], 0, 0, tiled=True)
     payload, leaving = attend_call(
         me, lengths, got, position, held.reshape(2, PER_GROUP, -1, 2 * HEAD_DIM)
     )

time: 187 us -> 182 us (0.973)
  blocking collectives: 140 us -> 134 us
    all_to_all x5 -> x4, blocking collectives: 140 us -> 73 us  [to_chips(): return lax.all_to_all(tiles, XY, 0, 0, tiled=True)]
    all_to_all x0 -> x1, blocking collectives: none -> 61.1 us  [on_device(): got = lax.all_to_all(buf, XY[::-1], 0, 0, tiled=True)]
where the time goes in v3:
time: 182 us; the launch traced here: 181 us
  blocking collectives  134 us (74%)
  starting transfers between devices  30.1 us (17%)
  Pallas kernels  11.6 us (6%)
  waiting for transfers between devices  3.35 us (2%)
    all_to_all x4, blocking collectives, to_chips(): return lax.all_to_all(tiles, XY, 0, 0, tiled=True)  73 us
    all_to_all x1, blocking collectives, on_device(): got = lax.all_to_all(buf, XY[::-1], 0, 0, tiled=True)  61.1 us
    ppermute x6, starting transfers between devices, core_swap(): return lax.ppermute(shard, 'tp_2', [(0, 1), (1, 0)])  30.1 us
    pallas_call x1, Pallas kernels, pages_call(): call(pages_kernel, (pltpu.VMEM((CHIPS, BULK_TILES, ROWS, LANES), BF16), p...  4.18 us
  transfers between devices with their start and end apart: 6, of which 3 were waited for; matrix products, arithmetic and copies ran while one was open for 1% of the time, Pallas kernels for 3%

profile of v3, /device:TPU:513, one launch (start us, length us, event | category | flops | bytes accessed | tf_op | source)
XLA Modules:
  0.0 181.4 jit_solution(5499696519553141591)
XLA Ops:
  0.6 20.5 %collective-permute-start = (bf16[1,64,4608]{2,1,0:T(8,128)(2,1)}, bf16[1,64,4608]{2,1,0:T(8,128)(2,1)S(1)}, u32[]{:S(2)}, u32[]{:S(2)}) collective-permute-start(bf16[1,64,4608]{2,1,0:T(8,128)(2,1)} %weight_hbm.1), channel_id=1, source_target_pairs={{0,1},{1,0},{2,3},{3,2},{4,5},{5,4},{6,7},{7,6},{8,9},{9,8},{10,11... | collective-permute-start | bytes 1769480 | tf_op jit(solution)/shard_map/ppermute | solution.py:431
  21.2 4.2 %shard_map.104 = (bf16[64,17,8,128]{3,2,1,0:T(8,128)(2,1)S(1)}, bf16[2,2,128,8,256]{4,3,2,1,0:T(8,128)(2,1)S(1)}, bf16[1,64,4608]{2,1,0:T(8,128)(2,1)S(1)}, f32[...) custom-call(s32[1]{0:T(128)} %bitcast.me_ref, s32[32]{0:T(128)} %lengths_ref.3, ...), custom_call_target="tpu_custom_call" | custom-call | tf_op jit(solution)/shard_map/pallas_call | solution.py:440
  25.4 0.1 multiply_sine_fusion
  25.4 0.0 collective-permute-done.other_ref
  25.5 0.7 shard_map.105
  26.2 0.0 copy-start.3
  26.2 61.1 %all_to_all.25.got_ref = bf16[64,17,8,128]{3,2,1,0:T(8,128)(2,1)S(1)} all-to-all(bf16[64,17,8,128]{3,2,1,0:T(8,128)(2,1)S(1)} %shard_map.105), channel_id=1, replica_groups=mesh['grp'=2,'tp_0'=8,'tp_1'=8,'tp_2'=2] {'tp_1','tp_0'}, dimensions={0} | all-to-all | bytes 4456448 | tf_op jit(solution)/shard_map/all_to_all | solution.py:552
  87.3 0.0 copy-done.3
  87.3 1.4 shard_map.106
  88.7 0.0 copy-start.1
  88.8 21.1 %all_to_all.26.own_ref.own_new_ref = bf16[64,16,128]{2,1,0:T(8,128)(2,1)S(1)} all-to-all(bf16[64,16,128]{2,1,0:T(8,128)(2,1)S(1)} %get-tuple-element.23), channel_id=1, replica_groups=mesh['grp'=2,'tp_0'=8,'tp_1'=8,'tp_2'=2] {'tp_0','tp_1'}, dimensions={0} | all-to-all | bytes 524288 | tf_op jit(solution)/shard_map/all_to_all | solution.py:435
  109.9 3.2 %collective-permute-start.1 = (bf16[64,16,128]{2,1,0:T(8,128)(2,1)S(1)}, bf16[64,16,128]{2,1,0:T(8,128)(2,1)S(1)}, u32[]{:S(2)}, u32[]{:S(2)}) collective-permute-start(bf16[64,16,128]{2,1,0:T(8,128)(2,1)S(1)} %all_to_all.26.own_ref.own_new_ref), channel_id=1, source_target_pairs={{0,1},{1,0},{2,3},{3,2},{4,5},{5,4},{6,7},{7,6},{8,9},{9,8},{10,11... | collective-permute-start | bytes 786440 | tf_op jit(solution)/shard_map/ppermute | solution.py:431
  113.1 1.2 collective-permute-done.1.other_ref.other_new_ref
  114.3 0.0 copy-done.2
  114.3 1.0 shard_map.107
  115.3 17.5 %all_to_all.27.own_ref = bf16[64,16,128]{2,1,0:T(8,128)(2,1)S(1)} all-to-all(bf16[64,16,128]{2,1,0:T(8,128)(2,1)S(1)} %shard_map.107), channel_id=1, replica_groups=mesh['grp'=2,'tp_0'=8,'tp_1'=8,'tp_2'=2] {'tp_0','tp_1'}, dimensions={0} | all-to-all | bytes 524288 | tf_op jit(solution)/shard_map/all_to_all | solution.py:435
  132.8 2.8 %collective-permute-start.2 = (bf16[64,16,128]{2,1,0:T(8,128)(2,1)S(1)}, bf16[64,16,128]{2,1,0:T(8,128)(2,1)S(1)}, u32[]{:S(2)}, u32[]{:S(2)}) collective-permute-start(bf16[64,16,128]{2,1,0:T(8,128)(2,1)S(1)} %all_to_all.27.own_ref), channel_id=1, source_target_pairs={{0,1},{1,0},{2,3},{3,2},{4,5},{5,4},{6,7},{7,6},{8,9},{9,8},{10,11... | collective-permute-start | bytes 786440 | tf_op jit(solution)/shard_map/ppermute | solution.py:431
  135.7 1.2 collective-permute-done.2.other_ref
  136.8 2.0 %shard_map.108 = (bf16[64,16,128]{2,1,0:T(8,128)(2,1)S(1)}, bf16[64,16,128]{2,1,0:T(8,128)(2,1)S(1)}, f32[32,128]{1,0:T(8,128)S(1)}) custom-call(s32[1]{0:T(128)} %bitcast.me_ref, bf16[64,16,128]{2,1,0:T(8,128)(2,1)S(1)} %all_to_all.27.own_ref, bf16[64,16,128]{2,1,0:T(8,128)(2,1)S(1)} %collective-permute-done.2.other_ref, ...), custom_call_target="tpu_custom_call" | custom-call | tf_op jit(solution)/shard_map/pallas_call | solution.py:492
  138.8 0.5 collective-permute-start.3
  139.3 0.1 collective-permute-start.5
  139.5 1.0 collective-permute-done.3
  140.5 0.1 add_convert_fusion
  140.6 17.7 %all_to_all.28.got_ref = bf16[64,16,128]{2,1,0:T(8,128)(2,1)S(1)} all-to-all(bf16[64,16,128]{2,1,0:T(8,128)(2,1)S(1)} %add_convert_fusion), channel_id=1, replica_groups=mesh['grp'=2,'tp_0'=8,'tp_1'=8,'tp_2'=2] {'tp_0','tp_1'}, dimensions={0} | all-to-all | bytes 524288 | tf_op jit(solution)/shard_map/all_to_all | solution.py:435
  158.3 0.3 shard_map.109
  158.6 16.6 %all_to_all.29.own_ref = f32[64,1,128]{2,1,0:T(1,128)S(1)} all-to-all(f32[64,1,128]{2,1,0:T(1,128)S(1)} %get-tuple-element.28), channel_id=1, replica_groups=mesh['grp'=2,'tp_0'=8,'tp_1'=8,'tp_2'=2] {'tp_0','tp_1'}, dimensions={0} | all-to-all | bytes 65536 | tf_op jit(solution)/shard_map/all_to_all | solution.py:435
  175.2 2.9 %collective-permute-start.4 = (f32[64,1,128]{2,1,0:T(1,128)S(1)}, f32[64,1,128]{2,1,0:T(1,128)S(1)}, u32[]{:S(2)}, u32[]{:S(2)}) collective-permute-start(f32[64,1,128]{2,1,0:T(1,128)S(1)} %all_to_all.29.own_ref), channel_id=1, source_target_pairs={{0,1},{1,0},{2,3},{3,2},{4,5},{5,4},{6,7},{7,6},{8,9},{9,8},{10,11... | collective-permute-start | bytes 98312 | tf_op jit(solution)/shard_map/ppermute | solution.py:431
  178.1 0.0 collective-permute-done.5.other_ref
  178.1 1.2 shard_map.111
  179.3 1.3 copy.13
  180.7 0.0 collective-permute-done.4.other_ref
  180.7 0.8 shard_map.110
  (5 shorter events, 0.0 us)
Async XLA Ops:
  0.6 24.8 %collective-permute-start = (bf16[1,64,4608]{2,1,0:T(8,128)(2,1)}, bf16[1,64,4608]{2,1,0:T(8,128)(2,1)S(1)}, u32[]{:S(2)}, u32[]{:S(2)}) collective-permute-start(bf16[1,64,4608]{2,1,0:T(8,128)(2,1)} %weight_hbm.1), channel_id=1, source_target_pairs={{0,1},{1,0},{2,3},{3,2},{4,5},{5,4},{6,7},{7,6},{8,9},{9,8},{10,11... | collective-permute-start | bytes 1769480 | tf_op jit(solution)/shard_map/ppermute | solution.py:431
  26.2 61.1 %copy-start.3 = (s32[32]{0:T(128)S(1)}, s32[32]{0:T(128)}, u32[]{:S(2)}) copy-start(s32[32]{0:T(128)} %lengths_ref.3) | copy-start | bytes 388
  87.3 27.0 %copy-start.2 = (bf16[1,36,4096]{2,1,0:T(8,128)(2,1)S(1)}, bf16[1,36,4096]{2,1,0:T(8,128)(2,1)}, u32[]{:S(2)}) copy-start(bf16[1,36,4096]{2,1,0:T(8,128)(2,1)} %weight_ref.1) | copy-start | bytes 884740
  87.3 49.6 %copy-start = (bf16[1,2,144,4608]{3,2,1,0:T(8,128)(2,1)S(1)}, bf16[1,2,144,4608]{3,2,1,0:T(8,128)(2,1)}, u32[]{:S(2)}) copy-start(bf16[1,2,144,4608]{3,2,1,0:T(8,128)(2,1)} %gate_up_ref.1) | copy-start | bytes 7962628
  88.7 48.1 %copy-start.1 = (bf16[1,144,4608]{2,1,0:T(8,128)(2,1)S(1)}, bf16[1,144,4608]{2,1,0:T(8,128)(2,1)}, u32[]{:S(2)}) copy-start(bf16[1,144,4608]{2,1,0:T(8,128)(2,1)} %down_ref.1) | copy-start | bytes 3981316
  109.9 4.4 %collective-permute-start.1 = (bf16[64,16,128]{2,1,0:T(8,128)(2,1)S(1)}, bf16[64,16,128]{2,1,0:T(8,128)(2,1)S(1)}, u32[]{:S(2)}, u32[]{:S(2)}) collective-permute-start(bf16[64,16,128]{2,1,0:T(8,128)(2,1)S(1)} %all_to_all.26.own_ref.own_new_ref), channel_id=1, source_target_pairs={{0,1},{1,0},{2,3},{3,2},{4,5},{5,4},{6,7},{7,6},{8,9},{9,8},{10,11... | collective-permute-start | bytes 786440 | tf_op jit(solution)/shard_map/ppermute | solution.py:431
  132.8 4.0 %collective-permute-start.2 = (bf16[64,16,128]{2,1,0:T(8,128)(2,1)S(1)}, bf16[64,16,128]{2,1,0:T(8,128)(2,1)S(1)}, u32[]{:S(2)}, u32[]{:S(2)}) collective-permute-start(bf16[64,16,128]{2,1,0:T(8,128)(2,1)S(1)} %all_to_all.27.own_ref), channel_id=1, source_target_pairs={{0,1},{1,0},{2,3},{3,2},{4,5},{5,4},{6,7},{7,6},{8,9},{9,8},{10,11... | collective-permute-start | bytes 786440 | tf_op jit(solution)/shard_map/ppermute | solution.py:431
  138.8 1.7 collective-permute-start.3
  139.3 38.8 %collective-permute-start.5 = (bf16[64,8,8,128]{3,2,1,0:T(8,128)(2,1)S(1)}, bf16[64,8,8,128]{3,2,1,0:T(8,128)(2,1)S(1)}, u32[]{:S(2)}, u32[]{:S(2)}) collective-permute-start(bf16[64,8,8,128]{3,2,1,0:T(8,128)(2,1)S(1)} %get-tuple-element.29), channel_id=1, source_target_pairs={{0,1},{1,0},{2,3},{3,2},{4,5},{5,4},{6,7},{7,6},{8,9},{9,8},{10,11... | collective-permute-start | bytes 3145736 | tf_op jit(solution)/shard_map/ppermute | solution.py:431
  175.2 5.4 %collective-permute-start.4 = (f32[64,1,128]{2,1,0:T(1,128)S(1)}, f32[64,1,128]{2,1,0:T(1,128)S(1)}, u32[]{:S(2)}, u32[]{:S(2)}) collective-permute-start(f32[64,1,128]{2,1,0:T(1,128)S(1)} %all_to_all.29.own_ref), channel_id=1, source_target_pairs={{0,1},{1,0},{2,3},{3,2},{4,5},{5,4},{6,7},{7,6},{8,9},{9,8},{10,11... | collective-permute-start | bytes 98312 | tf_op jit(solution)/shard_map/ppermute | solution.py:431

commit v4 on v3

--- a/solution.py
+++ b/solution.py
@@ -108,10 +108,11 @@
         (lengths_hbm, lengths_ref),
         (table_hbm, rows_ref),
         (table_hbm, table_ref),
-        (cache_hbm.at[0, 0], held_ref.at[0, 0]),
-        (cache_hbm.at[1, 0], held_ref.at[1, 0]),
-        (cache_hbm.at[0, 1], held_ref.at[0, 1]),
-        (cache_hbm.at[1, 1], held_ref.at[1, 1]),
+        *[
+            (cache_hbm.at[:, e, pl.ds(CHIPS * half, CHIPS)], held_ref.at[:, e, pl.ds(CHIPS * half, CHIPS)])
+            for e in range(PER_GROUP)
+            for half in range(2)
+        ],
         (hidden_hbm, hidden_ref),
         (weight_hbm, weight_ref),
         (gain_hbm, gain_ref),
@@ -137,19 +138,20 @@
     inside = iota((ROWS, ROWS * pages), 1) & 7
     position_ref[...] = nn_dot(blocks, spread.astype(BF16)).astype(jnp.int32) * ROWS + inside
     for e in range(PER_GROUP):
-        for kv in range(2):
-            loads[3 + 2 * e + kv].wait()
+        for half in range(2):
+            loads[3 + 2 * e + half].wait()
 
             def place(j, carry):
                 block = table_ref[PER_GROUP * group + e, j]
-                at = ((block & 1) ^ core) * PAGE_TILES + kv * 4 + e * 2
-                page = held_ref[kv, e, j]
                 chip = bulk_place(block >> 1)
-                out_ref[chip, at] = page[:, :LANES]
-                out_ref[chip, at + 1] = page[:, LANES:]
+                at = ((block & 1) ^ core) * PAGE_TILES + e * 2
+                for kv in range(2):
+                    page = held_ref[kv, e, j]
+                    out_ref[chip, at + kv * 4] = page[:, :LANES]
+                    out_ref[chip, at + kv * 4 + 1] = page[:, LANES:]
                 return carry
 
-            lax.fori_loop(0, pages, place, 0, unroll=8)
+            lax.fori_loop(CHIPS * half, CHIPS * half + CHIPS, place, 0, unroll=8)
     for load in loads[7:]:
         load.wait()
 
@@ -182,7 +184,7 @@
 
 
 def attend_kernel(me_ref, lengths_ref, got_ref, position_ref, cache_ref, out_ref, leaving_ref, sem):
-    leave = pltpu.make_async_copy(got_ref.at[:, PAGE_TILES : 2 * PAGE_TILES], leaving_ref, sem)
+    leave = pltpu.make_async_copy(got_ref.at[:, pl.ds(PAGE_TILES, PAGE_TILES // 2)], leaving_ref, sem)
     leave.start()
     me = me_ref[0]
     group = me >> 3
@@ -231,7 +233,11 @@
     leave.wait()
 
 
-def mix_kernel(me_ref, own_ref, other_ref, weight_ref, out_ref):
+def mix_kernel(me_ref, own_ref, other_ref, weight_ref, got_ref, out_ref, leaving_ref, sem):
+    leave = pltpu.make_async_copy(
+        got_ref.at[:, pl.ds(PAGE_TILES + PAGE_TILES // 2, PAGE_TILES // 2)], leaving_ref, sem
+    )
+    leave.start()
     me = me_ref[0]
     first = (me & 1) == 0
     n_src = CHIPS * ROWS
@@ -258,6 +264,7 @@
     packed = jnp.concatenate([values[:HALF], gap, values[HALF:], gap], axis=1)
     turned = pltpu.roll(packed, (me * SHARE) % LANES, 1).astype(BF16)
     out_ref[...] = jnp.broadcast_to(turned[None], (CHIPS, HALF, LANES))
+    leave.wait()
 
 
 def window(low_ref, high_ref, j):
@@ -371,7 +378,9 @@
     out_ref[...] = done[:, :SHARE]
 
 
-def decode_kernel(me_ref, lengths_ref, got_ref, other_ref, own_new_ref, other_new_ref, out_ref):
+def decode_kernel(
+    me_ref, lengths_ref, got_ref, keys_ref, values_ref, own_new_ref, other_new_ref, out_ref
+):
     me = me_ref[0]
     core = me & 1
 
@@ -379,13 +388,17 @@
         def body(g, carry):
             for y in range(QUARTERS):
                 s = bulk_place(g * QUARTERS + y)
-                for side, ref in ((0, got_ref), (1, other_ref)):
+                for side in range(2):
                     slot = 2 * y + (first_core if side == 0 else 1 - first_core)
                     for kv in range(2):
                         for e in range(PER_GROUP):
                             for h in range(2):
                                 cols = slice((2 * slot + h) * LANES, (2 * slot + h) * LANES + LANES)
-                                out_ref[kv, g * PER_GROUP + e, :, cols] = ref[s, kv * 4 + e * 2 + h]
+                                if side == 0:
+                                    tile = got_ref[s, kv * 4 + e * 2 + h]
+                                else:
+                                    tile = (keys_ref, values_ref)[kv][s, e * 2 + h]
+                                out_ref[kv, g * PER_GROUP + e, :, cols] = tile
             return carry
 
         lax.fori_loop(0, GROUPS, body, 0)
@@ -475,7 +488,7 @@
         attend_kernel,
         (
             pltpu.VMEM((CHIPS, 2 * ROWS, LANES), BF16),
-            pltpu.VMEM((CHIPS, PAGE_TILES, ROWS, LANES), BF16),
+            pltpu.VMEM((CHIPS, PAGE_TILES // 2, ROWS, LANES), BF16),
         ),
         [smem(), smem()] + [vmem()] * 3,
         (vmem(), vmem()),
@@ -483,8 +496,17 @@
     )(me, lengths, got, position, cache)
 
 
-def mix_call(me, own, other, weight):
-    return call(mix_kernel, shaped((CHIPS, HALF, LANES), BF16), [smem()] + [vmem()] * 3, vmem())(me, own, other, weight)
+def mix_call(me, own, other, weight, got):
+    return call(
+        mix_kernel,
+        (
+            pltpu.VMEM((CHIPS, HALF, LANES), BF16),
+            pltpu.VMEM((CHIPS, PAGE_TILES // 2, ROWS, LANES), BF16),
+        ),
+        [smem()] + [vmem()] * 4,
+        (vmem(), vmem()),
+        scratch_shapes=[pltpu.SemaphoreType.DMA],
+    )(me, own, other, weight, got)
 
 
 def ffn_call(me, own, other, hidden, gains, gate_up, down):
@@ -518,10 +540,10 @@
     )
 
 
-def decode_call(me, lengths, got, other, own_new, other_new):
+def decode_call(me, lengths, got, other_keys, other_values, own_new, other_new):
     return call(
-        decode_kernel, pltpu.VMEM((2, BATCH, ROWS, KV_HEADS * HEAD_DIM), BF16), [smem(), smem()] + [vmem()] * 4, vmem()
-    )(me, lengths, got, other, own_new, other_new)
+        decode_kernel, pltpu.VMEM((2, BATCH, ROWS, KV_HEADS * HEAD_DIM), BF16), [smem(), smem()] + [vmem()] * 5, vmem()
+    )(me, lengths, got, other_keys, other_values, own_new, other_new)
 
 
 def rope_tables(spread_length):
@@ -550,15 +572,16 @@
     cosine, sine = rope_tables(spread_length)
     buf = qkv_call(me, hidden, gains, own_rows, other_rows, cosine, sine, buf)
     got = lax.all_to_all(buf, XY[::-1], 0, 0, tiled=True)
-    payload, leaving = attend_call(
+    payload, leaving_keys = attend_call(
         me, lengths, got, position, held.reshape(2, PER_GROUP, -1, 2 * HEAD_DIM)
     )
     own_att = to_chips(payload)
     other_att = core_swap(own_att)
-    other_pages = core_swap(leaving)
-    payload = mix_call(me, own_att, other_att, out_weight)
+    other_keys = core_swap(leaving_keys)
+    payload, leaving_values = mix_call(me, own_att, other_att, out_weight, got)
     own_mix = to_chips(payload)
     other_mix = core_swap(own_mix)
+    other_values = core_swap(leaving_values)
     keep, send, stream = ffn_call(me, own_mix, other_mix, hidden, gains, gate_up_weight, down_weight)
     sent = core_swap(send)
     chip = (keep.astype(F32) + sent.astype(F32)).astype(BF16)
@@ -566,7 +589,7 @@
     portion, square = portion_call(me, got_branch)
     squares = to_chips(square)
     result = finish_call(me, portion, stream, squares, core_swap(squares), gains)
-    decoded = decode_call(me, lengths, got, other_pages, own_att, other_att)
+    decoded = decode_call(me, lengths, got, other_keys, other_values, own_att, other_att)
     return result, decoded[None, None]
 
 

time: 182 us -> 183 us (level)
  blocking collectives: 134 us -> 117 us
  waiting for transfers between devices: 3.35 us -> 14.7 us
  starting transfers between devices: 30.1 us -> 37.2 us
    all_to_all x4 -> x3, blocking collectives: 73 us -> 55.5 us  [to_chips(): return lax.all_to_all(tiles, XY, 0, 0, tiled=True)]
    all_to_all x0 -> x1, waiting for transfers between devices: none -> 11.2 us  [to_chips(): return lax.all_to_all(tiles, XY, 0, 0, tiled=True)]
    all_to_all x0 -> x1, starting transfers between devices: none -> 6.65 us  [to_chips(): return lax.all_to_all(tiles, XY, 0, 0, tiled=True)]
    ppermute x6 -> x7, starting transfers between devices: 30.1 us -> 30.5 us  [core_swap(): return lax.ppermute(shard, 'tp_2', [(0, 1), (1, 0)])]
  transfers between devices with their start and end apart: 6 -> 8, of which waited for: 3 -> 4; matrix products, arithmetic and copies ran while one was open for 1% -> 1% of each run, Pallas kernels for 3% -> 3%
where the time goes in v4:
time: 183 us
  blocking collectives  117 us (64%)
  starting transfers between devices  37.2 us (20%)
  waiting for transfers between devices  14.7 us (8%)
  Pallas kernels  10.9 us (6%)
  local copies, waits for them, and re-layouts  2.13 us (1%)
    all_to_all x1, blocking collectives, on_device(): got = lax.all_to_all(buf, XY[::-1], 0, 0, tiled=True)  61.1 us
    all_to_all x3, blocking collectives, to_chips(): return lax.all_to_all(tiles, XY, 0, 0, tiled=True)  55.5 us
    ppermute x7, starting transfers between devices, core_swap(): return lax.ppermute(shard, 'tp_2', [(0, 1), (1, 0)])  30.5 us
    all_to_all x1, waiting for transfers between devices, to_chips(): return lax.all_to_all(tiles, XY, 0, 0, tiled=True)  11.2 us
    all_to_all x1, starting transfers between devices, to_chips(): return lax.all_to_all(tiles, XY, 0, 0, tiled=True)  6.65 us
  transfers between devices with their start and end apart: 8, of which 4 were waited for; matrix products, arithmetic and copies ran while one was open for 1% of the time, Pallas kernels for 3%

profile of v4, /device:TPU:513, one launch (start us, length us, event | category | flops | bytes accessed | tf_op | source)
XLA Modules:
  0.0 183.1 jit_solution(9510971975987320746)
XLA Ops:
  0.6 20.5 %collective-permute-start = (bf16[1,64,4608]{2,1,0:T(8,128)(2,1)}, bf16[1,64,4608]{2,1,0:T(8,128)(2,1)S(1)}, u32[]{:S(2)}, u32[]{:S(2)}) collective-permute-start(bf16[1,64,4608]{2,1,0:T(8,128)(2,1)} %weight_hbm.1), channel_id=1, source_target_pairs={{0,1},{1,0},{2,3},{3,2},{4,5},{5,4},{6,7},{7,6},{8,9},{9,8},{10,11... | collective-permute-start | bytes 1769480 | tf_op jit(solution)/shard_map/ppermute | solution.py:444
  21.2 2.8 %shard_map.104 = (bf16[64,17,8,128]{3,2,1,0:T(8,128)(2,1)S(1)}, bf16[2,2,128,8,256]{4,3,2,1,0:T(8,128)(2,1)S(1)}, bf16[1,64,4608]{2,1,0:T(8,128)(2,1)S(1)}, f32[...) custom-call(s32[1]{0:T(128)} %bitcast.me_ref, s32[32]{0:T(128)} %lengths_ref.3, ...), custom_call_target="tpu_custom_call" | custom-call | tf_op jit(solution)/shard_map/pallas_call | solution.py:453
  24.0 0.1 multiply_sine_fusion
  24.1 0.0 collective-permute-done.other_ref
  24.1 0.7 shard_map.105
  24.8 0.0 copy-start.3
  24.8 61.1 %all_to_all.25.got_ref = bf16[64,17,8,128]{3,2,1,0:T(8,128)(2,1)S(1)} all-to-all(bf16[64,17,8,128]{3,2,1,0:T(8,128)(2,1)S(1)} %shard_map.105), channel_id=1, replica_groups=mesh['grp'=2,'tp_0'=8,'tp_1'=8,'tp_2'=2] {'tp_1','tp_0'}, dimensions={0} | all-to-all | bytes 4456448 | tf_op jit(solution)/shard_map/all_to_all | solution.py:574
  85.9 1.3 shard_map.106
  87.3 0.0 copy-start.4
  87.3 0.8 copy-done.4
  88.1 21.3 %all_to_all.26.own_ref.own_new_ref = bf16[64,16,128]{2,1,0:T(8,128)(2,1)S(1)} all-to-all(bf16[64,16,128]{2,1,0:T(8,128)(2,1)S(1)} %get-tuple-element.25), channel_id=1, replica_groups=mesh['grp'=2,'tp_0'=8,'tp_1'=8,'tp_2'=2] {'tp_0','tp_1'}, dimensions={0} | all-to-all | bytes 524288 | tf_op jit(solution)/shard_map/all_to_all | solution.py:448
  109.3 3.2 %collective-permute-start.1 = (bf16[64,16,128]{2,1,0:T(8,128)(2,1)S(1)}, bf16[64,16,128]{2,1,0:T(8,128)(2,1)S(1)}, u32[]{:S(2)}, u32[]{:S(2)}) collective-permute-start(bf16[64,16,128]{2,1,0:T(8,128)(2,1)S(1)} %all_to_all.26.own_ref.own_new_ref), channel_id=1, source_target_pairs={{0,1},{1,0},{2,3},{3,2},{4,5},{5,4},{6,7},{7,6},{8,9},{9,8},{10,11... | collective-permute-start | bytes 786440 | tf_op jit(solution)/shard_map/ppermute | solution.py:444
  112.6 1.2 collective-permute-done.1.other_ref.other_new_ref
  113.7 1.1 shard_map.107
  114.8 17.5 %all_to_all.27.own_ref = bf16[64,16,128]{2,1,0:T(8,128)(2,1)S(1)} all-to-all(bf16[64,16,128]{2,1,0:T(8,128)(2,1)S(1)} %get-tuple-element.26), channel_id=1, replica_groups=mesh['grp'=2,'tp_0'=8,'tp_1'=8,'tp_2'=2] {'tp_0','tp_1'}, dimensions={0} | all-to-all | bytes 524288 | tf_op jit(solution)/shard_map/all_to_all | solution.py:448
  132.4 2.8 %collective-permute-start.2 = (bf16[64,16,128]{2,1,0:T(8,128)(2,1)S(1)}, bf16[64,16,128]{2,1,0:T(8,128)(2,1)S(1)}, u32[]{:S(2)}, u32[]{:S(2)}) collective-permute-start(bf16[64,16,128]{2,1,0:T(8,128)(2,1)S(1)} %all_to_all.27.own_ref), channel_id=1, source_target_pairs={{0,1},{1,0},{2,3},{3,2},{4,5},{5,4},{6,7},{7,6},{8,9},{9,8},{10,11... | collective-permute-start | bytes 786440 | tf_op jit(solution)/shard_map/ppermute | solution.py:444
  135.2 1.2 collective-permute-done.2.other_ref
  136.4 2.0 %shard_map.108 = (bf16[64,16,128]{2,1,0:T(8,128)(2,1)S(1)}, bf16[64,16,128]{2,1,0:T(8,128)(2,1)S(1)}, f32[32,128]{1,0:T(8,128)S(1)}) custom-call(s32[1]{0:T(128)} %bitcast.me_ref, bf16[64,16,128]{2,1,0:T(8,128)(2,1)S(1)} %all_to_all.27.own_ref, bf16[64,16,128]{2,1,0:T(8,128)(2,1)S(1)} %collective-permute-done.2.other_ref, ...), custom_call_target="tpu_custom_call" | custom-call | tf_op jit(solution)/shard_map/pallas_call | solution.py:514
  138.3 0.5 collective-permute-start.3
  138.8 1.2 collective-permute-done.3
  140.0 0.8 add_convert_fusion
  140.8 6.6 %all-to-all-start.3 = ((bf16[64,16,128]{2,1,0:T(8,128)(2,1)}), bf16[64,16,128]{2,1,0:T(8,128)(2,1)S(1)}, u32[]{:S(2)}, u32[]{:S(2)}) async-start(bf16[64,16,128]{2,1,0:T(8,128)(2,1)} %add_convert_fusion), calls=%async_computation.3 | async-start | bytes 524288 | tf_op jit(solution)/shard_map/all_to_all | solution.py:448
  147.4 0.5 collective-permute-start.5
  147.9 0.1 collective-permute-start.6
  148.1 11.2 %all-to-all-done.3.got_ref = bf16[64,16,128]{2,1,0:T(8,128)(2,1)S(1)} async-done(((bf16[64,16,128]{2,1,0:T(8,128)(2,1)}), bf16[64,16,128]{2,1,0:T(8,128)(2,1)S(1)}, u32[]{:S(2)}, u32[]{:S(2)}) %all-to-all-start.3) | async-done | bytes 262176 | tf_op jit(solution)/shard_map/all_to_all | solution.py:448
  159.3 0.3 shard_map.109
  159.6 16.7 %all_to_all.28.own_ref = f32[64,1,128]{2,1,0:T(1,128)S(1)} all-to-all(f32[64,1,128]{2,1,0:T(1,128)S(1)} %get-tuple-element.31), channel_id=1, replica_groups=mesh['grp'=2,'tp_0'=8,'tp_1'=8,'tp_2'=2] {'tp_0','tp_1'}, dimensions={0} | all-to-all | bytes 65536 | tf_op jit(solution)/shard_map/all_to_all | solution.py:448
  176.3 2.8 %collective-permute-start.4 = (f32[64,1,128]{2,1,0:T(1,128)S(1)}, f32[64,1,128]{2,1,0:T(1,128)S(1)}, u32[]{:S(2)}, u32[]{:S(2)}) collective-permute-start(f32[64,1,128]{2,1,0:T(1,128)S(1)} %all_to_all.28.own_ref), channel_id=1, source_target_pairs={{0,1},{1,0},{2,3},{3,2},{4,5},{5,4},{6,7},{7,6},{8,9},{9,8},{10,11... | collective-permute-start | bytes 98312 | tf_op jit(solution)/shard_map/ppermute | solution.py:444
  179.1 0.0 collective-permute-done.5.keys_ref
  179.1 1.9 %shard_map.111 = bf16[2,32,8,2048]{3,2,1,0:T(8,128)(2,1)S(1)} custom-call(s32[1]{0:T(128)} %bitcast.me_ref, s32[32]{0:T(128)S(1)} %copy-done.3, bf16[64,17,8,128]{3,2,1,0:T(8,128)(2,1)S(1)} %all_to_all.25.got_ref, bf16[64,4,8,128]{3,2,1,0:T(8,128)(2,1)} %collective-permute-done.5.keys_ref, bf16[64,4,8,128]{3,2,1,0:T(8,128)(2,1)} %collective-permute-done.6.values_ref, ...), custom_call_target="tpu_custom_call" | custom-call | tf_op jit(solution)/shard_map/pallas_call | solution.py:544
  181.0 1.3 copy.13
  182.4 0.8 shard_map.110
  (12 shorter events, 0.0 us)
Async XLA Ops:
  0.6 23.4 %collective-permute-start = (bf16[1,64,4608]{2,1,0:T(8,128)(2,1)}, bf16[1,64,4608]{2,1,0:T(8,128)(2,1)S(1)}, u32[]{:S(2)}, u32[]{:S(2)}) collective-permute-start(bf16[1,64,4608]{2,1,0:T(8,128)(2,1)} %weight_hbm.1), channel_id=1, source_target_pairs={{0,1},{1,0},{2,3},{3,2},{4,5},{5,4},{6,7},{7,6},{8,9},{9,8},{10,11... | collective-permute-start | bytes 1769480 | tf_op jit(solution)/shard_map/ppermute | solution.py:444
  24.8 61.1 %copy-start.3 = (s32[32]{0:T(128)S(1)}, s32[32]{0:T(128)}, u32[]{:S(2)}) copy-start(s32[32]{0:T(128)} %lengths_ref.3) | copy-start | bytes 388
  85.9 27.8 %copy-start.2 = (bf16[1,36,4096]{2,1,0:T(8,128)(2,1)S(1)}, bf16[1,36,4096]{2,1,0:T(8,128)(2,1)}, u32[]{:S(2)}) copy-start(bf16[1,36,4096]{2,1,0:T(8,128)(2,1)} %weight_ref.1) | copy-start | bytes 884740
  87.3 0.8 copy-start.4
  88.1 48.3 %copy-start = (bf16[1,2,144,4608]{3,2,1,0:T(8,128)(2,1)S(1)}, bf16[1,2,144,4608]{3,2,1,0:T(8,128)(2,1)}, u32[]{:S(2)}) copy-start(bf16[1,2,144,4608]{3,2,1,0:T(8,128)(2,1)} %gate_up_ref.1) | copy-start | bytes 7962628
  88.1 48.3 %copy-start.1 = (bf16[1,144,4608]{2,1,0:T(8,128)(2,1)S(1)}, bf16[1,144,4608]{2,1,0:T(8,128)(2,1)}, u32[]{:S(2)}) copy-start(bf16[1,144,4608]{2,1,0:T(8,128)(2,1)} %down_ref.1) | copy-start | bytes 3981316
  109.3 4.4 %collective-permute-start.1 = (bf16[64,16,128]{2,1,0:T(8,128)(2,1)S(1)}, bf16[64,16,128]{2,1,0:T(8,128)(2,1)S(1)}, u32[]{:S(2)}, u32[]{:S(2)}) collective-permute-start(bf16[64,16,128]{2,1,0:T(8,128)(2,1)S(1)} %all_to_all.26.own_ref.own_new_ref), channel_id=1, source_target_pairs={{0,1},{1,0},{2,3},{3,2},{4,5},{5,4},{6,7},{7,6},{8,9},{9,8},{10,11... | collective-permute-start | bytes 786440 | tf_op jit(solution)/shard_map/ppermute | solution.py:444
  114.8 20.4 %copy-start.5 = (bf16[64,4,8,128]{3,2,1,0:T(8,128)(2,1)}, bf16[64,4,8,128]{3,2,1,0:T(8,128)(2,1)S(1)}, u32[]{:S(2)}) copy-start(bf16[64,4,8,128]{3,2,1,0:T(8,128)(2,1)S(1)} %get-tuple-element.33) | copy-start | bytes 1572868
  132.4 4.0 %collective-permute-start.2 = (bf16[64,16,128]{2,1,0:T(8,128)(2,1)S(1)}, bf16[64,16,128]{2,1,0:T(8,128)(2,1)S(1)}, u32[]{:S(2)}, u32[]{:S(2)}) collective-permute-start(bf16[64,16,128]{2,1,0:T(8,128)(2,1)S(1)} %all_to_all.27.own_ref), channel_id=1, source_target_pairs={{0,1},{1,0},{2,3},{3,2},{4,5},{5,4},{6,7},{7,6},{8,9},{9,8},{10,11... | collective-permute-start | bytes 786440 | tf_op jit(solution)/shard_map/ppermute | solution.py:444
  138.3 1.7 collective-permute-start.3
  140.8 18.5 %all-to-all-start.3 = ((bf16[64,16,128]{2,1,0:T(8,128)(2,1)}), bf16[64,16,128]{2,1,0:T(8,128)(2,1)S(1)}, u32[]{:S(2)}, u32[]{:S(2)}) async-start(bf16[64,16,128]{2,1,0:T(8,128)(2,1)} %add_convert_fusion), calls=%async_computation.3 | async-start | bytes 524288 | tf_op jit(solution)/shard_map/all_to_all | solution.py:448
  147.4 31.7 %collective-permute-start.5 = (bf16[64,4,8,128]{3,2,1,0:T(8,128)(2,1)}, bf16[64,4,8,128]{3,2,1,0:T(8,128)(2,1)}, u32[]{:S(2)}, u32[]{:S(2)}) collective-permute-start(bf16[64,4,8,128]{3,2,1,0:T(8,128)(2,1)} %copy-done.4), channel_id=1, source_target_pairs={{0,1},{1,0},{2,3},{3,2},{4,5},{5,4},{6,7},{7,6},{8,9},{9,8},{10,11... | collective-permute-start | bytes 1572872 | tf_op jit(solution)/shard_map/ppermute | solution.py:444
  147.9 31.2 %collective-permute-start.6 = (bf16[64,4,8,128]{3,2,1,0:T(8,128)(2,1)}, bf16[64,4,8,128]{3,2,1,0:T(8,128)(2,1)}, u32[]{:S(2)}, u32[]{:S(2)}) collective-permute-start(bf16[64,4,8,128]{3,2,1,0:T(8,128)(2,1)} %copy-done.5), channel_id=1, source_target_pairs={{0,1},{1,0},{2,3},{3,2},{4,5},{5,4},{6,7},{7,6},{8,9},{9,8},{10,11... | collective-permute-start | bytes 1572872 | tf_op jit(solution)/shard_map/ppermute | solution.py:444
  176.3 6.1 %collective-permute-start.4 = (f32[64,1,128]{2,1,0:T(1,128)S(1)}, f32[64,1,128]{2,1,0:T(1,128)S(1)}, u32[]{:S(2)}, u32[]{:S(2)}) collective-permute-start(f32[64,1,128]{2,1,0:T(1,128)S(1)} %all_to_all.28.own_ref), channel_id=1, source_target_pairs={{0,1},{1,0},{2,3},{3,2},{4,5},{5,4},{6,7},{7,6},{8,9},{9,8},{10,11... | collective-permute-start | bytes 98312 | tf_op jit(solution)/shard_map/ppermute | solution.py:444

commit v5 on v4

--- a/solution.py
+++ b/solution.py
@@ -73,7 +73,7 @@
     return lax.broadcasted_iota(jnp.int32, shape, dim)
 
 
-def bulk_place(chip):
+def place_of(chip):
     return ((chip & 7) << 3) | (chip >> 3)
 
 
@@ -143,7 +143,7 @@
 
             def place(j, carry):
                 block = table_ref[PER_GROUP * group + e, j]
-                chip = bulk_place(block >> 1)
+                chip = place_of(block >> 1)
                 at = ((block & 1) ^ core) * PAGE_TILES + e * 2
                 for kv in range(2):
                     page = held_ref[kv, e, j]
@@ -177,7 +177,7 @@
     whole = jnp.concatenate([new_front, new_back], axis=1)
     rows = [whole[ROWS * u : ROWS * u + ROWS, :].astype(BF16) for u in range(BATCH // ROWS)]
     for chip in range(CHIPS):
-        tile_ref[bulk_place(chip)] = rows[chip * BATCH // (CHIPS * ROWS)]
+        tile_ref[place_of(chip)] = rows[chip * BATCH // (CHIPS * ROWS)]
     copy = pltpu.make_async_copy(tile_ref, out_ref.at[:, BULK_TILES - 1], sem)
     copy.start()
     copy.wait()
@@ -201,7 +201,7 @@
     v_head = k_head + KV_HEADS
     fix_head = HEADS + slot * 2 + (m & 1) + KV_HEADS * (m >> 1)
     chosen = jnp.where(kind == 0, q_head, jnp.where(kind == 1, k_head, jnp.where(kind == 2, v_head, fix_head)))
-    pick = jnp.where(n == bulk_place(chosen) * ROWS + rows_at + e, 1.0, 0.0).astype(BF16)
+    pick = jnp.where(n == place_of(chosen) * ROWS + rows_at + e, 1.0, 0.0).astype(BF16)
     source = got_ref[:, BULK_TILES - 1].astype(F32).reshape(n_src, LANES).astype(BF16)
     picked = nn_dot(pick, source)
     q = picked[0:8]
@@ -246,7 +246,7 @@
     quarter = o >> 7
     m = (o >> 5) & 3
     group = (o >> 1) & 15
-    source_row = (group * QUARTERS + quarter) * ROWS + m * 2 + (o & 1)
+    source_row = place_of(group * QUARTERS + quarter) * ROWS + m * 2 + (o & 1)
     pick = jnp.where(n == source_row, 1.0, 0.0).astype(BF16)
     own = own_ref[...][:, :ROWS].astype(F32)
     other = other_ref[...][:, :ROWS].astype(F32)
@@ -304,8 +304,8 @@
     for v in range(BLOCKS):
         low = high = None
         for j in range((LANES * v) // SHARE, (LANES * v + LANES - 1) // SHARE + 1):
-            own = own_ref[j >> 1]
-            other = other_ref[j >> 1]
+            own = own_ref[place_of(j >> 1)]
+            other = other_ref[place_of(j >> 1)]
             piece = (jnp.where(first, own, other) if j % 2 == 0 else jnp.where(first, other, own)).astype(F32)
             start = j * SHARE - LANES * v
             low = piece if low is None else jnp.where(near >= start, piece, low)
@@ -335,8 +335,8 @@
     for p in range(CHIPS):
         even = window(low_ref, high_ref, 2 * p)
         odd = window(low_ref, high_ref, 2 * p + 1)
-        keep_ref[p] = jnp.where(first, even, odd).astype(BF16)
-        send_ref[p] = jnp.where(first, odd, even).astype(BF16)
+        keep_ref[place_of(p)] = jnp.where(first, even, odd).astype(BF16)
+        send_ref[place_of(p)] = jnp.where(first, odd, even).astype(BF16)
     start = me * SHARE
     at = start // LANES
     off = start % LANES
@@ -387,7 +387,7 @@
     def place(first_core):
         def body(g, carry):
             for y in range(QUARTERS):
-                s = bulk_place(g * QUARTERS + y)
+                s = place_of(g * QUARTERS + y)
                 for side in range(2):
                     slot = 2 * y + (first_core if side == 0 else 1 - first_core)
                     for kv in range(2):
@@ -421,7 +421,7 @@
             token = iota((ROWS, LANES), 0) == (length & 7)
             which = iota((2 * ROWS, LANES), 0)
             for y in range(QUARTERS):
-                s = g * QUARTERS + y
+                s = place_of(g * QUARTERS + y)
                 own = own_new_ref[s].astype(F32)
                 other = other_new_ref[s].astype(F32)
                 for c in range(2):
@@ -445,7 +445,7 @@
 
 
 def to_chips(tiles):
-    return lax.all_to_all(tiles, XY, 0, 0, tiled=True)
+    return lax.all_to_all(tiles, XY[::-1], 0, 0, tiled=True)
 
 
 def pages_call(me, lengths, table, cache, weight, hidden, gains):
@@ -571,7 +571,7 @@
     )
     cosine, sine = rope_tables(spread_length)
     buf = qkv_call(me, hidden, gains, own_rows, other_rows, cosine, sine, buf)
-    got = lax.all_to_all(buf, XY[::-1], 0, 0, tiled=True)
+    got = to_chips(buf)
     payload, leaving_keys = attend_call(
         me, lengths, got, position, held.reshape(2, PER_GROUP, -1, 2 * HEAD_DIM)
     )

time: 183 us -> 183 us (level)
  no operation moved by 1% of the time
where the time goes in v5:
time: 183 us
  blocking collectives  117 us (64%)
  starting transfers between devices  36.8 us (20%)
  waiting for transfers between devices  14.9 us (8%)
  Pallas kernels  11 us (6%)
  local copies, waits for them, and re-layouts  2.13 us (1%)
    all_to_all x4, blocking collectives, to_chips(): return lax.all_to_all(tiles, XY[::-1], 0, 0, tiled=True)  117 us
    ppermute x7, starting transfers between devices, core_swap(): return lax.ppermute(shard, 'tp_2', [(0, 1), (1, 0)])  30.1 us
    all_to_all x1, waiting for transfers between devices, to_chips(): return lax.all_to_all(tiles, XY[::-1], 0, 0, tiled=True)  11.4 us
    all_to_all x1, starting transfers between devices, to_chips(): return lax.all_to_all(tiles, XY[::-1], 0, 0, tiled=True)  6.65 us
  transfers between devices with their start and end apart: 8, of which 4 were waited for; matrix products, arithmetic and copies ran while one was open for 1% of the time, Pallas kernels for 3%

profile of v5, /device:TPU:513, one launch (start us, length us, event | category | flops | bytes accessed | tf_op | source)
XLA Modules:
  0.0 182.8 jit_solution(5795554222894863265)
XLA Ops:
  0.6 20.5 %collective-permute-start = (bf16[1,64,4608]{2,1,0:T(8,128)(2,1)}, bf16[1,64,4608]{2,1,0:T(8,128)(2,1)S(1)}, u32[]{:S(2)}, u32[]{:S(2)}) collective-permute-start(bf16[1,64,4608]{2,1,0:T(8,128)(2,1)} %weight_hbm.1), channel_id=1, source_target_pairs={{0,1},{1,0},{2,3},{3,2},{4,5},{5,4},{6,7},{7,6},{8,9},{9,8},{10,11... | collective-permute-start | bytes 1769480 | tf_op jit(solution)/shard_map/ppermute | solution.py:444
  21.2 2.8 %shard_map.104 = (bf16[64,17,8,128]{3,2,1,0:T(8,128)(2,1)S(1)}, bf16[2,2,128,8,256]{4,3,2,1,0:T(8,128)(2,1)S(1)}, bf16[1,64,4608]{2,1,0:T(8,128)(2,1)S(1)}, f32[...) custom-call(s32[1]{0:T(128)} %bitcast.me_ref, s32[32]{0:T(128)} %lengths_ref.3, ...), custom_call_target="tpu_custom_call" | custom-call | tf_op jit(solution)/shard_map/pallas_call | solution.py:453
  24.0 0.1 multiply_sine_fusion
  24.1 0.0 collective-permute-done.other_ref
  24.1 0.7 shard_map.105
  24.8 0.0 copy-start.3
  24.8 61.1 %all_to_all.25.got_ref = bf16[64,17,8,128]{3,2,1,0:T(8,128)(2,1)S(1)} all-to-all(bf16[64,17,8,128]{3,2,1,0:T(8,128)(2,1)S(1)} %shard_map.105), channel_id=1, replica_groups=mesh['grp'=2,'tp_0'=8,'tp_1'=8,'tp_2'=2] {'tp_1','tp_0'}, dimensions={0} | all-to-all | bytes 4456448 | tf_op jit(solution)/shard_map/all_to_all | solution.py:448
  85.9 1.3 shard_map.106
  87.3 0.0 copy-start.4
  87.3 0.8 copy-done.4
  88.1 21.2 %all_to_all.26.own_ref.own_new_ref = bf16[64,16,128]{2,1,0:T(8,128)(2,1)S(1)} all-to-all(bf16[64,16,128]{2,1,0:T(8,128)(2,1)S(1)} %get-tuple-element.25), channel_id=1, replica_groups=mesh['grp'=2,'tp_0'=8,'tp_1'=8,'tp_2'=2] {'tp_1','tp_0'}, dimensions={0} | all-to-all | bytes 524288 | tf_op jit(solution)/shard_map/all_to_all | solution.py:448
  109.3 3.2 %collective-permute-start.1 = (bf16[64,16,128]{2,1,0:T(8,128)(2,1)S(1)}, bf16[64,16,128]{2,1,0:T(8,128)(2,1)S(1)}, u32[]{:S(2)}, u32[]{:S(2)}) collective-permute-start(bf16[64,16,128]{2,1,0:T(8,128)(2,1)S(1)} %all_to_all.26.own_ref.own_new_ref), channel_id=1, source_target_pairs={{0,1},{1,0},{2,3},{3,2},{4,5},{5,4},{6,7},{7,6},{8,9},{9,8},{10,11... | collective-permute-start | bytes 786440 | tf_op jit(solution)/shard_map/ppermute | solution.py:444
  112.5 1.2 collective-permute-done.1.other_ref.other_new_ref
  113.6 1.1 shard_map.107
  114.8 17.5 %all_to_all.27.own_ref = bf16[64,16,128]{2,1,0:T(8,128)(2,1)S(1)} all-to-all(bf16[64,16,128]{2,1,0:T(8,128)(2,1)S(1)} %get-tuple-element.26), channel_id=1, replica_groups=mesh['grp'=2,'tp_0'=8,'tp_1'=8,'tp_2'=2] {'tp_1','tp_0'}, dimensions={0} | all-to-all | bytes 524288 | tf_op jit(solution)/shard_map/all_to_all | solution.py:448
  132.3 2.6 %collective-permute-start.2 = (bf16[64,16,128]{2,1,0:T(8,128)(2,1)S(1)}, bf16[64,16,128]{2,1,0:T(8,128)(2,1)S(1)}, u32[]{:S(2)}, u32[]{:S(2)}) collective-permute-start(bf16[64,16,128]{2,1,0:T(8,128)(2,1)S(1)} %all_to_all.27.own_ref), channel_id=1, source_target_pairs={{0,1},{1,0},{2,3},{3,2},{4,5},{5,4},{6,7},{7,6},{8,9},{9,8},{10,11... | collective-permute-start | bytes 786440 | tf_op jit(solution)/shard_map/ppermute | solution.py:444
  134.9 1.2 collective-permute-done.2.other_ref
  136.1 2.0 %shard_map.108 = (bf16[64,16,128]{2,1,0:T(8,128)(2,1)S(1)}, bf16[64,16,128]{2,1,0:T(8,128)(2,1)S(1)}, f32[32,128]{1,0:T(8,128)S(1)}) custom-call(s32[1]{0:T(128)} %bitcast.me_ref, bf16[64,16,128]{2,1,0:T(8,128)(2,1)S(1)} %all_to_all.27.own_ref, bf16[64,16,128]{2,1,0:T(8,128)(2,1)S(1)} %collective-permute-done.2.other_ref, ...), custom_call_target="tpu_custom_call" | custom-call | tf_op jit(solution)/shard_map/pallas_call | solution.py:514
  138.0 0.5 collective-permute-start.3
  138.5 1.2 collective-permute-done.3
  139.7 0.8 add_convert_fusion
  140.5 6.6 %all-to-all-start.3 = ((bf16[64,16,128]{2,1,0:T(8,128)(2,1)}), bf16[64,16,128]{2,1,0:T(8,128)(2,1)S(1)}, u32[]{:S(2)}, u32[]{:S(2)}) async-start(bf16[64,16,128]{2,1,0:T(8,128)(2,1)} %add_convert_fusion), calls=%async_computation.3 | async-start | bytes 524288 | tf_op jit(solution)/shard_map/all_to_all | solution.py:448
  147.1 0.5 collective-permute-start.5
  147.6 0.1 collective-permute-start.6
  147.8 11.4 %all-to-all-done.3.got_ref = bf16[64,16,128]{2,1,0:T(8,128)(2,1)S(1)} async-done(((bf16[64,16,128]{2,1,0:T(8,128)(2,1)}), bf16[64,16,128]{2,1,0:T(8,128)(2,1)S(1)}, u32[]{:S(2)}, u32[]{:S(2)}) %all-to-all-start.3) | async-done | bytes 262176 | tf_op jit(solution)/shard_map/all_to_all | solution.py:448
  159.1 0.3 shard_map.109
  159.5 16.7 %all_to_all.28.own_ref = f32[64,1,128]{2,1,0:T(1,128)S(1)} all-to-all(f32[64,1,128]{2,1,0:T(1,128)S(1)} %get-tuple-element.31), channel_id=1, replica_groups=mesh['grp'=2,'tp_0'=8,'tp_1'=8,'tp_2'=2] {'tp_1','tp_0'}, dimensions={0} | all-to-all | bytes 65536 | tf_op jit(solution)/shard_map/all_to_all | solution.py:448
  176.1 2.7 %collective-permute-start.4 = (f32[64,1,128]{2,1,0:T(1,128)S(1)}, f32[64,1,128]{2,1,0:T(1,128)S(1)}, u32[]{:S(2)}, u32[]{:S(2)}) collective-permute-start(f32[64,1,128]{2,1,0:T(1,128)S(1)} %all_to_all.28.own_ref), channel_id=1, source_target_pairs={{0,1},{1,0},{2,3},{3,2},{4,5},{5,4},{6,7},{7,6},{8,9},{9,8},{10,11... | collective-permute-start | bytes 98312 | tf_op jit(solution)/shard_map/ppermute | solution.py:444
  178.8 0.0 collective-permute-done.5.keys_ref
  178.8 1.9 %shard_map.111 = bf16[2,32,8,2048]{3,2,1,0:T(8,128)(2,1)S(1)} custom-call(s32[1]{0:T(128)} %bitcast.me_ref, s32[32]{0:T(128)S(1)} %copy-done.3, bf16[64,17,8,128]{3,2,1,0:T(8,128)(2,1)S(1)} %all_to_all.25.got_ref, bf16[64,4,8,128]{3,2,1,0:T(8,128)(2,1)} %collective-permute-done.5.keys_ref, bf16[64,4,8,128]{3,2,1,0:T(8,128)(2,1)} %collective-permute-done.6.values_ref, ...), custom_call_target="tpu_custom_call" | custom-call | tf_op jit(solution)/shard_map/pallas_call | solution.py:544
  180.7 1.3 copy.13
  182.1 0.8 shard_map.110
  (12 shorter events, 0.0 us)
Async XLA Ops:
  0.6 23.4 %collective-permute-start = (bf16[1,64,4608]{2,1,0:T(8,128)(2,1)}, bf16[1,64,4608]{2,1,0:T(8,128)(2,1)S(1)}, u32[]{:S(2)}, u32[]{:S(2)}) collective-permute-start(bf16[1,64,4608]{2,1,0:T(8,128)(2,1)} %weight_hbm.1), channel_id=1, source_target_pairs={{0,1},{1,0},{2,3},{3,2},{4,5},{5,4},{6,7},{7,6},{8,9},{9,8},{10,11... | collective-permute-start | bytes 1769480 | tf_op jit(solution)/shard_map/ppermute | solution.py:444
  24.8 61.1 %copy-start.3 = (s32[32]{0:T(128)S(1)}, s32[32]{0:T(128)}, u32[]{:S(2)}) copy-start(s32[32]{0:T(128)} %lengths_ref.3) | copy-start | bytes 388
  85.9 27.7 %copy-start.2 = (bf16[1,36,4096]{2,1,0:T(8,128)(2,1)S(1)}, bf16[1,36,4096]{2,1,0:T(8,128)(2,1)}, u32[]{:S(2)}) copy-start(bf16[1,36,4096]{2,1,0:T(8,128)(2,1)} %weight_ref.1) | copy-start | bytes 884740
  87.3 0.8 copy-start.4
  88.1 48.0 %copy-start = (bf16[1,2,144,4608]{3,2,1,0:T(8,128)(2,1)S(1)}, bf16[1,2,144,4608]{3,2,1,0:T(8,128)(2,1)}, u32[]{:S(2)}) copy-start(bf16[1,2,144,4608]{3,2,1,0:T(8,128)(2,1)} %gate_up_ref.1) | copy-start | bytes 7962628
  88.1 48.0 %copy-start.1 = (bf16[1,144,4608]{2,1,0:T(8,128)(2,1)S(1)}, bf16[1,144,4608]{2,1,0:T(8,128)(2,1)}, u32[]{:S(2)}) copy-start(bf16[1,144,4608]{2,1,0:T(8,128)(2,1)} %down_ref.1) | copy-start | bytes 3981316
  109.3 4.3 %collective-permute-start.1 = (bf16[64,16,128]{2,1,0:T(8,128)(2,1)S(1)}, bf16[64,16,128]{2,1,0:T(8,128)(2,1)S(1)}, u32[]{:S(2)}, u32[]{:S(2)}) collective-permute-start(bf16[64,16,128]{2,1,0:T(8,128)(2,1)S(1)} %all_to_all.26.own_ref.own_new_ref), channel_id=1, source_target_pairs={{0,1},{1,0},{2,3},{3,2},{4,5},{5,4},{6,7},{7,6},{8,9},{9,8},{10,11... | collective-permute-start | bytes 786440 | tf_op jit(solution)/shard_map/ppermute | solution.py:444
  114.8 20.1 %copy-start.5 = (bf16[64,4,8,128]{3,2,1,0:T(8,128)(2,1)}, bf16[64,4,8,128]{3,2,1,0:T(8,128)(2,1)S(1)}, u32[]{:S(2)}) copy-start(bf16[64,4,8,128]{3,2,1,0:T(8,128)(2,1)S(1)} %get-tuple-element.33) | copy-start | bytes 1572868
  132.3 3.7 %collective-permute-start.2 = (bf16[64,16,128]{2,1,0:T(8,128)(2,1)S(1)}, bf16[64,16,128]{2,1,0:T(8,128)(2,1)S(1)}, u32[]{:S(2)}, u32[]{:S(2)}) collective-permute-start(bf16[64,16,128]{2,1,0:T(8,128)(2,1)S(1)} %all_to_all.27.own_ref), channel_id=1, source_target_pairs={{0,1},{1,0},{2,3},{3,2},{4,5},{5,4},{6,7},{7,6},{8,9},{9,8},{10,11... | collective-permute-start | bytes 786440 | tf_op jit(solution)/shard_map/ppermute | solution.py:444
  138.0 1.7 collective-permute-start.3
  140.5 18.7 %all-to-all-start.3 = ((bf16[64,16,128]{2,1,0:T(8,128)(2,1)}), bf16[64,16,128]{2,1,0:T(8,128)(2,1)S(1)}, u32[]{:S(2)}, u32[]{:S(2)}) async-start(bf16[64,16,128]{2,1,0:T(8,128)(2,1)} %add_convert_fusion), calls=%async_computation.3 | async-start | bytes 524288 | tf_op jit(solution)/shard_map/all_to_all | solution.py:448
  147.1 31.7 %collective-permute-start.5 = (bf16[64,4,8,128]{3,2,1,0:T(8,128)(2,1)}, bf16[64,4,8,128]{3,2,1,0:T(8,128)(2,1)}, u32[]{:S(2)}, u32[]{:S(2)}) collective-permute-start(bf16[64,4,8,128]{3,2,1,0:T(8,128)(2,1)} %copy-done.4), channel_id=1, source_target_pairs={{0,1},{1,0},{2,3},{3,2},{4,5},{5,4},{6,7},{7,6},{8,9},{9,8},{10,11... | collective-permute-start | bytes 1572872 | tf_op jit(solution)/shard_map/ppermute | solution.py:444
  147.6 31.2 %collective-permute-start.6 = (bf16[64,4,8,128]{3,2,1,0:T(8,128)(2,1)}, bf16[64,4,8,128]{3,2,1,0:T(8,128)(2,1)}, u32[]{:S(2)}, u32[]{:S(2)}) collective-permute-start(bf16[64,4,8,128]{3,2,1,0:T(8,128)(2,1)} %copy-done.5), channel_id=1, source_target_pairs={{0,1},{1,0},{2,3},{3,2},{4,5},{5,4},{6,7},{7,6},{8,9},{9,8},{10,11... | collective-permute-start | bytes 1572872 | tf_op jit(solution)/shard_map/ppermute | solution.py:444
  176.1 5.9 %collective-permute-start.4 = (f32[64,1,128]{2,1,0:T(1,128)S(1)}, f32[64,1,128]{2,1,0:T(1,128)S(1)}, u32[]{:S(2)}, u32[]{:S(2)}) collective-permute-start(f32[64,1,128]{2,1,0:T(1,128)S(1)} %all_to_all.28.own_ref), channel_id=1, source_target_pairs={{0,1},{1,0},{2,3},{3,2},{4,5},{5,4},{6,7},{7,6},{8,9},{9,8},{10,11... | collective-permute-start | bytes 98312 | tf_op jit(solution)/shard_map/ppermute | solution.py:444

commit v6 on v5

--- a/solution.py
+++ b/solution.py
@@ -233,13 +233,22 @@
     leave.wait()
 
 
-def mix_kernel(me_ref, own_ref, other_ref, weight_ref, got_ref, out_ref, leaving_ref, sem):
+def mixed_half(pieces, weight_ref, core, pick):
+    rows = nn_dot(pick, pieces[:, :ROWS].astype(F32).reshape(CHIPS * ROWS, LANES).astype(BF16)).astype(BF16)
+    left = jnp.concatenate([rows[BATCH * b : BATCH * b + BATCH] for b in range(16)], axis=1)
+    wide = 4 * HEAD_DIM
+    right = jnp.concatenate(
+        [weight_ref[0, :, pl.ds(pl.multiple_of((2 * y + core) * wide, wide), wide)] for y in range(QUARTERS)],
+        axis=1,
+    )
+    return nt_dot(left, right)
+
+
+def mix_own_kernel(me_ref, own_ref, weight_ref, got_ref, part_ref, pick_ref, leaving_ref, sem):
     leave = pltpu.make_async_copy(
         got_ref.at[:, pl.ds(PAGE_TILES + PAGE_TILES // 2, PAGE_TILES // 2)], leaving_ref, sem
     )
     leave.start()
-    me = me_ref[0]
-    first = (me & 1) == 0
     n_src = CHIPS * ROWS
     o = iota((n_src, n_src), 0)
     n = iota((n_src, n_src), 1)
@@ -247,24 +256,19 @@
     m = (o >> 5) & 3
     group = (o >> 1) & 15
     source_row = place_of(group * QUARTERS + quarter) * ROWS + m * 2 + (o & 1)
-    pick = jnp.where(n == source_row, 1.0, 0.0).astype(BF16)
-    own = own_ref[...][:, :ROWS].astype(F32)
-    other = other_ref[...][:, :ROWS].astype(F32)
-    mixed = jnp.zeros((BATCH, SHARE), F32)
-    for c in range(2):
-        mine = jnp.where(first, own, other) if c == 0 else jnp.where(first, other, own)
-        rows = nn_dot(pick, mine.reshape(n_src, LANES).astype(BF16)).astype(BF16)
-        left = jnp.concatenate([rows[BATCH * b : BATCH * b + BATCH] for b in range(16)], axis=1)
-        right = jnp.concatenate(
-            [weight_ref[0, :, (2 * y + c) * 512 : (2 * y + c) * 512 + 512] for y in range(QUARTERS)], axis=1
-        )
-        mixed = mixed + nt_dot(left, right)
+    pick_ref[...] = jnp.where(n == source_row, 1.0, 0.0).astype(BF16)
+    part_ref[...] = mixed_half(own_ref[...], weight_ref, me_ref[0] & 1, pick_ref[...])
+    leave.wait()
+
+
+def mix_kernel(me_ref, other_ref, weight_ref, part_ref, pick_ref, out_ref):
+    me = me_ref[0]
+    mixed = part_ref[...] + mixed_half(other_ref[...], weight_ref, 1 - (me & 1), pick_ref[...])
     values = mixed.astype(BF16).astype(F32)
     gap = jnp.zeros((HALF, LANES // 2 - SHARE), F32)
     packed = jnp.concatenate([values[:HALF], gap, values[HALF:], gap], axis=1)
     turned = pltpu.roll(packed, (me * SHARE) % LANES, 1).astype(BF16)
     out_ref[...] = jnp.broadcast_to(turned[None], (CHIPS, HALF, LANES))
-    leave.wait()
 
 
 def window(low_ref, high_ref, j):
@@ -279,9 +283,31 @@
     return jnp.where((lane - off) % LANES < LANES // 2, low, high)
 
 
+def placed(pieces_ref, parity, v):
+    near = iota((HALF, LANES), 1)
+    far = (near + LANES // 2) % LANES
+    low = high = jnp.zeros((HALF, LANES), F32)
+    for j in range((LANES * v) // SHARE, (LANES * v + LANES - 1) // SHARE + 1):
+        if j % 2 == parity:
+            piece = pieces_ref[place_of(j >> 1)].astype(F32)
+            start = j * SHARE - LANES * v
+            low = jnp.where((near >= start) & (near < start + SHARE), piece, low)
+            high = jnp.where((far >= start) & (far < start + SHARE), piece, high)
+    return jnp.concatenate([low, pltpu.roll(high, LANES // 2, 1)], axis=0)
+
+
+def place_own_kernel(me_ref, own_ref, out_ref):
+    for parity in range(2):
+
+        @pl.when((me_ref[0] & 1) == parity)
+        def _():
+            for v in range(BLOCKS):
+                out_ref[v] = placed(own_ref, parity, v)
+
+
 def ffn_kernel(
     me_ref,
-    own_ref,
+    placed_ref,
     other_ref,
     hidden_ref,
     gain_ref,
@@ -298,21 +324,16 @@
     me = me_ref[0]
     first = (me & 1) == 0
     lane = iota((BATCH, LANES), 1)
-    near = iota((HALF, LANES), 1)
-    far = (near + LANES // 2) % LANES
+    for parity in range(2):
+
+        @pl.when((me & 1) != parity)
+        def _():
+            for v in range(BLOCKS):
+                wide_ref[v] = placed_ref[v] + placed(other_ref, parity, v)
+
     total = jnp.zeros((BATCH, LANES), F32)
     for v in range(BLOCKS):
-        low = high = None
-        for j in range((LANES * v) // SHARE, (LANES * v + LANES - 1) // SHARE + 1):
-            own = own_ref[place_of(j >> 1)]
-            other = other_ref[place_of(j >> 1)]
-            piece = (jnp.where(first, own, other) if j % 2 == 0 else jnp.where(first, other, own)).astype(F32)
-            start = j * SHARE - LANES * v
-            low = piece if low is None else jnp.where(near >= start, piece, low)
-            high = piece if high is None else jnp.where(far >= start, piece, high)
-        block = jnp.concatenate([low, pltpu.roll(high, LANES // 2, 1)], axis=0)
-        wide_ref[v] = block
-        total = total + block * block
+        total = total + wide_ref[v] * wide_ref[v]
     scale = lax.rsqrt(jnp.sum(total, axis=-1, keepdims=True) * (1.0 / D) + EPSILON)
     total = jnp.zeros((BATCH, LANES), F32)
     for v in range(BLOCKS):
@@ -496,17 +517,28 @@
     )(me, lengths, got, position, cache)
 
 
-def mix_call(me, own, other, weight, got):
-    return call(
-        mix_kernel,
+def mix_own_call(me, own, weight, got):
+    return call(
+        mix_own_kernel,
         (
-            pltpu.VMEM((CHIPS, HALF, LANES), BF16),
+            pltpu.VMEM((BATCH, SHARE), F32),
+            pltpu.VMEM((CHIPS * ROWS, CHIPS * ROWS), BF16),
             pltpu.VMEM((CHIPS, PAGE_TILES // 2, ROWS, LANES), BF16),
         ),
-        [smem()] + [vmem()] * 4,
-        (vmem(), vmem()),
+        [smem()] + [vmem()] * 3,
+        (vmem(),) * 3,
         scratch_shapes=[pltpu.SemaphoreType.DMA],
-    )(me, own, other, weight, got)
+    )(me, own, weight, got)
+
+
+def mix_call(me, other, weight, part, pick):
+    return call(
+        mix_kernel, pltpu.VMEM((CHIPS, HALF, LANES), BF16), [smem()] + [vmem()] * 4, vmem()
+    )(me, other, weight, part, pick)
+
+
+def place_own_call(me, own):
+    return call(place_own_kernel, pltpu.VMEM((BLOCKS, BATCH, LANES), F32), [smem(), vmem()], vmem())(me, own)
 
 
 def ffn_call(me, own, other, hidden, gains, gate_up, down):
@@ -578,11 +610,13 @@
     own_att = to_chips(payload)
     other_att = core_swap(own_att)
     other_keys = core_swap(leaving_keys)
-    payload, leaving_values = mix_call(me, own_att, other_att, out_weight, got)
+    part, pick, leaving_values = mix_own_call(me, own_att, out_weight, got)
+    payload = mix_call(me, other_att, out_weight, part, pick)
     own_mix = to_chips(payload)
     other_mix = core_swap(own_mix)
+    placed_mix = place_own_call(me, own_mix)
     other_values = core_swap(leaving_values)
-    keep, send, stream = ffn_call(me, own_mix, other_mix, hidden, gains, gate_up_weight, down_weight)
+    keep, send, stream = ffn_call(me, placed_mix, other_mix, hidden, gains, gate_up_weight, down_weight)
     sent = core_swap(send)
     chip = (keep.astype(F32) + sent.astype(F32)).astype(BF16)
     got_branch = to_chips(chip)

time: 183 us -> 183 us (level)
  transfers between devices with their start and end apart: 8 -> 8, of which waited for: 4 -> 3; matrix products, arithmetic and copies ran while one was open for 1% -> 1% of each run, Pallas kernels for 3% -> 3%
where the time goes in v6:
time: 183 us; the launch traced here: 182 us
  blocking collectives  116 us (63%)
  starting transfers between devices  36.6 us (20%)
  waiting for transfers between devices  13.5 us (7%)
  Pallas kernels  11.1 us (6%)
  local copies, waits for them, and re-layouts  2.91 us (2%)
    all_to_all x4, blocking collectives, to_chips(): return lax.all_to_all(tiles, XY[::-1], 0, 0, tiled=True)  116 us
    ppermute x7, starting transfers between devices, core_swap(): return lax.ppermute(shard, 'tp_2', [(0, 1), (1, 0)])  30 us
    all_to_all x1, waiting for transfers between devices, to_chips(): return lax.all_to_all(tiles, XY[::-1], 0, 0, tiled=True)  11.4 us
    all_to_all x1, starting transfers between devices, to_chips(): return lax.all_to_all(tiles, XY[::-1], 0, 0, tiled=True)  6.65 us
  transfers between devices with their start and end apart: 8, of which 3 were waited for; matrix products, arithmetic and copies ran while one was open for 1% of the time, Pallas kernels for 3%

profile of v6, /device:TPU:513, one launch (start us, length us, event | category | flops | bytes accessed | tf_op | source)
XLA Modules:
  0.0 182.2 jit_solution(10583862474840123912)
XLA Ops:
  0.6 20.5 %collective-permute-start = (bf16[1,64,4608]{2,1,0:T(8,128)(2,1)}, bf16[1,64,4608]{2,1,0:T(8,128)(2,1)S(1)}, u32[]{:S(2)}, u32[]{:S(2)}) collective-permute-start(bf16[1,64,4608]{2,1,0:T(8,128)(2,1)} %weight_hbm.1), channel_id=1, source_target_pairs={{0,1},{1,0},{2,3},{3,2},{4,5},{5,4},{6,7},{7,6},{8,9},{9,8},{10,11... | collective-permute-start | bytes 1769480 | tf_op jit(solution)/shard_map/ppermute | solution.py:465
  21.2 2.8 %shard_map.104 = (bf16[64,17,8,128]{3,2,1,0:T(8,128)(2,1)S(1)}, bf16[2,2,128,8,256]{4,3,2,1,0:T(8,128)(2,1)S(1)}, bf16[1,64,4608]{2,1,0:T(8,128)(2,1)S(1)}, f32[...) custom-call(s32[1]{0:T(128)} %bitcast.me_ref, s32[32]{0:T(128)} %lengths_ref.3, ...), custom_call_target="tpu_custom_call" | custom-call | tf_op jit(solution)/shard_map/pallas_call | solution.py:474
  24.0 0.1 multiply_sine_fusion
  24.1 0.7 shard_map.105
  24.8 0.0 copy-start.3
  24.8 61.1 %all_to_all.25.got_ref = bf16[64,17,8,128]{3,2,1,0:T(8,128)(2,1)S(1)} all-to-all(bf16[64,17,8,128]{3,2,1,0:T(8,128)(2,1)S(1)} %shard_map.105), channel_id=1, replica_groups=mesh['grp'=2,'tp_0'=8,'tp_1'=8,'tp_2'=2] {'tp_1','tp_0'}, dimensions={0} | all-to-all | bytes 4456448 | tf_op jit(solution)/shard_map/all_to_all | solution.py:469
  85.9 1.3 shard_map.106
  87.3 0.0 copy-start.4
  87.3 0.8 copy-done.4
  88.1 20.9 %all_to_all.26.own_ref.own_new_ref = bf16[64,16,128]{2,1,0:T(8,128)(2,1)S(1)} all-to-all(bf16[64,16,128]{2,1,0:T(8,128)(2,1)S(1)} %get-tuple-element.26), channel_id=1, replica_groups=mesh['grp'=2,'tp_0'=8,'tp_1'=8,'tp_2'=2] {'tp_1','tp_0'}, dimensions={0} | all-to-all | bytes 524288 | tf_op jit(solution)/shard_map/all_to_all | solution.py:469
  109.0 3.2 %collective-permute-start.1 = (bf16[64,16,128]{2,1,0:T(8,128)(2,1)S(1)}, bf16[64,16,128]{2,1,0:T(8,128)(2,1)S(1)}, u32[]{:S(2)}, u32[]{:S(2)}) collective-permute-start(bf16[64,16,128]{2,1,0:T(8,128)(2,1)S(1)} %all_to_all.26.own_ref.own_new_ref), channel_id=1, source_target_pairs={{0,1},{1,0},{2,3},{3,2},{4,5},{5,4},{6,7},{7,6},{8,9},{9,8},{10,11... | collective-permute-start | bytes 786440 | tf_op jit(solution)/shard_map/ppermute | solution.py:465
  112.2 0.6 shard_map.107
  112.8 0.8 copy-done.5
  113.5 0.6 shard_map.108
  114.2 17.7 %all_to_all.27.own_ref = bf16[64,16,128]{2,1,0:T(8,128)(2,1)S(1)} all-to-all(bf16[64,16,128]{2,1,0:T(8,128)(2,1)S(1)} %shard_map.108), channel_id=1, replica_groups=mesh['grp'=2,'tp_0'=8,'tp_1'=8,'tp_2'=2] {'tp_1','tp_0'}, dimensions={0} | all-to-all | bytes 524288 | tf_op jit(solution)/shard_map/all_to_all | solution.py:469
  131.9 2.4 %collective-permute-start.2 = (bf16[64,16,128]{2,1,0:T(8,128)(2,1)S(1)}, bf16[64,16,128]{2,1,0:T(8,128)(2,1)S(1)}, u32[]{:S(2)}, u32[]{:S(2)}) collective-permute-start(bf16[64,16,128]{2,1,0:T(8,128)(2,1)S(1)} %all_to_all.27.own_ref), channel_id=1, source_target_pairs={{0,1},{1,0},{2,3},{3,2},{4,5},{5,4},{6,7},{7,6},{8,9},{9,8},{10,11... | collective-permute-start | bytes 786440 | tf_op jit(solution)/shard_map/ppermute | solution.py:465
  134.3 0.2 shard_map.109.placed_ref
  134.5 1.0 collective-permute-done.2.other_ref
  135.5 2.0 %shard_map.110 = (bf16[64,16,128]{2,1,0:T(8,128)(2,1)S(1)}, bf16[64,16,128]{2,1,0:T(8,128)(2,1)S(1)}, f32[32,128]{1,0:T(8,128)S(1)}) custom-call(s32[1]{0:T(128)} %bitcast.me_ref, f32[36,32,128]{2,1,0:T(8,128)S(1)} %shard_map.109.placed_ref, bf16[64,16,128]{2,1,0:T(8,128)(2,1)S(1)} %collective-permute-done.2.other_ref, ...), custom_call_target="tpu_custom_call" | custom-call | tf_op jit(solution)/shard_map/pallas_call | solution.py:546
  137.4 0.5 collective-permute-start.3
  137.9 1.2 collective-permute-done.3
  139.1 0.8 add_convert_fusion
  139.9 6.7 %all-to-all-start.3 = ((bf16[64,16,128]{2,1,0:T(8,128)(2,1)}), bf16[64,16,128]{2,1,0:T(8,128)(2,1)S(1)}, u32[]{:S(2)}, u32[]{:S(2)}) async-start(bf16[64,16,128]{2,1,0:T(8,128)(2,1)} %add_convert_fusion), calls=%async_computation.3 | async-start | bytes 524288 | tf_op jit(solution)/shard_map/all_to_all | solution.py:469
  146.5 0.5 collective-permute-start.5
  147.0 0.1 collective-permute-start.6
  147.2 11.4 %all-to-all-done.3.got_ref = bf16[64,16,128]{2,1,0:T(8,128)(2,1)S(1)} async-done(((bf16[64,16,128]{2,1,0:T(8,128)(2,1)}), bf16[64,16,128]{2,1,0:T(8,128)(2,1)S(1)}, u32[]{:S(2)}, u32[]{:S(2)}) %all-to-all-start.3) | async-done | bytes 262176 | tf_op jit(solution)/shard_map/all_to_all | solution.py:469
  158.5 0.3 shard_map.111
  158.9 16.7 %all_to_all.28.own_ref = f32[64,1,128]{2,1,0:T(1,128)S(1)} all-to-all(f32[64,1,128]{2,1,0:T(1,128)S(1)} %get-tuple-element.33), channel_id=1, replica_groups=mesh['grp'=2,'tp_0'=8,'tp_1'=8,'tp_2'=2] {'tp_1','tp_0'}, dimensions={0} | all-to-all | bytes 65536 | tf_op jit(solution)/shard_map/all_to_all | solution.py:469
  175.5 2.7 %collective-permute-start.4 = (f32[64,1,128]{2,1,0:T(1,128)S(1)}, f32[64,1,128]{2,1,0:T(1,128)S(1)}, u32[]{:S(2)}, u32[]{:S(2)}) collective-permute-start(f32[64,1,128]{2,1,0:T(1,128)S(1)} %all_to_all.28.own_ref), channel_id=1, source_target_pairs={{0,1},{1,0},{2,3},{3,2},{4,5},{5,4},{6,7},{7,6},{8,9},{9,8},{10,11... | collective-permute-start | bytes 98312 | tf_op jit(solution)/shard_map/ppermute | solution.py:465
  178.2 1.9 %shard_map.113 = bf16[2,32,8,2048]{3,2,1,0:T(8,128)(2,1)S(1)} custom-call(s32[1]{0:T(128)} %bitcast.me_ref, s32[32]{0:T(128)S(1)} %copy-done.3, bf16[64,17,8,128]{3,2,1,0:T(8,128)(2,1)S(1)} %all_to_all.25.got_ref, bf16[64,4,8,128]{3,2,1,0:T(8,128)(2,1)} %collective-permute-done.5.keys_ref, bf16[64,4,8,128]{3,2,1,0:T(8,128)(2,1)} %collective-permute-done.6.values_ref, ...), custom_call_target="tpu_custom_call" | custom-call | tf_op jit(solution)/shard_map/pallas_call | solution.py:576
  180.1 1.3 copy.13
  181.5 0.8 shard_map.112
  (14 shorter events, 0.0 us)
Async XLA Ops:
  0.6 23.4 %collective-permute-start = (bf16[1,64,4608]{2,1,0:T(8,128)(2,1)}, bf16[1,64,4608]{2,1,0:T(8,128)(2,1)S(1)}, u32[]{:S(2)}, u32[]{:S(2)}) collective-permute-start(bf16[1,64,4608]{2,1,0:T(8,128)(2,1)} %weight_hbm.1), channel_id=1, source_target_pairs={{0,1},{1,0},{2,3},{3,2},{4,5},{5,4},{6,7},{7,6},{8,9},{9,8},{10,11... | collective-permute-start | bytes 1769480 | tf_op jit(solution)/shard_map/ppermute | solution.py:465
  24.8 61.1 %copy-start.3 = (s32[32]{0:T(128)S(1)}, s32[32]{0:T(128)}, u32[]{:S(2)}) copy-start(s32[32]{0:T(128)} %lengths_ref.3) | copy-start | bytes 388
  85.9 26.3 %copy-start.2 = (bf16[1,36,4096]{2,1,0:T(8,128)(2,1)S(1)}, bf16[1,36,4096]{2,1,0:T(8,128)(2,1)}, u32[]{:S(2)}) copy-start(bf16[1,36,4096]{2,1,0:T(8,128)(2,1)} %weight_ref.3) | copy-start | bytes 884740
  87.3 0.8 copy-start.4
  109.0 26.5 %copy-start = (bf16[1,2,144,4608]{3,2,1,0:T(8,128)(2,1)S(1)}, bf16[1,2,144,4608]{3,2,1,0:T(8,128)(2,1)}, u32[]{:S(2)}) copy-start(bf16[1,2,144,4608]{3,2,1,0:T(8,128)(2,1)} %gate_up_ref.1) | copy-start | bytes 7962628
  109.0 26.5 %copy-start.1 = (bf16[1,144,4608]{2,1,0:T(8,128)(2,1)S(1)}, bf16[1,144,4608]{2,1,0:T(8,128)(2,1)}, u32[]{:S(2)}) copy-start(bf16[1,144,4608]{2,1,0:T(8,128)(2,1)} %down_ref.1) | copy-start | bytes 3981316
  109.0 4.6 %collective-permute-start.1 = (bf16[64,16,128]{2,1,0:T(8,128)(2,1)S(1)}, bf16[64,16,128]{2,1,0:T(8,128)(2,1)S(1)}, u32[]{:S(2)}, u32[]{:S(2)}) collective-permute-start(bf16[64,16,128]{2,1,0:T(8,128)(2,1)S(1)} %all_to_all.26.own_ref.own_new_ref), channel_id=1, source_target_pairs={{0,1},{1,0},{2,3},{3,2},{4,5},{5,4},{6,7},{7,6},{8,9},{9,8},{10,11... | collective-permute-start | bytes 786440 | tf_op jit(solution)/shard_map/ppermute | solution.py:465
  112.7 0.8 copy-start.5
  131.9 3.6 %collective-permute-start.2 = (bf16[64,16,128]{2,1,0:T(8,128)(2,1)S(1)}, bf16[64,16,128]{2,1,0:T(8,128)(2,1)S(1)}, u32[]{:S(2)}, u32[]{:S(2)}) collective-permute-start(bf16[64,16,128]{2,1,0:T(8,128)(2,1)S(1)} %all_to_all.27.own_ref), channel_id=1, source_target_pairs={{0,1},{1,0},{2,3},{3,2},{4,5},{5,4},{6,7},{7,6},{8,9},{9,8},{10,11... | collective-permute-start | bytes 786440 | tf_op jit(solution)/shard_map/ppermute | solution.py:465
  137.4 1.7 collective-permute-start.3
  139.9 18.7 %all-to-all-start.3 = ((bf16[64,16,128]{2,1,0:T(8,128)(2,1)}), bf16[64,16,128]{2,1,0:T(8,128)(2,1)S(1)}, u32[]{:S(2)}, u32[]{:S(2)}) async-start(bf16[64,16,128]{2,1,0:T(8,128)(2,1)} %add_convert_fusion), calls=%async_computation.3 | async-start | bytes 524288 | tf_op jit(solution)/shard_map/all_to_all | solution.py:469
  146.5 31.7 %collective-permute-start.5 = (bf16[64,4,8,128]{3,2,1,0:T(8,128)(2,1)}, bf16[64,4,8,128]{3,2,1,0:T(8,128)(2,1)}, u32[]{:S(2)}, u32[]{:S(2)}) collective-permute-start(bf16[64,4,8,128]{3,2,1,0:T(8,128)(2,1)} %copy-done.4), channel_id=1, source_target_pairs={{0,1},{1,0},{2,3},{3,2},{4,5},{5,4},{6,7},{7,6},{8,9},{9,8},{10,11... | collective-permute-start | bytes 1572872 | tf_op jit(solution)/shard_map/ppermute | solution.py:465
  147.0 31.2 %collective-permute-start.6 = (bf16[64,4,8,128]{3,2,1,0:T(8,128)(2,1)}, bf16[64,4,8,128]{3,2,1,0:T(8,128)(2,1)}, u32[]{:S(2)}, u32[]{:S(2)}) collective-permute-start(bf16[64,4,8,128]{3,2,1,0:T(8,128)(2,1)} %copy-done.5), channel_id=1, source_target_pairs={{0,1},{1,0},{2,3},{3,2},{4,5},{5,4},{6,7},{7,6},{8,9},{9,8},{10,11... | collective-permute-start | bytes 1572872 | tf_op jit(solution)/shard_map/ppermute | solution.py:465
  175.5 5.9 %collective-permute-start.4 = (f32[64,1,128]{2,1,0:T(1,128)S(1)}, f32[64,1,128]{2,1,0:T(1,128)S(1)}, u32[]{:S(2)}, u32[]{:S(2)}) collective-permute-start(f32[64,1,128]{2,1,0:T(1,128)S(1)} %all_to_all.28.own_ref), channel_id=1, source_target_pairs={{0,1},{1,0},{2,3},{3,2},{4,5},{5,4},{6,7},{7,6},{8,9},{9,8},{10,11... | collective-permute-start | bytes 98312 | tf_op jit(solution)/shard_map/ppermute | solution.py:465

commit v7 on v6

--- a/solution.py
+++ b/solution.py
@@ -183,9 +183,7 @@
     copy.wait()
 
 
-def attend_kernel(me_ref, lengths_ref, got_ref, position_ref, cache_ref, out_ref, leaving_ref, sem):
-    leave = pltpu.make_async_copy(got_ref.at[:, pl.ds(PAGE_TILES, PAGE_TILES // 2)], leaving_ref, sem)
-    leave.start()
+def attend_kernel(me_ref, lengths_ref, got_ref, position_ref, cache_ref, out_ref):
     me = me_ref[0]
     group = me >> 3
     slot = me & 7
@@ -230,7 +228,6 @@
     attended = numerator / denominator
     payload = jnp.concatenate([attended, picked[24:32]], axis=0).astype(BF16)
     out_ref[...] = jnp.broadcast_to(payload[None], (CHIPS, 2 * ROWS, LANES))
-    leave.wait()
 
 
 def mixed_half(pieces, weight_ref, core, pick):
@@ -296,13 +293,17 @@
     return jnp.concatenate([low, pltpu.roll(high, LANES // 2, 1)], axis=0)
 
 
-def place_own_kernel(me_ref, own_ref, out_ref):
+def place_own_kernel(me_ref, own_ref, got_ref, out_ref, leaving_ref, sem):
+    leave = pltpu.make_async_copy(got_ref.at[:, pl.ds(PAGE_TILES, PAGE_TILES // 2)], leaving_ref, sem)
+    leave.start()
     for parity in range(2):
 
         @pl.when((me_ref[0] & 1) == parity)
         def _():
             for v in range(BLOCKS):
                 out_ref[v] = placed(own_ref, parity, v)
+
+    leave.wait()
 
 
 def ffn_kernel(
@@ -507,13 +508,9 @@
 def attend_call(me, lengths, got, position, cache):
     return call(
         attend_kernel,
-        (
-            pltpu.VMEM((CHIPS, 2 * ROWS, LANES), BF16),
-            pltpu.VMEM((CHIPS, PAGE_TILES // 2, ROWS, LANES), BF16),
-        ),
+        pltpu.VMEM((CHIPS, 2 * ROWS, LANES), BF16),
         [smem(), smem()] + [vmem()] * 3,
-        (vmem(), vmem()),
-        scratch_shapes=[pltpu.SemaphoreType.DMA],
+        vmem(),
     )(me, lengths, got, position, cache)
 
 
@@ -537,8 +534,17 @@
     )(me, other, weight, part, pick)
 
 
-def place_own_call(me, own):
-    return call(place_own_kernel, pltpu.VMEM((BLOCKS, BATCH, LANES), F32), [smem(), vmem()], vmem())(me, own)
+def place_own_call(me, own, got):
+    return call(
+        place_own_kernel,
+        (
+            pltpu.VMEM((BLOCKS, BATCH, LANES), F32),
+            pltpu.VMEM((CHIPS, PAGE_TILES // 2, ROWS, LANES), BF16),
+        ),
+        [smem(), vmem(), vmem()],
+        (vmem(), vmem()),
+        scratch_shapes=[pltpu.SemaphoreType.DMA],
+    )(me, own, got)
 
 
 def ffn_call(me, own, other, hidden, gains, gate_up, down):
@@ -574,7 +580,10 @@
 
 def decode_call(me, lengths, got, other_keys, other_values, own_new, other_new):
     return call(
-        decode_kernel, pltpu.VMEM((2, BATCH, ROWS, KV_HEADS * HEAD_DIM), BF16), [smem(), smem()] + [vmem()] * 5, vmem()
+        decode_kernel,
+        pltpu.VMEM((2, BATCH, ROWS, KV_HEADS * HEAD_DIM), BF16),
+        [smem(), smem()] + [vmem()] * 5,
+        vmem(),
     )(me, lengths, got, other_keys, other_values, own_new, other_new)
 
 
@@ -604,17 +613,15 @@
     cosine, sine = rope_tables(spread_length)
     buf = qkv_call(me, hidden, gains, own_rows, other_rows, cosine, sine, buf)
     got = to_chips(buf)
-    payload, leaving_keys = attend_call(
-        me, lengths, got, position, held.reshape(2, PER_GROUP, -1, 2 * HEAD_DIM)
-    )
+    payload = attend_call(me, lengths, got, position, held.reshape(2, PER_GROUP, -1, 2 * HEAD_DIM))
     own_att = to_chips(payload)
     other_att = core_swap(own_att)
-    other_keys = core_swap(leaving_keys)
     part, pick, leaving_values = mix_own_call(me, own_att, out_weight, got)
     payload = mix_call(me, other_att, out_weight, part, pick)
     own_mix = to_chips(payload)
     other_mix = core_swap(own_mix)
-    placed_mix = place_own_call(me, own_mix)
+    placed_mix, leaving_keys = place_own_call(me, own_mix, got)
+    other_keys = core_swap(leaving_keys)
     other_values = core_swap(leaving_values)
     keep, send, stream = ffn_call(me, placed_mix, other_mix, hidden, gains, gate_up_weight, down_weight)
     sent = core_swap(send)

time: 183 us -> 182 us (level)
  no operation moved by 1% of the time
where the time goes in v7:
time: 182 us
  blocking collectives  117 us (64%)
  starting transfers between devices  36.6 us (20%)
  waiting for transfers between devices  12.7 us (7%)
  Pallas kernels  11.1 us (6%)
  local copies, waits for them, and re-layouts  2.91 us (2%)
    all_to_all x4, blocking collectives, to_chips(): return lax.all_to_all(tiles, XY[::-1], 0, 0, tiled=True)  117 us
    ppermute x7, starting transfers between devices, core_swap(): return lax.ppermute(shard, 'tp_2', [(0, 1), (1, 0)])  30 us
    all_to_all x1, waiting for transfers between devices, to_chips(): return lax.all_to_all(tiles, XY[::-1], 0, 0, tiled=True)  11.4 us
    all_to_all x1, starting transfers between devices, to_chips(): return lax.all_to_all(tiles, XY[::-1], 0, 0, tiled=True)  6.65 us
  transfers between devices with their start and end apart: 8, of which 3 were waited for; matrix products, arithmetic and copies ran while one was open for 1% of the time, Pallas kernels for 3%

profile of v7, /device:TPU:513, one launch (start us, length us, event | category | flops | bytes accessed | tf_op | source)
XLA Modules:
  0.0 181.5 jit_solution(10160345768716682491)
XLA Ops:
  0.6 20.5 %collective-permute-start = (bf16[1,64,4608]{2,1,0:T(8,128)(2,1)}, bf16[1,64,4608]{2,1,0:T(8,128)(2,1)S(1)}, u32[]{:S(2)}, u32[]{:S(2)}) collective-permute-start(bf16[1,64,4608]{2,1,0:T(8,128)(2,1)} %weight_hbm.1), channel_id=1, source_target_pairs={{0,1},{1,0},{2,3},{3,2},{4,5},{5,4},{6,7},{7,6},{8,9},{9,8},{10,11... | collective-permute-start | bytes 1769480 | tf_op jit(solution)/shard_map/ppermute | solution.py:466
  21.2 2.8 %shard_map.104 = (bf16[64,17,8,128]{3,2,1,0:T(8,128)(2,1)S(1)}, bf16[2,2,128,8,256]{4,3,2,1,0:T(8,128)(2,1)S(1)}, bf16[1,64,4608]{2,1,0:T(8,128)(2,1)S(1)}, f32[...) custom-call(s32[1]{0:T(128)} %bitcast.me_ref, s32[32]{0:T(128)} %lengths_ref.3, ...), custom_call_target="tpu_custom_call" | custom-call | tf_op jit(solution)/shard_map/pallas_call | solution.py:475
  24.0 0.1 multiply_sine_fusion
  24.1 0.7 shard_map.105
  24.8 0.0 copy-start.3
  24.8 61.1 %all_to_all.25.got_ref = bf16[64,17,8,128]{3,2,1,0:T(8,128)(2,1)S(1)} all-to-all(bf16[64,17,8,128]{3,2,1,0:T(8,128)(2,1)S(1)} %shard_map.105), channel_id=1, replica_groups=mesh['grp'=2,'tp_0'=8,'tp_1'=8,'tp_2'=2] {'tp_1','tp_0'}, dimensions={0} | all-to-all | bytes 4456448 | tf_op jit(solution)/shard_map/all_to_all | solution.py:470
  85.9 1.3 shard_map.106
  87.2 20.9 %all_to_all.26.own_ref.own_new_ref = bf16[64,16,128]{2,1,0:T(8,128)(2,1)S(1)} all-to-all(bf16[64,16,128]{2,1,0:T(8,128)(2,1)S(1)} %shard_map.106), channel_id=1, replica_groups=mesh['grp'=2,'tp_0'=8,'tp_1'=8,'tp_2'=2] {'tp_1','tp_0'}, dimensions={0} | all-to-all | bytes 524288 | tf_op jit(solution)/shard_map/all_to_all | solution.py:470
  108.1 3.2 %collective-permute-start.1 = (bf16[64,16,128]{2,1,0:T(8,128)(2,1)S(1)}, bf16[64,16,128]{2,1,0:T(8,128)(2,1)S(1)}, u32[]{:S(2)}, u32[]{:S(2)}) collective-permute-start(bf16[64,16,128]{2,1,0:T(8,128)(2,1)S(1)} %all_to_all.26.own_ref.own_new_ref), channel_id=1, source_target_pairs={{0,1},{1,0},{2,3},{3,2},{4,5},{5,4},{6,7},{7,6},{8,9},{9,8},{10,11... | collective-permute-start | bytes 786440 | tf_op jit(solution)/shard_map/ppermute | solution.py:466
  111.3 0.6 shard_map.107
  111.9 0.8 copy-done.4
  112.7 0.6 shard_map.108
  113.3 17.9 %all_to_all.27.own_ref = bf16[64,16,128]{2,1,0:T(8,128)(2,1)S(1)} all-to-all(bf16[64,16,128]{2,1,0:T(8,128)(2,1)S(1)} %shard_map.108), channel_id=1, replica_groups=mesh['grp'=2,'tp_0'=8,'tp_1'=8,'tp_2'=2] {'tp_1','tp_0'}, dimensions={0} | all-to-all | bytes 524288 | tf_op jit(solution)/shard_map/all_to_all | solution.py:470
  131.2 2.4 %collective-permute-start.2 = (bf16[64,16,128]{2,1,0:T(8,128)(2,1)S(1)}, bf16[64,16,128]{2,1,0:T(8,128)(2,1)S(1)}, u32[]{:S(2)}, u32[]{:S(2)}) collective-permute-start(bf16[64,16,128]{2,1,0:T(8,128)(2,1)S(1)} %all_to_all.27.own_ref), channel_id=1, source_target_pairs={{0,1},{1,0},{2,3},{3,2},{4,5},{5,4},{6,7},{7,6},{8,9},{9,8},{10,11... | collective-permute-start | bytes 786440 | tf_op jit(solution)/shard_map/ppermute | solution.py:466
  133.6 0.2 shard_map.109
  133.8 0.0 copy-start.5
  133.8 0.8 copy-done.5
  134.6 0.1 collective-permute-done.2.other_ref
  134.8 2.0 %shard_map.110 = (bf16[64,16,128]{2,1,0:T(8,128)(2,1)S(1)}, bf16[64,16,128]{2,1,0:T(8,128)(2,1)S(1)}, f32[32,128]{1,0:T(8,128)S(1)}) custom-call(s32[1]{0:T(128)} %bitcast.me_ref, f32[36,32,128]{2,1,0:T(8,128)S(1)} %get-tuple-element.28.placed_ref, bf16[64,16,128]{2,1,0:T(8,128)(2,1)S(1)} %collective-permute-done.2.other_ref, ...), custom_call_target="tpu_custom_call" | custom-call | tf_op jit(solution)/shard_map/pallas_call | solution.py:552
  136.7 0.5 collective-permute-start.3
  137.2 1.2 collective-permute-done.3
  138.4 0.8 add_convert_fusion
  139.2 6.7 %all-to-all-start.3 = ((bf16[64,16,128]{2,1,0:T(8,128)(2,1)}), bf16[64,16,128]{2,1,0:T(8,128)(2,1)S(1)}, u32[]{:S(2)}, u32[]{:S(2)}) async-start(bf16[64,16,128]{2,1,0:T(8,128)(2,1)} %add_convert_fusion), calls=%async_computation.3 | async-start | bytes 524288 | tf_op jit(solution)/shard_map/all_to_all | solution.py:470
  145.8 0.5 collective-permute-start.6
  146.3 0.1 collective-permute-start.5
  146.5 11.4 %all-to-all-done.3.got_ref = bf16[64,16,128]{2,1,0:T(8,128)(2,1)S(1)} async-done(((bf16[64,16,128]{2,1,0:T(8,128)(2,1)}), bf16[64,16,128]{2,1,0:T(8,128)(2,1)S(1)}, u32[]{:S(2)}, u32[]{:S(2)}) %all-to-all-start.3) | async-done | bytes 262176 | tf_op jit(solution)/shard_map/all_to_all | solution.py:470
  157.8 0.3 shard_map.111
  158.1 16.7 %all_to_all.28.own_ref = f32[64,1,128]{2,1,0:T(1,128)S(1)} all-to-all(f32[64,1,128]{2,1,0:T(1,128)S(1)} %get-tuple-element.33), channel_id=1, replica_groups=mesh['grp'=2,'tp_0'=8,'tp_1'=8,'tp_2'=2] {'tp_1','tp_0'}, dimensions={0} | all-to-all | bytes 65536 | tf_op jit(solution)/shard_map/all_to_all | solution.py:470
  174.8 2.7 %collective-permute-start.4 = (f32[64,1,128]{2,1,0:T(1,128)S(1)}, f32[64,1,128]{2,1,0:T(1,128)S(1)}, u32[]{:S(2)}, u32[]{:S(2)}) collective-permute-start(f32[64,1,128]{2,1,0:T(1,128)S(1)} %all_to_all.28.own_ref), channel_id=1, source_target_pairs={{0,1},{1,0},{2,3},{3,2},{4,5},{5,4},{6,7},{7,6},{8,9},{9,8},{10,11... | collective-permute-start | bytes 98312 | tf_op jit(solution)/shard_map/ppermute | solution.py:466
  177.5 1.9 %shard_map.113 = bf16[2,32,8,2048]{3,2,1,0:T(8,128)(2,1)S(1)} custom-call(s32[1]{0:T(128)} %bitcast.me_ref, s32[32]{0:T(128)S(1)} %copy-done.3, bf16[64,17,8,128]{3,2,1,0:T(8,128)(2,1)S(1)} %all_to_all.25.got_ref, bf16[64,4,8,128]{3,2,1,0:T(8,128)(2,1)} %collective-permute-done.5.keys_ref, bf16[64,4,8,128]{3,2,1,0:T(8,128)(2,1)} %collective-permute-done.6.values_ref, ...), custom_call_target="tpu_custom_call" | custom-call | tf_op jit(solution)/shard_map/pallas_call | solution.py:582
  179.4 1.3 copy.13
  180.7 0.8 shard_map.112
  (14 shorter events, 0.0 us)
Async XLA Ops:
  0.6 23.4 %collective-permute-start = (bf16[1,64,4608]{2,1,0:T(8,128)(2,1)}, bf16[1,64,4608]{2,1,0:T(8,128)(2,1)S(1)}, u32[]{:S(2)}, u32[]{:S(2)}) collective-permute-start(bf16[1,64,4608]{2,1,0:T(8,128)(2,1)} %weight_hbm.1), channel_id=1, source_target_pairs={{0,1},{1,0},{2,3},{3,2},{4,5},{5,4},{6,7},{7,6},{8,9},{9,8},{10,11... | collective-permute-start | bytes 1769480 | tf_op jit(solution)/shard_map/ppermute | solution.py:466
  24.8 61.1 %copy-start.3 = (s32[32]{0:T(128)S(1)}, s32[32]{0:T(128)}, u32[]{:S(2)}) copy-start(s32[32]{0:T(128)} %lengths_ref.3) | copy-start | bytes 388
  85.9 25.4 %copy-start.2 = (bf16[1,36,4096]{2,1,0:T(8,128)(2,1)S(1)}, bf16[1,36,4096]{2,1,0:T(8,128)(2,1)}, u32[]{:S(2)}) copy-start(bf16[1,36,4096]{2,1,0:T(8,128)(2,1)} %weight_ref.3) | copy-start | bytes 884740
  108.1 4.6 %collective-permute-start.1 = (bf16[64,16,128]{2,1,0:T(8,128)(2,1)S(1)}, bf16[64,16,128]{2,1,0:T(8,128)(2,1)S(1)}, u32[]{:S(2)}, u32[]{:S(2)}) collective-permute-start(bf16[64,16,128]{2,1,0:T(8,128)(2,1)S(1)} %all_to_all.26.own_ref.own_new_ref), channel_id=1, source_target_pairs={{0,1},{1,0},{2,3},{3,2},{4,5},{5,4},{6,7},{7,6},{8,9},{9,8},{10,11... | collective-permute-start | bytes 786440 | tf_op jit(solution)/shard_map/ppermute | solution.py:466
  111.9 0.8 copy-start.4
  112.7 22.1 %copy-start = (bf16[1,2,144,4608]{3,2,1,0:T(8,128)(2,1)S(1)}, bf16[1,2,144,4608]{3,2,1,0:T(8,128)(2,1)}, u32[]{:S(2)}) copy-start(bf16[1,2,144,4608]{3,2,1,0:T(8,128)(2,1)} %gate_up_ref.1) | copy-start | bytes 7962628
  112.7 22.1 %copy-start.1 = (bf16[1,144,4608]{2,1,0:T(8,128)(2,1)S(1)}, bf16[1,144,4608]{2,1,0:T(8,128)(2,1)}, u32[]{:S(2)}) copy-start(bf16[1,144,4608]{2,1,0:T(8,128)(2,1)} %down_ref.1) | copy-start | bytes 3981316
  131.2 3.6 %collective-permute-start.2 = (bf16[64,16,128]{2,1,0:T(8,128)(2,1)S(1)}, bf16[64,16,128]{2,1,0:T(8,128)(2,1)S(1)}, u32[]{:S(2)}, u32[]{:S(2)}) collective-permute-start(bf16[64,16,128]{2,1,0:T(8,128)(2,1)S(1)} %all_to_all.27.own_ref), channel_id=1, source_target_pairs={{0,1},{1,0},{2,3},{3,2},{4,5},{5,4},{6,7},{7,6},{8,9},{9,8},{10,11... | collective-permute-start | bytes 786440 | tf_op jit(solution)/shard_map/ppermute | solution.py:466
  133.8 0.8 copy-start.5
  136.7 1.7 collective-permute-start.3
  139.2 18.7 %all-to-all-start.3 = ((bf16[64,16,128]{2,1,0:T(8,128)(2,1)}), bf16[64,16,128]{2,1,0:T(8,128)(2,1)S(1)}, u32[]{:S(2)}, u32[]{:S(2)}) async-start(bf16[64,16,128]{2,1,0:T(8,128)(2,1)} %add_convert_fusion), calls=%async_computation.3 | async-start | bytes 524288 | tf_op jit(solution)/shard_map/all_to_all | solution.py:470
  145.8 31.7 %collective-permute-start.6 = (bf16[64,4,8,128]{3,2,1,0:T(8,128)(2,1)}, bf16[64,4,8,128]{3,2,1,0:T(8,128)(2,1)}, u32[]{:S(2)}, u32[]{:S(2)}) collective-permute-start(bf16[64,4,8,128]{3,2,1,0:T(8,128)(2,1)} %copy-done.4), channel_id=1, source_target_pairs={{0,1},{1,0},{2,3},{3,2},{4,5},{5,4},{6,7},{7,6},{8,9},{9,8},{10,11... | collective-permute-start | bytes 1572872 | tf_op jit(solution)/shard_map/ppermute | solution.py:466
  146.3 31.2 %collective-permute-start.5 = (bf16[64,4,8,128]{3,2,1,0:T(8,128)(2,1)}, bf16[64,4,8,128]{3,2,1,0:T(8,128)(2,1)}, u32[]{:S(2)}, u32[]{:S(2)}) collective-permute-start(bf16[64,4,8,128]{3,2,1,0:T(8,128)(2,1)} %copy-done.5), channel_id=1, source_target_pairs={{0,1},{1,0},{2,3},{3,2},{4,5},{5,4},{6,7},{7,6},{8,9},{9,8},{10,11... | collective-permute-start | bytes 1572872 | tf_op jit(solution)/shard_map/ppermute | solution.py:466
  174.8 5.9 %collective-permute-start.4 = (f32[64,1,128]{2,1,0:T(1,128)S(1)}, f32[64,1,128]{2,1,0:T(1,128)S(1)}, u32[]{:S(2)}, u32[]{:S(2)}) collective-permute-start(f32[64,1,128]{2,1,0:T(1,128)S(1)} %all_to_all.28.own_ref), channel_id=1, source_target_pairs={{0,1},{1,0},{2,3},{3,2},{4,5},{5,4},{6,7},{7,6},{8,9},{9,8},{10,11... | collective-permute-start | bytes 98312 | tf_op jit(solution)/shard_map/ppermute | solution.py:466

commit v8 on v7

--- a/solution.py
+++ b/solution.py
@@ -205,26 +205,19 @@
     q = picked[0:8]
     new_k = picked[8:16]
     new_v = picked[16:24]
-    q16 = q.astype(BF16)
     scale = (D / HEADS) ** (-0.5)
     row = iota((ROWS, 1), 0)
-    scores = jnp.zeros((ROWS, 8 * 2 * CHIPS), F32)
-    for ee in range(PER_GROUP):
-        for a in range(2):
-            keys = cache_ref[0, ee, :, a * LANES : a * LANES + LANES]
-            part = nt_dot(q16, keys)
-            scores = jnp.where(((row & 1) == ee) & ((row >> 2) == a), part, scores)
+    both = jnp.concatenate([jnp.where(row < 4, q, 0.0), jnp.where(row < 4, 0.0, q)], axis=1).astype(BF16)
+    even = (row & 1) == 0
+    scores = jnp.where(even, nt_dot(both, cache_ref[0, 0]), nt_dot(both, cache_ref[0, 1]))
     limit = jnp.where((row & 1) == 0, lengths_ref[group * PER_GROUP], lengths_ref[group * PER_GROUP + 1])
     weights = jnp.where(position_ref[...] < limit, jnp.exp(capped(scores * scale)), 0.0)
     own = jnp.exp(capped(jnp.sum(q * new_k, axis=-1, keepdims=True) * scale))
     denominator = jnp.sum(weights, axis=-1, keepdims=True) + own
     w16 = weights.astype(BF16)
-    numerator = own.astype(BF16).astype(F32) * new_v
-    for ee in range(PER_GROUP):
-        for a in range(2):
-            values = cache_ref[1, ee, :, a * LANES : a * LANES + LANES]
-            part = nn_dot(w16, values)
-            numerator = numerator + jnp.where(((row & 1) == ee) & ((row >> 2) == a), part, 0.0)
+    taken = jnp.where(even, nn_dot(w16, cache_ref[1, 0]), nn_dot(w16, cache_ref[1, 1]))
+    taken = jnp.where(row < 4, taken[:, :LANES], taken[:, LANES:])
+    numerator = own.astype(BF16).astype(F32) * new_v + taken
     attended = numerator / denominator
     payload = jnp.concatenate([attended, picked[24:32]], axis=0).astype(BF16)
     out_ref[...] = jnp.broadcast_to(payload[None], (CHIPS, 2 * ROWS, LANES))
@@ -350,10 +343,12 @@
     gate = nt_dot(ffn_in, gate_up_ref[0, 0])
     up = nt_dot(ffn_in, gate_up_ref[0, 1])
     active = (jax.nn.gelu(gate, approximate=True) * up).astype(BF16)
-    for v in range(BLOCKS):
-        block = nn_dot(active, down_ref[0, :, LANES * v : LANES * v + LANES])
-        low_ref[v] = block[:HALF]
-        high_ref[v] = pltpu.roll(block[HALF:], LANES // 2, 1)
+    for w in range(BLOCKS // 2):
+        pair = nn_dot(active, down_ref[0, :, 2 * LANES * w : 2 * LANES * w + 2 * LANES])
+        for side in range(2):
+            block = pair[:, LANES * side : LANES * side + LANES]
+            low_ref[2 * w + side] = block[:HALF]
+            high_ref[2 * w + side] = pltpu.roll(block[HALF:], LANES // 2, 1)
     for p in range(CHIPS):
         even = window(low_ref, high_ref, 2 * p)
         odd = window(low_ref, high_ref, 2 * p + 1)
@@ -507,10 +502,7 @@
 
 def attend_call(me, lengths, got, position, cache):
     return call(
-        attend_kernel,
-        pltpu.VMEM((CHIPS, 2 * ROWS, LANES), BF16),
-        [smem(), smem()] + [vmem()] * 3,
-        vmem(),
+        attend_kernel, pltpu.VMEM((CHIPS, 2 * ROWS, LANES), BF16), [smem(), smem()] + [vmem()] * 3, vmem()
     )(me, lengths, got, position, cache)
 
 
@@ -580,10 +572,7 @@
 
 def decode_call(me, lengths, got, other_keys, other_values, own_new, other_new):
     return call(
-        decode_kernel,
-        pltpu.VMEM((2, BATCH, ROWS, KV_HEADS * HEAD_DIM), BF16),
-        [smem(), smem()] + [vmem()] * 5,
-        vmem(),
+        decode_kernel, pltpu.VMEM((2, BATCH, ROWS, KV_HEADS * HEAD_DIM), BF16), [smem(), smem()] + [vmem()] * 5, vmem()
     )(me, lengths, got, other_keys, other_values, own_new, other_new)
 
 
@@ -613,7 +602,9 @@
     cosine, sine = rope_tables(spread_length)
     buf = qkv_call(me, hidden, gains, own_rows, other_rows, cosine, sine, buf)
     got = to_chips(buf)
-    payload = attend_call(me, lengths, got, position, held.reshape(2, PER_GROUP, -1, 2 * HEAD_DIM))
+    payload = attend_call(
+        me, lengths, got, position, held.reshape(2, PER_GROUP, -1, 2 * HEAD_DIM)
+    )
     own_att = to_chips(payload)
     other_att = core_swap(own_att)
     part, pick, leaving_values = mix_own_call(me, own_att, out_weight, got)

time: 182 us -> 182 us (level)
  no operation moved by 1% of the time
where the time goes in v8:
time: 182 us; the launch traced here: 181 us
  blocking collectives  117 us (64%)
  starting transfers between devices  36.6 us (20%)
  waiting for transfers between devices  12.7 us (7%)
  Pallas kernels  10.9 us (6%)
  local copies, waits for them, and re-layouts  2.91 us (2%)
    all_to_all x4, blocking collectives, to_chips(): return lax.all_to_all(tiles, XY[::-1], 0, 0, tiled=True)  117 us
    ppermute x7, starting transfers between devices, core_swap(): return lax.ppermute(shard, 'tp_2', [(0, 1), (1, 0)])  30 us
    all_to_all x1, waiting for transfers between devices, to_chips(): return lax.all_to_all(tiles, XY[::-1], 0, 0, tiled=True)  11.4 us
    all_to_all x1, starting transfers between devices, to_chips(): return lax.all_to_all(tiles, XY[::-1], 0, 0, tiled=True)  6.65 us
  transfers between devices with their start and end apart: 8, of which 3 were waited for; matrix products, arithmetic and copies ran while one was open for 1% of the time, Pallas kernels for 3%

profile of v8, /device:TPU:513, one launch (start us, length us, event | category | flops | bytes accessed | tf_op | source)
XLA Modules:
  0.0 181.3 jit_solution(4878680851165570848)
XLA Ops:
  0.6 20.5 %collective-permute-start = (bf16[1,64,4608]{2,1,0:T(8,128)(2,1)}, bf16[1,64,4608]{2,1,0:T(8,128)(2,1)S(1)}, u32[]{:S(2)}, u32[]{:S(2)}) collective-permute-start(bf16[1,64,4608]{2,1,0:T(8,128)(2,1)} %weight_hbm.1), channel_id=1, source_target_pairs={{0,1},{1,0},{2,3},{3,2},{4,5},{5,4},{6,7},{7,6},{8,9},{9,8},{10,11... | collective-permute-start | bytes 1769480 | tf_op jit(solution)/shard_map/ppermute | solution.py:461
  21.2 2.8 %shard_map.104 = (bf16[64,17,8,128]{3,2,1,0:T(8,128)(2,1)S(1)}, bf16[2,2,128,8,256]{4,3,2,1,0:T(8,128)(2,1)S(1)}, bf16[1,64,4608]{2,1,0:T(8,128)(2,1)S(1)}, f32[...) custom-call(s32[1]{0:T(128)} %bitcast.me_ref, s32[32]{0:T(128)} %lengths_ref.3, ...), custom_call_target="tpu_custom_call" | custom-call | tf_op jit(solution)/shard_map/pallas_call | solution.py:470
  24.0 0.1 multiply_sine_fusion
  24.1 0.7 shard_map.105
  24.8 0.0 copy-start.3
  24.8 61.1 %all_to_all.25.got_ref = bf16[64,17,8,128]{3,2,1,0:T(8,128)(2,1)S(1)} all-to-all(bf16[64,17,8,128]{3,2,1,0:T(8,128)(2,1)S(1)} %shard_map.105), channel_id=1, replica_groups=mesh['grp'=2,'tp_0'=8,'tp_1'=8,'tp_2'=2] {'tp_1','tp_0'}, dimensions={0} | all-to-all | bytes 4456448 | tf_op jit(solution)/shard_map/all_to_all | solution.py:465
  85.9 1.2 shard_map.106
  87.1 20.9 %all_to_all.26.own_ref.own_new_ref = bf16[64,16,128]{2,1,0:T(8,128)(2,1)S(1)} all-to-all(bf16[64,16,128]{2,1,0:T(8,128)(2,1)S(1)} %shard_map.106), channel_id=1, replica_groups=mesh['grp'=2,'tp_0'=8,'tp_1'=8,'tp_2'=2] {'tp_1','tp_0'}, dimensions={0} | all-to-all | bytes 524288 | tf_op jit(solution)/shard_map/all_to_all | solution.py:465
  108.0 3.2 %collective-permute-start.1 = (bf16[64,16,128]{2,1,0:T(8,128)(2,1)S(1)}, bf16[64,16,128]{2,1,0:T(8,128)(2,1)S(1)}, u32[]{:S(2)}, u32[]{:S(2)}) collective-permute-start(bf16[64,16,128]{2,1,0:T(8,128)(2,1)S(1)} %all_to_all.26.own_ref.own_new_ref), channel_id=1, source_target_pairs={{0,1},{1,0},{2,3},{3,2},{4,5},{5,4},{6,7},{7,6},{8,9},{9,8},{10,11... | collective-permute-start | bytes 786440 | tf_op jit(solution)/shard_map/ppermute | solution.py:461
  111.2 0.6 shard_map.107
  111.8 0.8 copy-done.4
  112.6 0.6 shard_map.108
  113.2 17.9 %all_to_all.27.own_ref = bf16[64,16,128]{2,1,0:T(8,128)(2,1)S(1)} all-to-all(bf16[64,16,128]{2,1,0:T(8,128)(2,1)S(1)} %shard_map.108), channel_id=1, replica_groups=mesh['grp'=2,'tp_0'=8,'tp_1'=8,'tp_2'=2] {'tp_1','tp_0'}, dimensions={0} | all-to-all | bytes 524288 | tf_op jit(solution)/shard_map/all_to_all | solution.py:465
  131.1 2.4 %collective-permute-start.2 = (bf16[64,16,128]{2,1,0:T(8,128)(2,1)S(1)}, bf16[64,16,128]{2,1,0:T(8,128)(2,1)S(1)}, u32[]{:S(2)}, u32[]{:S(2)}) collective-permute-start(bf16[64,16,128]{2,1,0:T(8,128)(2,1)S(1)} %all_to_all.27.own_ref), channel_id=1, source_target_pairs={{0,1},{1,0},{2,3},{3,2},{4,5},{5,4},{6,7},{7,6},{8,9},{9,8},{10,11... | collective-permute-start | bytes 786440 | tf_op jit(solution)/shard_map/ppermute | solution.py:461
  133.5 0.2 shard_map.109
  133.7 0.0 copy-start.5
  133.7 0.8 copy-done.5
  134.5 0.1 collective-permute-done.2.other_ref
  134.7 1.8 shard_map.110
  136.5 0.5 collective-permute-start.3
  137.0 1.2 collective-permute-done.3
  138.1 0.8 add_convert_fusion
  138.9 6.7 %all-to-all-start.3 = ((bf16[64,16,128]{2,1,0:T(8,128)(2,1)}), bf16[64,16,128]{2,1,0:T(8,128)(2,1)S(1)}, u32[]{:S(2)}, u32[]{:S(2)}) async-start(bf16[64,16,128]{2,1,0:T(8,128)(2,1)} %add_convert_fusion), calls=%async_computation.3 | async-start | bytes 524288 | tf_op jit(solution)/shard_map/all_to_all | solution.py:465
  145.6 0.5 collective-permute-start.6
  146.1 0.1 collective-permute-start.5
  146.2 11.4 %all-to-all-done.3.got_ref = bf16[64,16,128]{2,1,0:T(8,128)(2,1)S(1)} async-done(((bf16[64,16,128]{2,1,0:T(8,128)(2,1)}), bf16[64,16,128]{2,1,0:T(8,128)(2,1)S(1)}, u32[]{:S(2)}, u32[]{:S(2)}) %all-to-all-start.3) | async-done | bytes 262176 | tf_op jit(solution)/shard_map/all_to_all | solution.py:465
  157.6 0.3 shard_map.111
  157.9 16.7 %all_to_all.28.own_ref = f32[64,1,128]{2,1,0:T(1,128)S(1)} all-to-all(f32[64,1,128]{2,1,0:T(1,128)S(1)} %get-tuple-element.33), channel_id=1, replica_groups=mesh['grp'=2,'tp_0'=8,'tp_1'=8,'tp_2'=2] {'tp_1','tp_0'}, dimensions={0} | all-to-all | bytes 65536 | tf_op jit(solution)/shard_map/all_to_all | solution.py:465
  174.6 2.7 %collective-permute-start.4 = (f32[64,1,128]{2,1,0:T(1,128)S(1)}, f32[64,1,128]{2,1,0:T(1,128)S(1)}, u32[]{:S(2)}, u32[]{:S(2)}) collective-permute-start(f32[64,1,128]{2,1,0:T(1,128)S(1)} %all_to_all.28.own_ref), channel_id=1, source_target_pairs={{0,1},{1,0},{2,3},{3,2},{4,5},{5,4},{6,7},{7,6},{8,9},{9,8},{10,11... | collective-permute-start | bytes 98312 | tf_op jit(solution)/shard_map/ppermute | solution.py:461
  177.2 1.9 %shard_map.113 = bf16[2,32,8,2048]{3,2,1,0:T(8,128)(2,1)S(1)} custom-call(s32[1]{0:T(128)} %bitcast.me_ref, s32[32]{0:T(128)S(1)} %copy-done.3, bf16[64,17,8,128]{3,2,1,0:T(8,128)(2,1)S(1)} %all_to_all.25.got_ref, bf16[64,4,8,128]{3,2,1,0:T(8,128)(2,1)} %collective-permute-done.5.keys_ref, bf16[64,4,8,128]{3,2,1,0:T(8,128)(2,1)} %collective-permute-done.6.values_ref, ...), custom_call_target="tpu_custom_call" | custom-call | tf_op jit(solution)/shard_map/pallas_call | solution.py:574
  179.2 1.3 copy.13
  180.5 0.8 shard_map.112
  (14 shorter events, 0.0 us)
Async XLA Ops:
  0.6 23.4 %collective-permute-start = (bf16[1,64,4608]{2,1,0:T(8,128)(2,1)}, bf16[1,64,4608]{2,1,0:T(8,128)(2,1)S(1)}, u32[]{:S(2)}, u32[]{:S(2)}) collective-permute-start(bf16[1,64,4608]{2,1,0:T(8,128)(2,1)} %weight_hbm.1), channel_id=1, source_target_pairs={{0,1},{1,0},{2,3},{3,2},{4,5},{5,4},{6,7},{7,6},{8,9},{9,8},{10,11... | collective-permute-start | bytes 1769480 | tf_op jit(solution)/shard_map/ppermute | solution.py:461
  24.8 61.1 %copy-start.3 = (s32[32]{0:T(128)S(1)}, s32[32]{0:T(128)}, u32[]{:S(2)}) copy-start(s32[32]{0:T(128)} %lengths_ref.3) | copy-start | bytes 388
  85.9 25.3 %copy-start.2 = (bf16[1,36,4096]{2,1,0:T(8,128)(2,1)S(1)}, bf16[1,36,4096]{2,1,0:T(8,128)(2,1)}, u32[]{:S(2)}) copy-start(bf16[1,36,4096]{2,1,0:T(8,128)(2,1)} %weight_ref.3) | copy-start | bytes 884740
  108.0 4.6 %collective-permute-start.1 = (bf16[64,16,128]{2,1,0:T(8,128)(2,1)S(1)}, bf16[64,16,128]{2,1,0:T(8,128)(2,1)S(1)}, u32[]{:S(2)}, u32[]{:S(2)}) collective-permute-start(bf16[64,16,128]{2,1,0:T(8,128)(2,1)S(1)} %all_to_all.26.own_ref.own_new_ref), channel_id=1, source_target_pairs={{0,1},{1,0},{2,3},{3,2},{4,5},{5,4},{6,7},{7,6},{8,9},{9,8},{10,11... | collective-permute-start | bytes 786440 | tf_op jit(solution)/shard_map/ppermute | solution.py:461
  111.8 0.8 copy-start.4
  112.6 22.1 %copy-start = (bf16[1,2,144,4608]{3,2,1,0:T(8,128)(2,1)S(1)}, bf16[1,2,144,4608]{3,2,1,0:T(8,128)(2,1)}, u32[]{:S(2)}) copy-start(bf16[1,2,144,4608]{3,2,1,0:T(8,128)(2,1)} %gate_up_ref.1) | copy-start | bytes 7962628
  112.6 22.1 %copy-start.1 = (bf16[1,144,4608]{2,1,0:T(8,128)(2,1)S(1)}, bf16[1,144,4608]{2,1,0:T(8,128)(2,1)}, u32[]{:S(2)}) copy-start(bf16[1,144,4608]{2,1,0:T(8,128)(2,1)} %down_ref.1) | copy-start | bytes 3981316
  131.1 3.6 %collective-permute-start.2 = (bf16[64,16,128]{2,1,0:T(8,128)(2,1)S(1)}, bf16[64,16,128]{2,1,0:T(8,128)(2,1)S(1)}, u32[]{:S(2)}, u32[]{:S(2)}) collective-permute-start(bf16[64,16,128]{2,1,0:T(8,128)(2,1)S(1)} %all_to_all.27.own_ref), channel_id=1, source_target_pairs={{0,1},{1,0},{2,3},{3,2},{4,5},{5,4},{6,7},{7,6},{8,9},{9,8},{10,11... | collective-permute-start | bytes 786440 | tf_op jit(solution)/shard_map/ppermute | solution.py:461
  133.7 0.8 copy-start.5
  136.5 1.7 collective-permute-start.3
  138.9 18.7 %all-to-all-start.3 = ((bf16[64,16,128]{2,1,0:T(8,128)(2,1)}), bf16[64,16,128]{2,1,0:T(8,128)(2,1)S(1)}, u32[]{:S(2)}, u32[]{:S(2)}) async-start(bf16[64,16,128]{2,1,0:T(8,128)(2,1)} %add_convert_fusion), calls=%async_computation.3 | async-start | bytes 524288 | tf_op jit(solution)/shard_map/all_to_all | solution.py:465
  145.6 31.7 %collective-permute-start.6 = (bf16[64,4,8,128]{3,2,1,0:T(8,128)(2,1)}, bf16[64,4,8,128]{3,2,1,0:T(8,128)(2,1)}, u32[]{:S(2)}, u32[]{:S(2)}) collective-permute-start(bf16[64,4,8,128]{3,2,1,0:T(8,128)(2,1)} %copy-done.4), channel_id=1, source_target_pairs={{0,1},{1,0},{2,3},{3,2},{4,5},{5,4},{6,7},{7,6},{8,9},{9,8},{10,11... | collective-permute-start | bytes 1572872 | tf_op jit(solution)/shard_map/ppermute | solution.py:461
  146.1 31.2 %collective-permute-start.5 = (bf16[64,4,8,128]{3,2,1,0:T(8,128)(2,1)}, bf16[64,4,8,128]{3,2,1,0:T(8,128)(2,1)}, u32[]{:S(2)}, u32[]{:S(2)}) collective-permute-start(bf16[64,4,8,128]{3,2,1,0:T(8,128)(2,1)} %copy-done.5), channel_id=1, source_target_pairs={{0,1},{1,0},{2,3},{3,2},{4,5},{5,4},{6,7},{7,6},{8,9},{9,8},{10,11... | collective-permute-start | bytes 1572872 | tf_op jit(solution)/shard_map/ppermute | solution.py:461
  174.6 5.9 %collective-permute-start.4 = (f32[64,1,128]{2,1,0:T(1,128)S(1)}, f32[64,1,128]{2,1,0:T(1,128)S(1)}, u32[]{:S(2)}, u32[]{:S(2)}) collective-permute-start(f32[64,1,128]{2,1,0:T(1,128)S(1)} %all_to_all.28.own_ref), channel_id=1, source_target_pairs={{0,1},{1,0},{2,3},{3,2},{4,5},{5,4},{6,7},{7,6},{8,9},{9,8},{10,11... | collective-permute-start | bytes 98312 | tf_op jit(solution)/shard_map/ppermute | solution.py:461

commit v9 on v8

--- a/solution.py
+++ b/solution.py
@@ -316,7 +316,6 @@
     ffn_ref,
 ):
     me = me_ref[0]
-    first = (me & 1) == 0
     lane = iota((BATCH, LANES), 1)
     for parity in range(2):
 
@@ -349,11 +348,14 @@
             block = pair[:, LANES * side : LANES * side + LANES]
             low_ref[2 * w + side] = block[:HALF]
             high_ref[2 * w + side] = pltpu.roll(block[HALF:], LANES // 2, 1)
-    for p in range(CHIPS):
-        even = window(low_ref, high_ref, 2 * p)
-        odd = window(low_ref, high_ref, 2 * p + 1)
-        keep_ref[place_of(p)] = jnp.where(first, even, odd).astype(BF16)
-        send_ref[place_of(p)] = jnp.where(first, odd, even).astype(BF16)
+    for core in range(2):
+
+        @pl.when((me & 1) == core)
+        def _():
+            for p in range(CHIPS):
+                keep_ref[place_of(p)] = window(low_ref, high_ref, 2 * p + core).astype(BF16)
+                send_ref[place_of(p)] = window(low_ref, high_ref, 2 * p + 1 - core).astype(BF16)
+
     start = me * SHARE
     at = start // LANES
     off = start % LANES

time: 182 us -> 182 us (level)
  no operation moved by 1% of the time
where the time goes in v9:
time: 182 us; the launch traced here: 181 us
  blocking collectives  117 us (64%)
  starting transfers between devices  36.6 us (20%)
  waiting for transfers between devices  12.7 us (7%)
  Pallas kernels  11 us (6%)
  local copies, waits for them, and re-layouts  2.91 us (2%)
    all_to_all x4, blocking collectives, to_chips(): return lax.all_to_all(tiles, XY[::-1], 0, 0, tiled=True)  117 us
    ppermute x7, starting transfers between devices, core_swap(): return lax.ppermute(shard, 'tp_2', [(0, 1), (1, 0)])  30 us
    all_to_all x1, waiting for transfers between devices, to_chips(): return lax.all_to_all(tiles, XY[::-1], 0, 0, tiled=True)  11.4 us
    all_to_all x1, starting transfers between devices, to_chips(): return lax.all_to_all(tiles, XY[::-1], 0, 0, tiled=True)  6.65 us
  transfers between devices with their start and end apart: 8, of which 3 were waited for; matrix products, arithmetic and copies ran while one was open for 1% of the time, Pallas kernels for 3%

profile of v9, /device:TPU:513, one launch (start us, length us, event | category | flops | bytes accessed | tf_op | source)
XLA Modules:
  0.0 181.4 jit_solution(16568890492578086474)
XLA Ops:
  0.6 20.5 %collective-permute-start = (bf16[1,64,4608]{2,1,0:T(8,128)(2,1)}, bf16[1,64,4608]{2,1,0:T(8,128)(2,1)S(1)}, u32[]{:S(2)}, u32[]{:S(2)}) collective-permute-start(bf16[1,64,4608]{2,1,0:T(8,128)(2,1)} %weight_hbm.1), channel_id=1, source_target_pairs={{0,1},{1,0},{2,3},{3,2},{4,5},{5,4},{6,7},{7,6},{8,9},{9,8},{10,11... | collective-permute-start | bytes 1769480 | tf_op jit(solution)/shard_map/ppermute | solution.py:463
  21.2 2.8 %shard_map.104 = (bf16[64,17,8,128]{3,2,1,0:T(8,128)(2,1)S(1)}, bf16[2,2,128,8,256]{4,3,2,1,0:T(8,128)(2,1)S(1)}, bf16[1,64,4608]{2,1,0:T(8,128)(2,1)S(1)}, f32[...) custom-call(s32[1]{0:T(128)} %bitcast.me_ref, s32[32]{0:T(128)} %lengths_ref.3, ...), custom_call_target="tpu_custom_call" | custom-call | tf_op jit(solution)/shard_map/pallas_call | solution.py:472
  24.0 0.1 multiply_sine_fusion
  24.1 0.7 shard_map.105
  24.8 0.0 copy-start.3
  24.8 61.1 %all_to_all.25.got_ref = bf16[64,17,8,128]{3,2,1,0:T(8,128)(2,1)S(1)} all-to-all(bf16[64,17,8,128]{3,2,1,0:T(8,128)(2,1)S(1)} %shard_map.105), channel_id=1, replica_groups=mesh['grp'=2,'tp_0'=8,'tp_1'=8,'tp_2'=2] {'tp_1','tp_0'}, dimensions={0} | all-to-all | bytes 4456448 | tf_op jit(solution)/shard_map/all_to_all | solution.py:467
  85.9 1.2 shard_map.106
  87.1 20.9 %all_to_all.26.own_ref.own_new_ref = bf16[64,16,128]{2,1,0:T(8,128)(2,1)S(1)} all-to-all(bf16[64,16,128]{2,1,0:T(8,128)(2,1)S(1)} %shard_map.106), channel_id=1, replica_groups=mesh['grp'=2,'tp_0'=8,'tp_1'=8,'tp_2'=2] {'tp_1','tp_0'}, dimensions={0} | all-to-all | bytes 524288 | tf_op jit(solution)/shard_map/all_to_all | solution.py:467
  108.0 3.2 %collective-permute-start.1 = (bf16[64,16,128]{2,1,0:T(8,128)(2,1)S(1)}, bf16[64,16,128]{2,1,0:T(8,128)(2,1)S(1)}, u32[]{:S(2)}, u32[]{:S(2)}) collective-permute-start(bf16[64,16,128]{2,1,0:T(8,128)(2,1)S(1)} %all_to_all.26.own_ref.own_new_ref), channel_id=1, source_target_pairs={{0,1},{1,0},{2,3},{3,2},{4,5},{5,4},{6,7},{7,6},{8,9},{9,8},{10,11... | collective-permute-start | bytes 786440 | tf_op jit(solution)/shard_map/ppermute | solution.py:463
  111.2 0.6 shard_map.107
  111.8 0.8 copy-done.4
  112.6 0.6 shard_map.108
  113.2 17.9 %all_to_all.27.own_ref = bf16[64,16,128]{2,1,0:T(8,128)(2,1)S(1)} all-to-all(bf16[64,16,128]{2,1,0:T(8,128)(2,1)S(1)} %shard_map.108), channel_id=1, replica_groups=mesh['grp'=2,'tp_0'=8,'tp_1'=8,'tp_2'=2] {'tp_1','tp_0'}, dimensions={0} | all-to-all | bytes 524288 | tf_op jit(solution)/shard_map/all_to_all | solution.py:467
  131.1 2.4 %collective-permute-start.2 = (bf16[64,16,128]{2,1,0:T(8,128)(2,1)S(1)}, bf16[64,16,128]{2,1,0:T(8,128)(2,1)S(1)}, u32[]{:S(2)}, u32[]{:S(2)}) collective-permute-start(bf16[64,16,128]{2,1,0:T(8,128)(2,1)S(1)} %all_to_all.27.own_ref), channel_id=1, source_target_pairs={{0,1},{1,0},{2,3},{3,2},{4,5},{5,4},{6,7},{7,6},{8,9},{9,8},{10,11... | collective-permute-start | bytes 786440 | tf_op jit(solution)/shard_map/ppermute | solution.py:463
  133.5 0.2 shard_map.109
  133.7 0.0 copy-start.5
  133.7 0.8 copy-done.5
  134.5 0.1 collective-permute-done.2.other_ref
  134.7 1.9 %shard_map.110 = (bf16[64,16,128]{2,1,0:T(8,128)(2,1)S(1)}, bf16[64,16,128]{2,1,0:T(8,128)(2,1)S(1)}, f32[32,128]{1,0:T(8,128)S(1)}) custom-call(s32[1]{0:T(128)} %bitcast.me_ref, f32[36,32,128]{2,1,0:T(8,128)S(1)} %get-tuple-element.28.placed_ref, bf16[64,16,128]{2,1,0:T(8,128)(2,1)S(1)} %collective-permute-done.2.other_ref, ...), custom_call_target="tpu_custom_call" | custom-call | tf_op jit(solution)/shard_map/pallas_call | solution.py:546
  136.6 0.5 collective-permute-start.3
  137.1 1.2 collective-permute-done.3
  138.3 0.8 add_convert_fusion
  139.0 6.7 %all-to-all-start.3 = ((bf16[64,16,128]{2,1,0:T(8,128)(2,1)}), bf16[64,16,128]{2,1,0:T(8,128)(2,1)S(1)}, u32[]{:S(2)}, u32[]{:S(2)}) async-start(bf16[64,16,128]{2,1,0:T(8,128)(2,1)} %add_convert_fusion), calls=%async_computation.3 | async-start | bytes 524288 | tf_op jit(solution)/shard_map/all_to_all | solution.py:467
  145.7 0.5 collective-permute-start.6
  146.2 0.1 collective-permute-start.5
  146.3 11.4 %all-to-all-done.3.got_ref = bf16[64,16,128]{2,1,0:T(8,128)(2,1)S(1)} async-done(((bf16[64,16,128]{2,1,0:T(8,128)(2,1)}), bf16[64,16,128]{2,1,0:T(8,128)(2,1)S(1)}, u32[]{:S(2)}, u32[]{:S(2)}) %all-to-all-start.3) | async-done | bytes 262176 | tf_op jit(solution)/shard_map/all_to_all | solution.py:467
  157.7 0.3 shard_map.111
  158.0 16.7 %all_to_all.28.own_ref = f32[64,1,128]{2,1,0:T(1,128)S(1)} all-to-all(f32[64,1,128]{2,1,0:T(1,128)S(1)} %get-tuple-element.33), channel_id=1, replica_groups=mesh['grp'=2,'tp_0'=8,'tp_1'=8,'tp_2'=2] {'tp_1','tp_0'}, dimensions={0} | all-to-all | bytes 65536 | tf_op jit(solution)/shard_map/all_to_all | solution.py:467
  174.7 2.7 %collective-permute-start.4 = (f32[64,1,128]{2,1,0:T(1,128)S(1)}, f32[64,1,128]{2,1,0:T(1,128)S(1)}, u32[]{:S(2)}, u32[]{:S(2)}) collective-permute-start(f32[64,1,128]{2,1,0:T(1,128)S(1)} %all_to_all.28.own_ref), channel_id=1, source_target_pairs={{0,1},{1,0},{2,3},{3,2},{4,5},{5,4},{6,7},{7,6},{8,9},{9,8},{10,11... | collective-permute-start | bytes 98312 | tf_op jit(solution)/shard_map/ppermute | solution.py:463
  177.4 1.9 %shard_map.113 = bf16[2,32,8,2048]{3,2,1,0:T(8,128)(2,1)S(1)} custom-call(s32[1]{0:T(128)} %bitcast.me_ref, s32[32]{0:T(128)S(1)} %copy-done.3, bf16[64,17,8,128]{3,2,1,0:T(8,128)(2,1)S(1)} %all_to_all.25.got_ref, bf16[64,4,8,128]{3,2,1,0:T(8,128)(2,1)} %collective-permute-done.5.keys_ref, bf16[64,4,8,128]{3,2,1,0:T(8,128)(2,1)} %collective-permute-done.6.values_ref, ...), custom_call_target="tpu_custom_call" | custom-call | tf_op jit(solution)/shard_map/pallas_call | solution.py:576
  179.3 1.3 copy.13
  180.6 0.8 shard_map.112
  (14 shorter events, 0.0 us)
Async XLA Ops:
  0.6 23.4 %collective-permute-start = (bf16[1,64,4608]{2,1,0:T(8,128)(2,1)}, bf16[1,64,4608]{2,1,0:T(8,128)(2,1)S(1)}, u32[]{:S(2)}, u32[]{:S(2)}) collective-permute-start(bf16[1,64,4608]{2,1,0:T(8,128)(2,1)} %weight_hbm.1), channel_id=1, source_target_pairs={{0,1},{1,0},{2,3},{3,2},{4,5},{5,4},{6,7},{7,6},{8,9},{9,8},{10,11... | collective-permute-start | bytes 1769480 | tf_op jit(solution)/shard_map/ppermute | solution.py:463
  24.8 61.1 %copy-start.3 = (s32[32]{0:T(128)S(1)}, s32[32]{0:T(128)}, u32[]{:S(2)}) copy-start(s32[32]{0:T(128)} %lengths_ref.3) | copy-start | bytes 388
  85.9 25.3 %copy-start.2 = (bf16[1,36,4096]{2,1,0:T(8,128)(2,1)S(1)}, bf16[1,36,4096]{2,1,0:T(8,128)(2,1)}, u32[]{:S(2)}) copy-start(bf16[1,36,4096]{2,1,0:T(8,128)(2,1)} %weight_ref.3) | copy-start | bytes 884740
  108.0 4.6 %collective-permute-start.1 = (bf16[64,16,128]{2,1,0:T(8,128)(2,1)S(1)}, bf16[64,16,128]{2,1,0:T(8,128)(2,1)S(1)}, u32[]{:S(2)}, u32[]{:S(2)}) collective-permute-start(bf16[64,16,128]{2,1,0:T(8,128)(2,1)S(1)} %all_to_all.26.own_ref.own_new_ref), channel_id=1, source_target_pairs={{0,1},{1,0},{2,3},{3,2},{4,5},{5,4},{6,7},{7,6},{8,9},{9,8},{10,11... | collective-permute-start | bytes 786440 | tf_op jit(solution)/shard_map/ppermute | solution.py:463
  111.8 0.8 copy-start.4
  112.6 22.1 %copy-start = (bf16[1,2,144,4608]{3,2,1,0:T(8,128)(2,1)S(1)}, bf16[1,2,144,4608]{3,2,1,0:T(8,128)(2,1)}, u32[]{:S(2)}) copy-start(bf16[1,2,144,4608]{3,2,1,0:T(8,128)(2,1)} %gate_up_ref.1) | copy-start | bytes 7962628
  112.6 22.1 %copy-start.1 = (bf16[1,144,4608]{2,1,0:T(8,128)(2,1)S(1)}, bf16[1,144,4608]{2,1,0:T(8,128)(2,1)}, u32[]{:S(2)}) copy-start(bf16[1,144,4608]{2,1,0:T(8,128)(2,1)} %down_ref.1) | copy-start | bytes 3981316
  131.1 3.6 %collective-permute-start.2 = (bf16[64,16,128]{2,1,0:T(8,128)(2,1)S(1)}, bf16[64,16,128]{2,1,0:T(8,128)(2,1)S(1)}, u32[]{:S(2)}, u32[]{:S(2)}) collective-permute-start(bf16[64,16,128]{2,1,0:T(8,128)(2,1)S(1)} %all_to_all.27.own_ref), channel_id=1, source_target_pairs={{0,1},{1,0},{2,3},{3,2},{4,5},{5,4},{6,7},{7,6},{8,9},{9,8},{10,11... | collective-permute-start | bytes 786440 | tf_op jit(solution)/shard_map/ppermute | solution.py:463
  133.7 0.8 copy-start.5
  136.6 1.7 collective-permute-start.3
  139.0 18.7 %all-to-all-start.3 = ((bf16[64,16,128]{2,1,0:T(8,128)(2,1)}), bf16[64,16,128]{2,1,0:T(8,128)(2,1)S(1)}, u32[]{:S(2)}, u32[]{:S(2)}) async-start(bf16[64,16,128]{2,1,0:T(8,128)(2,1)} %add_convert_fusion), calls=%async_computation.3 | async-start | bytes 524288 | tf_op jit(solution)/shard_map/all_to_all | solution.py:467
  145.7 31.7 %collective-permute-start.6 = (bf16[64,4,8,128]{3,2,1,0:T(8,128)(2,1)}, bf16[64,4,8,128]{3,2,1,0:T(8,128)(2,1)}, u32[]{:S(2)}, u32[]{:S(2)}) collective-permute-start(bf16[64,4,8,128]{3,2,1,0:T(8,128)(2,1)} %copy-done.4), channel_id=1, source_target_pairs={{0,1},{1,0},{2,3},{3,2},{4,5},{5,4},{6,7},{7,6},{8,9},{9,8},{10,11... | collective-permute-start | bytes 1572872 | tf_op jit(solution)/shard_map/ppermute | solution.py:463
  146.2 31.2 %collective-permute-start.5 = (bf16[64,4,8,128]{3,2,1,0:T(8,128)(2,1)}, bf16[64,4,8,128]{3,2,1,0:T(8,128)(2,1)}, u32[]{:S(2)}, u32[]{:S(2)}) collective-permute-start(bf16[64,4,8,128]{3,2,1,0:T(8,128)(2,1)} %copy-done.5), channel_id=1, source_target_pairs={{0,1},{1,0},{2,3},{3,2},{4,5},{5,4},{6,7},{7,6},{8,9},{9,8},{10,11... | collective-permute-start | bytes 1572872 | tf_op jit(solution)/shard_map/ppermute | solution.py:463
  174.7 5.9 %collective-permute-start.4 = (f32[64,1,128]{2,1,0:T(1,128)S(1)}, f32[64,1,128]{2,1,0:T(1,128)S(1)}, u32[]{:S(2)}, u32[]{:S(2)}) collective-permute-start(f32[64,1,128]{2,1,0:T(1,128)S(1)} %all_to_all.28.own_ref), channel_id=1, source_target_pairs={{0,1},{1,0},{2,3},{3,2},{4,5},{5,4},{6,7},{7,6},{8,9},{9,8},{10,11... | collective-permute-start | bytes 98312 | tf_op jit(solution)/shard_map/ppermute | solution.py:463
